TPU v7x, 32 devices: a whole 2x2x4 slice. The times are simulated.
32 devices in a mesh: dp: 8 (over z, x), tensor: 4 (over y, core).
Axes of the slice: x: 2, y: 2, z: 4, core: 2. Of those that a mesh axis runs over, the one named last changes fastest.
Arguments:
- inputs: bfloat16 [8, 512, 1024], P(None, 'dp'), may hold values from -6 to 6
- norm1_gain: float32 [1024], replicated, may hold values from 0.5 to 1.5
- w_query: bfloat16 [1024, 1024], P(None, 'tensor'), may hold values from -0.1875 to 0.1875
- w_key: bfloat16 [1024, 1024], P(None, 'tensor'), may hold values from -0.1875 to 0.1875
- w_value: bfloat16 [1024, 2048], P(None, 'tensor'), may hold values from -0.1875 to 0.1875
- w_gate: bfloat16 [1024, 2048], P(None, 'tensor'), may hold values from -0.1875 to 0.1875
- w_beta: bfloat16 [1024, 8], P(None, 'tensor'), may hold values from -0.1875 to 0.1875
- w_decay: bfloat16 [1024, 8], P(None, 'tensor'), may hold values from -0.1875 to 0.1875
- decay_rate: float32 [8], P('tensor'), may hold values from 0.0009765625 to 0.05
- conv_query: float32 [4, 1024], P(None, 'tensor'), may hold values from -3 to 3
- conv_key: float32 [4, 1024], P(None, 'tensor'), may hold values from -3 to 3
- conv_value: float32 [4, 2048], P(None, 'tensor'), may hold values from -3 to 3
- head_gain: float32 [2048], P('tensor'), may hold values from 0.5 to 1.5
- w_out: bfloat16 [2048, 1024], P('tensor'), may hold values from -0.1875 to 0.1875
- norm2_gain: float32 [1024], replicated, may hold values from 0.5 to 1.5
- w_ffn_gate: bfloat16 [1024, 2816], P(None, 'tensor'), may hold values from -0.1875 to 0.1875
- w_ffn_up: bfloat16 [1024, 2816], P(None, 'tensor'), may hold values from -0.1875 to 0.1875
- w_ffn_down: bfloat16 [2816, 1024], P('tensor'), may hold values from -0.109375 to 0.109375
- cotangent: bfloat16 [8, 512, 1024], P(None, 'dp'), may hold values from -6 to 6
Outputs:
- output: bfloat16 [8, 512, 1024], P(None, 'dp')
- grad_inputs: float32 [8, 512, 1024], P(None, 'dp')
- grad_norm1_gain: float32 [1024], replicated
- grad_w_query: float32 [1024, 1024], P(None, 'tensor')
- grad_w_key: float32 [1024, 1024], P(None, 'tensor')
- grad_w_value: float32 [1024, 2048], P(None, 'tensor')
- grad_w_gate: float32 [1024, 2048], P(None, 'tensor')
- grad_w_beta: float32 [1024, 8], P(None, 'tensor')
- grad_w_decay: float32 [1024, 8], P(None, 'tensor')
- grad_decay_rate: float32 [8], P('tensor')
- grad_conv_query: float32 [4, 1024], P(None, 'tensor')
- grad_conv_key: float32 [4, 1024], P(None, 'tensor')
- grad_conv_value: float32 [4, 2048], P(None, 'tensor')
- grad_head_gain: float32 [2048], P('tensor')
- grad_w_out: float32 [2048, 1024], P('tensor')
- grad_norm2_gain: float32 [1024], replicated
- grad_w_ffn_gate: float32 [1024, 2816], P(None, 'tensor')
- grad_w_ffn_up: float32 [1024, 2816], P(None, 'tensor')
- grad_w_ffn_down: float32 [2816, 1024], P('tensor')
All inputs are finite; a program needn't handle non-finite values.
Results may differ from a plain program's by a relative error of at most 0.01.
Values sent between devices are 32-bit elements; how exact they have to be, the bound alone decides.
A program may use at most 320 MiB of HBM per device.

v0:
```python
from functools import partial

import jax
import jax.numpy as jnp
from jax import lax
from jax.sharding import PartitionSpec as P

SPAN = 64


EPS = 1e-06


def from_behind(shard, axis, by):
    count = lax.axis_size(axis)
    pairs = [(i, i + by) for i in range(count) if 0 <= i + by < count]
    return lax.ppermute(shard, axis, pairs)


def carried_in(part, axis, combine, identity, reverse):
    count = lax.axis_size(axis)
    place = lax.axis_index(axis)
    ahead = count - 1 - place if reverse else place
    gathered = jax.tree.map(lambda a: lax.all_gather(a, axis), part)
    state = jax.tree.map(lambda a, e: jnp.zeros_like(a) + jnp.asarray(e, a.dtype), part, identity)

    def one(turn, state):
        source = count - 1 - turn if reverse else turn
        return combine(
            state, jax.tree.map(lambda a: lax.dynamic_index_in_dim(a, source, 0, False), gathered)
        )

    return lax.fori_loop(0, ahead, one, state)


def exact(left, right):
    return jnp.matmul(left, right, precision=lax.Precision.HIGHEST)


def span_apply(state, inputs):
    query, key, values, beta, logdecay = inputs
    count = query.shape[0]
    cumul = jnp.cumsum(logdecay)
    row_ids = lax.broadcasted_iota(jnp.int32, (count, count), 0)
    col_ids = lax.broadcasted_iota(jnp.int32, (count, count), 1)
    within = col_ids <= row_ids
    strict = col_ids < row_ids
    spread = jnp.where(within, cumul[:, None] - cumul[None, :], 0.0)
    decays = jnp.where(within, jnp.exp(spread), 0.0)
    scaled = decays * beta[None, :]
    lower = jnp.where(strict, scaled * exact(key, key.T), 0.0)
    start_decay = jnp.exp(cumul)[:, None]
    right_side = values - start_decay * exact(key, state)
    system = jnp.eye(count, dtype=lower.dtype) + lower
    update = jax.scipy.linalg.solve_triangular(system, right_side, lower=True, unit_diagonal=True)
    output = start_decay * exact(query, state) + exact(scaled * exact(query, key.T), update)
    tail = jnp.exp(cumul[-1] - cumul) * beta
    new_state = jnp.exp(cumul[-1]) * state + exact((key * tail[:, None]).T, update)
    return (new_state, output)


def run_segment(query, key, values, beta, logdecay, state):
    length = query.shape[0]
    blocks = length // SPAN

    def split(array):
        return array.reshape((blocks, SPAN) + array.shape[1:])

    final, outputs = lax.scan(
        span_apply, state, (split(query), split(key), split(values), split(beta), split(logdecay))
    )
    return (outputs.reshape((length,) + outputs.shape[2:]), final)


def run_heads(query, key, values, beta, logdecay, state):
    return jax.vmap(jax.vmap(run_segment))(query, key, values, beta, logdecay, state)


def prepare(extended, beta_pre, decay_pre, conv_all, decay_rate, key_dim):
    batch, seg, heads = beta_pre.shape
    reach = conv_all.shape[0] - 1
    total = conv_all[0] * extended[:, 0:seg, :]
    for offset in range(1, reach + 1):
        total = total + conv_all[offset] * extended[:, offset : offset + seg, :]
    active = jax.nn.silu(total)
    qk_width = heads * key_dim
    query = active[..., :qk_width].reshape(batch, seg, heads, key_dim)
    key = active[..., qk_width : 2 * qk_width].reshape(batch, seg, heads, key_dim)
    values = active[..., 2 * qk_width :].reshape(batch, seg, heads, -1)
    query = query * lax.rsqrt(jnp.sum(query * query, -1, keepdims=True) + EPS) * key_dim ** (-0.5)
    key = key * lax.rsqrt(jnp.sum(key * key, -1, keepdims=True) + EPS)
    beta = jax.nn.sigmoid(beta_pre)
    logdecay = -decay_rate * jax.nn.softplus(decay_pre)
    return (
        jnp.moveaxis(query, 2, 1),
        jnp.moveaxis(key, 2, 1),
        jnp.moveaxis(values, 2, 1),
        jnp.moveaxis(beta, 2, 1),
        jnp.moveaxis(logdecay, 2, 1),
    )


def gate_norm(core, gate_pre, head_gain):
    normed = core * lax.rsqrt(jnp.mean(core * core, -1, keepdims=True) + EPS)
    return normed * head_gain * jax.nn.silu(gate_pre)


def rms_apply(resid, gain):
    return resid * lax.rsqrt(jnp.mean(resid * resid, -1, keepdims=True) + EPS) * gain


def swiglu(gate, upper):
    return jax.nn.silu(gate) * upper


def project(left, right):
    return jnp.dot(left, right, preferred_element_type=jnp.float32)


def contract_rows(left, right):
    return jnp.einsum("ra,rb->ab", left, right, preferred_element_type=jnp.float32)


def back_project(grad, weight):
    return jnp.einsum("rb,ab->ra", grad, weight, preferred_element_type=jnp.float32)


def compose(earlier, later):
    return (exact(later[0], earlier[0]), exact(later[0], earlier[1]) + later[1])


def shards(
    inputs,
    norm1_gain,
    w_query,
    w_key,
    w_value,
    w_gate,
    w_beta,
    w_decay,
    decay_rate,
    conv_query,
    conv_key,
    conv_value,
    head_gain,
    w_out,
    norm2_gain,
    w_ffn_gate,
    w_ffn_up,
    w_ffn_down,
    cotangent,
):
    batch, seg, width = inputs.shape
    count = batch * seg
    heads = decay_rate.shape[0]
    key_dim = w_query.shape[1] // heads
    value_dim = w_value.shape[1] // heads
    qk_width = heads * key_dim
    reach = conv_query.shape[0] - 1
    bf = jnp.bfloat16
    resid = inputs.reshape(count, width).astype(jnp.float32)
    normed1, norm1_back = jax.vjp(rms_apply, resid, norm1_gain)
    hidden1 = normed1.astype(bf)
    query_pre = project(hidden1, w_query)
    key_pre = project(hidden1, w_key)
    value_pre = project(hidden1, w_value)
    gate_pre = project(hidden1, w_gate)
    beta_pre = project(hidden1, w_beta)
    decay_pre = project(hidden1, w_decay)
    mixed_pre = jnp.concatenate([query_pre, key_pre, value_pre], axis=1).reshape(batch, seg, -1)
    rim = from_behind(mixed_pre[:, seg - reach :, :], "dp", 1)
    extended = jnp.concatenate([rim, mixed_pre], axis=1)
    conv_all = jnp.concatenate([conv_query, conv_key, conv_value], axis=1)
    features, prep_back = jax.vjp(
        partial(prepare, key_dim=key_dim),
        extended,
        beta_pre.reshape(batch, seg, heads),
        decay_pre.reshape(batch, seg, heads),
        conv_all,
        decay_rate,
    )
    query_h, key_h, value_h, beta_h, decay_h = features
    eye_block = jnp.broadcast_to(
        jnp.eye(key_dim, dtype=jnp.float32), (batch, heads, key_dim, key_dim)
    )
    zero_block = jnp.zeros((batch, heads, key_dim, value_dim), jnp.float32)
    values_aug = jnp.concatenate(
        [jnp.zeros(value_h.shape[:3] + (key_dim,), jnp.float32), value_h], axis=-1
    )
    state_aug = jnp.concatenate([eye_block, zero_block], axis=-1)
    outputs_aug, final_aug = run_heads(query_h, key_h, values_aug, beta_h, decay_h, state_aug)
    out_carry = outputs_aug[..., :key_dim]
    out_local = outputs_aug[..., key_dim:]
    transition = final_aug[..., :key_dim]
    offset_part = final_aug[..., key_dim:]
    prefix = carried_in((transition, offset_part), "dp", compose, (eye_block, zero_block), False)
    start_state = prefix[1]
    core = jnp.moveaxis(exact(out_carry, start_state) + out_local, 1, 2)
    gate4 = gate_pre.reshape(batch, seg, heads, value_dim)
    gated, gate_back = jax.vjp(gate_norm, core, gate4, head_gain.reshape(heads, value_dim))
    mixed = gated.reshape(count, heads * value_dim).astype(bf)
    attention = lax.psum(project(mixed, w_out), "tensor")
    resid1 = resid + attention
    normed2, norm2_back = jax.vjp(rms_apply, resid1, norm2_gain)
    hidden2 = normed2.astype(bf)
    ffn_gate = project(hidden2, w_ffn_gate)
    ffn_up = project(hidden2, w_ffn_up)
    inner_full, swiglu_back = jax.vjp(swiglu, ffn_gate, ffn_up)
    inner = inner_full.astype(bf)
    ffn = lax.psum(project(inner, w_ffn_down), "tensor")
    output = (resid1 + ffn).astype(bf).reshape(batch, seg, width)
    upstream = cotangent.reshape(count, width)
    grad_down = contract_rows(inner, upstream)
    grad_inner = back_project(upstream, w_ffn_down)
    grad_fgate, grad_fup = swiglu_back(grad_inner)
    grad_fgate = grad_fgate.astype(bf)
    grad_fup = grad_fup.astype(bf)
    grad_ffn_gate_w = contract_rows(hidden2, grad_fgate)
    grad_ffn_up_w = contract_rows(hidden2, grad_fup)
    grad_hidden2 = lax.psum(
        back_project(grad_fgate, w_ffn_gate) + back_project(grad_fup, w_ffn_up), "tensor"
    )
    grad_from_norm2, grad_norm2_gain = norm2_back(grad_hidden2)
    grad_resid1 = upstream.astype(jnp.float32) + grad_from_norm2
    grad_resid1_low = grad_resid1.astype(bf)
    grad_out_w = contract_rows(mixed, grad_resid1_low)
    grad_mixed = back_project(grad_resid1_low, w_out).reshape(batch, seg, heads, value_dim)
    grad_core, grad_gate4, grad_head_gain = gate_back(grad_mixed)
    grad_core_h = jnp.moveaxis(grad_core, 2, 1)
    carry_term = exact(jnp.swapaxes(out_carry, -1, -2), grad_core_h)
    suffix = carried_in(
        (jnp.swapaxes(transition, -1, -2), carry_term), "dp", compose, (eye_block, zero_block), True
    )

    def local_delta(query, key, values, beta, logdecay):
        return run_heads(query, key, values, beta, logdecay, start_state)

    recomputed, delta_back = jax.vjp(local_delta, query_h, key_h, value_h, beta_h, decay_h)
    feature_grads = delta_back((grad_core_h, suffix[1]))
    grad_ext, grad_beta_in, grad_decay_in, grad_conv, grad_rate = prep_back(feature_grads)
    returned = from_behind(grad_ext[:, :reach, :], "dp", -1)
    grad_mixed_pre = grad_ext[:, reach:, :] + jnp.pad(returned, ((0, 0), (seg - reach, 0), (0, 0)))
    grad_mixed_pre = grad_mixed_pre.reshape(count, -1)
    grad_query_low = grad_mixed_pre[:, :qk_width].astype(bf)
    grad_key_low = grad_mixed_pre[:, qk_width : 2 * qk_width].astype(bf)
    grad_value_low = grad_mixed_pre[:, 2 * qk_width :].astype(bf)
    grad_gate_low = grad_gate4.reshape(count, heads * value_dim).astype(bf)
    grad_beta_low = grad_beta_in.reshape(count, heads).astype(bf)
    grad_decay_low = grad_decay_in.reshape(count, heads).astype(bf)
    partial_hidden1 = (
        back_project(grad_query_low, w_query)
        + back_project(grad_key_low, w_key)
        + back_project(grad_value_low, w_value)
        + back_project(grad_gate_low, w_gate)
        + back_project(grad_beta_low, w_beta)
        + back_project(grad_decay_low, w_decay)
    )
    grad_hidden1 = lax.psum(partial_hidden1, "tensor")
    grad_from_norm1, grad_norm1_gain = norm1_back(grad_hidden1)
    grad_inputs = (grad_resid1 + grad_from_norm1).reshape(batch, seg, width)
    grad_query_w = contract_rows(hidden1, grad_query_low)
    grad_key_w = contract_rows(hidden1, grad_key_low)
    grad_value_w = contract_rows(hidden1, grad_value_low)
    grad_gate_w = contract_rows(hidden1, grad_gate_low)
    grad_beta_w = contract_rows(hidden1, grad_beta_low)
    grad_decay_w = contract_rows(hidden1, grad_decay_low)
    grad_convq = grad_conv[:, :qk_width]
    grad_convk = grad_conv[:, qk_width : 2 * qk_width]
    grad_convv = grad_conv[:, 2 * qk_width :]
    grad_head_flat = grad_head_gain.reshape(-1)
    (
        grad_norm1_gain,
        grad_query_w,
        grad_key_w,
        grad_value_w,
        grad_gate_w,
        grad_beta_w,
        grad_decay_w,
        grad_rate,
        grad_convq,
        grad_convk,
        grad_convv,
        grad_head_flat,
        grad_out_w,
        grad_norm2_gain,
        grad_ffn_gate_w,
        grad_ffn_up_w,
        grad_down,
    ) = lax.psum(
        (
            grad_norm1_gain,
            grad_query_w,
            grad_key_w,
            grad_value_w,
            grad_gate_w,
            grad_beta_w,
            grad_decay_w,
            grad_rate,
            grad_convq,
            grad_convk,
            grad_convv,
            grad_head_flat,
            grad_out_w,
            grad_norm2_gain,
            grad_ffn_gate_w,
            grad_ffn_up_w,
            grad_down,
        ),
        "dp",
    )
    return (
        output,
        grad_inputs,
        grad_norm1_gain,
        grad_query_w,
        grad_key_w,
        grad_value_w,
        grad_gate_w,
        grad_beta_w,
        grad_decay_w,
        grad_rate,
        grad_convq,
        grad_convk,
        grad_convv,
        grad_head_flat,
        grad_out_w,
        grad_norm2_gain,
        grad_ffn_gate_w,
        grad_ffn_up_w,
        grad_down,
    )


def solution(mesh):
    placed = (
        P(None, "dp", None),
        P(),
        P(None, "tensor"),
        P(None, "tensor"),
        P(None, "tensor"),
        P(None, "tensor"),
        P(None, "tensor"),
        P(None, "tensor"),
        P("tensor"),
        P(None, "tensor"),
        P(None, "tensor"),
        P(None, "tensor"),
        P("tensor"),
        P("tensor", None),
        P(),
        P(None, "tensor"),
        P(None, "tensor"),
        P("tensor", None),
        P(None, "dp", None),
    )
    return jax.shard_map(
        shards,
        mesh=mesh,
        in_specs=placed,
        out_specs=(
            P(None, "dp", None),
            P(None, "dp", None),
            P(),
            P(None, "tensor"),
            P(None, "tensor"),
            P(None, "tensor"),
            P(None, "tensor"),
            P(None, "tensor"),
            P(None, "tensor"),
            P("tensor"),
            P(None, "tensor"),
            P(None, "tensor"),
            P(None, "tensor"),
            P("tensor"),
            P("tensor", None),
            P(),
            P(None, "tensor"),
            P(None, "tensor"),
            P("tensor", None),
        ),
        check_vma=False,
    )
```

profile of v0, /device:TPU:0, one launch (start us, length us, event | category | flops | bytes accessed | tf_op | source)
XLA Modules:
  0.0 1750.0 jit_solution(10911321478041373754)
XLA Ops:
  15.1 3.0 copy.256
  19.7 5.7 collective-permute-start
  38.8 5.9 fusion.26
  46.2 2.4 reshape.595
  48.6 2.4 multiply_reduce_fusion.13
  56.5 80.0 %custom-call.22 = f32[8,2,1,64,64]{3,4,2,1,0:T(8,128)} custom-call(f32[8,2,1,64,64]{4,3,2,1,0:T(8,128)} %add_bitcast_fusion), custom_call_target="InvertDiagBlocksLowerTriangular" | custom-call | tf_op jit(solution)/shard_map/vmap(vmap())/while/body/eval_jaxpr/jit(_solve_triangular)/triangular_solve | solution.py:55
  141.0 3.3 fusion.10
  147.2 3.1 slice.156
  156.1 2.5 multiply_reduce_fusion.14
  165.4 2.8 multiply_add_fusion.1
  168.3 102.8 %all-gather.9.cloned.1.call-done = f32[64,2,128,128]{3,2,1,0:T(8,128)} async-done(((f32[8,2,128,128]{3,2,1,0:T(8,128)}), f32[64,2,128,128]{3,2,1,0:T(8,128)}) %all-gather.9.cloned.1.call-update) | async-done | bytes 8388624 | tf_op jit(solution)/shard_map/all_gather | solution.py:24
  271.1 228.2 %all-gather.11.cloned.1.call-done = f32[64,2,128,256]{3,2,1,0:T(8,128)} async-done(((f32[8,2,128,256]{3,2,1,0:T(8,128)}), f32[64,2,128,256]{3,2,1,0:T(8,128)}) %all-gather.11.cloned.1.call-update) | async-done | bytes 16777232 | tf_op jit(solution)/shard_map/all_gather | solution.py:24
  499.5 3.0 multiply_reduce_fusion.11
  508.1 77.7 %all-reduce.24.cloned.1.call-done = f32[512,1024]{1,0:T(8,128)} async-done(((f32[512,1024]{1,0:T(8,128)}), f32[512,1024]{1,0:T(8,128)}) %all-reduce.24.cloned.1.call-update) | async-done | bytes 2097168 | tf_op jit(solution)/shard_map/psum | solution.py:202
  593.2 2.4 multiply_convert_fusion.1
  599.1 2.5 copy.279
  601.7 49.0 %all-reduce.26.cloned.1.call-done = f32[512,1024]{1,0:T(8,128)} async-done(((f32[512,1024]{1,0:T(8,128)}), f32[512,1024]{1,0:T(8,128)}) %all-reduce.26.cloned.1.call-update) | async-done | bytes 2097168 | tf_op jit(solution)/shard_map/psum | solution.py:220
  650.6 3.5 multiply_reduce_fusion
  659.2 2.9 reshape.599
  662.1 4.5 multiply_reduce_fusion.8
  668.1 4.3 fusion.96
  673.9 3.6 fusion.206
  677.5 2.5 fusion.214
  683.3 3.5 fusion.210
  686.8 91.0 %all-gather.13.cloned.1.call-done = f32[64,2,128,128]{3,2,1,0:T(8,128)} async-done(((f32[8,2,128,128]{3,2,1,0:T(8,128)}), f32[64,2,128,128]{3,2,1,0:T(8,128)}) %all-gather.13.cloned.1.call-update) | async-done | bytes 8388624 | tf_op jit(solution)/shard_map/all_gather | solution.py:24
  777.7 228.1 %all-gather.15.cloned.1.call-done = f32[64,2,128,256]{3,2,1,0:T(8,128)} async-done(((f32[8,2,128,256]{3,2,1,0:T(8,128)}), f32[64,2,128,256]{3,2,1,0:T(8,128)}) %all-gather.15.cloned.1.call-update) | async-done | bytes 16777232 | tf_op jit(solution)/shard_map/all_gather | solution.py:24
  1007.3 47.4 %while.22 = (s32[]{:T(128)}, f32[8,2,128,256]{3,2,1,0:T(8,128)}, s32[]{:T(128)}, f32[8,8,2,128,128]{4,3,2,1,0:T(8,128)}, f32[8,8,2,128,256]{4,3,2,1,0:T(8,128)},...) while((s32[]{:T(128)}, f32[8,2,128,256]{3,2,1,0:T(8,128)}, s32[]{:T(128)}, ...), condition=%wide.region_14.15_spmd, body=%wide.region_13.14_spmd.sunk | while | flops 805830656 | bytes 11535507 | solution.py:33
  1008.9 5.1 bitcast_add_fusion.7
  1015.6 5.1 bitcast_add_fusion.7
  1022.4 5.1 bitcast_add_fusion.7
  1029.1 5.1 bitcast_add_fusion.7
  1035.8 5.1 bitcast_add_fusion.7
  1042.5 5.1 bitcast_add_fusion.7
  1049.2 5.1 bitcast_add_fusion.7
  1063.7 3.1 fusion.83
  1077.1 2.3 copy.333
  1088.6 3.9 fusion.65
  1094.1 2.5 fusion.62
  1100.0 2.8 multiply_reduce_fusion.3
  1106.8 4.3 collective-permute-done.1
  1114.1 2.4 add_add_fusion.2
  1117.9 2.5 fusion.216
  1120.4 2.5 fusion.215
  1134.9 64.6 %all-reduce.30.cloned.1.call-done = (f32[512,1024]{1,0:T(8,128)}, f32[512,1024]{1,0:T(8,128)}) async-done(((f32[512,1024]{1,0:T(8,128)}, f32[512,1024]{1,0:T(8,128)}), (f32[512,1024]{1,0:T(8,128)}, f32[512,1024]{1,0:T(8,128)})) %all-reduce.30.cloned.1.call-update) | async-done | bytes 4194320 | tf_op jit(solution)/shard_map/psum | solution.py:210
  1201.8 40.4 %all-reduce.16 = (f32[1024]{0:T(1024)}, f32[1024,2]{0,1:T(2,128)}, f32[1024,2]{0,1:T(2,128)}, f32[2]{0:T(128)}, f32[4,256]{1,0:T(4,128)}, /*index=5*/f32[4,256]{...) all-reduce(f32[1024]{0:T(1024)S(1)} %get-tuple-element.705, ...), channel_id=1, replica_groups=mesh['dp'=8,'tensor'=4] {'dp'}, use_global_device_ids=true, to_apply=%region_29.30 | all-reduce | flops 10754 | bytes 86032 | tf_op jit(solution)/shard_map/psum | solution.py:289
  1242.2 3.1 add_convert_fusion
  1247.2 477.8 %all-reduce.28.cloned.1.call-done = (f32[1024,256]{1,0:T(8,128)}, f32[1024,256]{1,0:T(8,128)}, f32[1024,512]{1,0:T(8,128)}, f32[1024,512]{1,0:T(8,128)}, f32[512...) async-done(((f32[1024,256]{1,0:T(8,128)}, f32[1024,256]{1,0:T(8,128)}, f32[1024,512]{1,0:T(8,128)}, f32[1024,512]{1,0:T(8,128)}, ...) | async-done | bytes 17039376 | tf_op jit(solution)/shard_map/psum | solution.py:289
  1725.0 2.4 copy.446
  (470 shorter events, 162.6 us)
Async XLA Ops:
  7.2 585.7 %copy-start = (bf16[704,1024]{1,0:T(8,128)(2,1)S(1)}, bf16[704,1024]{1,0:T(8,128)(2,1)}, u32[]{:S(2)}) copy-start(bf16[704,1024]{1,0:T(8,128)(2,1)} %param.40) | copy-start | bytes 4325380
  7.2 263.9 %all-gather.9.cloned.1.call-start = ((), (), s32[]{:S(2)}) async-start(), calls=%async_computation.2 | async-start | bytes 9437184 | tf_op jit(solution)/shard_map/all_gather | solution.py:24
  15.1 13.3 copy-start.144
  15.1 13.3 copy-start.8
  15.1 13.3 copy-start.107
  18.0 10.7 copy-start.134
  18.0 16.5 copy-start.132
  19.7 19.1 %collective-permute-start = (f32[8,3,1024]{2,1,0:T(4,128)}, f32[8,3,1024]{2,1,0:T(4,128)}, u32[]{:S(2)}, u32[]{:S(2)}) collective-permute-start(f32[8,3,1024]{2,1,0:T(4,128)} %slice.142), channel_id=1, source_target_pairs={{0,4},{4,8},{8,12},{12,16},{16,20},{20,24},{24,28},{1,5},{5,9},{9,... | collective-permute-start | bytes 294920 | tf_op jit(solution)/shard_map/ppermute | solution.py:17
  28.7 16.0 copy-start.10
  34.5 10.2 copy-start.109
  34.5 10.1 copy-start.111
  34.6 10.1 copy-start.113
  34.6 10.1 copy-start.115
  36.1 8.6 copy-start.75
  36.8 7.9 copy-start.77
  36.9 7.9 copy-start.85
  44.8 91.7 %copy-start.30 = (f32[8,64,512]{2,1,0:T(8,128)}, f32[8,64,512]{2,1,0:T(8,128)S(1)}, u32[]{:S(2)}) copy-start(f32[8,64,512]{2,1,0:T(8,128)S(1)} %slice.152) | copy-start | bytes 3145732
  46.2 114.9 %copy-start.6 = (f32[8,8,2,8,128]{4,3,2,1,0:T(8,128)}, f32[8,8,2,8,128]{4,3,2,1,0:T(8,128)S(1)}, u32[]{:S(2)}) copy-start(f32[8,8,2,8,128]{4,3,2,1,0:T(8,128)S(1)} %get-tuple-element.769) | copy-start | bytes 1572868
  46.2 119.2 %copy-start.22 = (f32[8,8,2,8,128]{4,3,2,1,0:T(8,128)}, f32[8,8,2,8,128]{4,3,2,1,0:T(8,128)S(1)}, u32[]{:S(2)}) copy-start(f32[8,8,2,8,128]{4,3,2,1,0:T(8,128)S(1)} %get-tuple-element.768) | copy-start | bytes 1572868
  146.7 352.5 %all-gather.11.cloned.1.call-start = ((), (), s32[]{:S(2)}) async-start(), calls=%async_computation.3 | async-start | bytes 18874368 | tf_op jit(solution)/shard_map/all_gather | solution.py:24
  150.3 435.6 %all-reduce.24.cloned.1.call-start = ((), (), s32[]{:S(2)}) async-start(), calls=%async_computation | async-start | bytes 4194304 | tf_op jit(solution)/shard_map/psum | solution.py:202
  161.0 4.3 copy-start.94
  507.9 142.7 %all-reduce.26.cloned.1.call-start = ((), (), s32[]{:S(2)}) async-start(), calls=%async_computation.1 | async-start | bytes 4194304 | tf_op jit(solution)/shard_map/psum | solution.py:220
  599.0 178.7 %all-gather.13.cloned.1.call-start = ((), (), s32[]{:S(2)}) async-start(), calls=%async_computation.4 | async-start | bytes 9437184 | tf_op jit(solution)/shard_map/all_gather | solution.py:24
  601.6 404.2 %all-gather.15.cloned.1.call-start = ((), (), s32[]{:S(2)}) async-start(), calls=%async_computation.5 | async-start | bytes 18874368 | tf_op jit(solution)/shard_map/all_gather | solution.py:24
  662.1 4.5 copy-start.101
  662.1 4.5 copy-start.33
  662.1 4.6 copy-start.34
  662.1 4.6 copy-start.51
  662.1 4.6 copy-start.99
  662.1 4.6 copy-start.127
  672.4 527.1 %all-reduce.30.cloned.1.call-start = ((), (), s32[]{:S(2)}) async-start(), calls=%async_computation.7 | async-start | bytes 8388608 | tf_op jit(solution)/shard_map/psum | solution.py:210
  683.3 324.0 %copy-start.47 = (bf16[64,8,2,256]{3,1,2,0:T(8,128)(2,1)}, bf16[64,8,2,256]{3,1,2,0:T(8,128)(2,1)S(1)}, u32[]{:S(2)}) copy-start(bf16[64,8,2,256]{3,1,2,0:T(8,128)(2,1)S(1)} %copy.337) | copy-start | bytes 1572868
  1074.4 5.2 copy-start.76
  1074.4 5.2 copy-start.78
  1074.4 12.3 copy-start.103
  1074.4 13.8 copy-start.139
  1076.5 12.0 copy-start.24
  1104.2 6.9 collective-permute-start.1
  1106.8 4.6 copy-start.71
  1116.5 608.5 %all-reduce.28.cloned.1.call-start = ((), (), s32[]{:S(2)}) async-start(), calls=%async_computation.6 | async-start | bytes 34078720 | tf_op jit(solution)/shard_map/psum | solution.py:289
  1132.1 67.4 %copy-start.9 = (bf16[8,64,1024]{2,1,0:T(8,128)(2,1)S(1)}, bf16[8,64,1024]{2,1,0:T(8,128)(2,1)}, u32[]{:S(2)}) copy-start(bf16[8,64,1024]{2,1,0:T(8,128)(2,1)} %param.23) | copy-start | bytes 3145732
  1132.1 67.4 %copy-start.108 = (f32[1024]{0:T(1024)S(1)}, f32[1024]{0:T(1024)}, u32[]{:S(2)}) copy-start(f32[1024]{0:T(1024)} %param.24) | copy-start | bytes 12292
  1132.1 67.3 %copy-start.122 = (f32[512]{0:T(512)S(1)}, f32[512]{0:T(512)}, u32[]{:S(2)}) copy-start(f32[512]{0:T(512)} %copy-done.121) | copy-start | bytes 6148
  1133.2 68.6 %copy-start.136 = (f32[1024]{0:T(1024)S(1)}, f32[1024]{0:T(1024)}, u32[]{:S(2)}) copy-start(f32[1024]{0:T(1024)} %get-tuple-element.701) | copy-start | bytes 12292
  1133.2 109.0 %copy-start.131 = (f32[512]{0:T(512)S(1)}, f32[512]{0:T(512)}, u32[]{:S(2)}) copy-start(f32[512]{0:T(512)} %copy-done.130) | copy-start | bytes 6148
  1133.2 109.0 %copy-start.5 = (f32[512,1024]{1,0:T(8,128)S(1)}, f32[512,1024]{1,0:T(8,128)}, u32[]{:S(2)}) copy-start(f32[512,1024]{1,0:T(8,128)} %copy-done.3) | copy-start | bytes 6291460
  1738.5 4.4 copy-start.1
  (107 other events, 234.7 us)
Sparse Core Ops, SparseCore 0:
  146.9 124.1 all-gather.8
  273.8 225.4 all-gather.10
  508.0 77.7 all-reduce.23
  599.1 51.4 all-reduce.25
  653.2 124.5 all-gather.12
  780.3 225.4 all-gather.14
  1116.7 82.7 all-reduce.29
  1206.5 518.5 all-reduce.27
where the time goes:
time: 1760 us; the launch traced here: 1750 us
  waiting for transfers between devices  1320 us (75%)
  other arithmetic  137 us (8%)
  matrix products  132 us (8%)
  local copies, waits for them, and re-layouts  92.1 us (5%)
  blocking collectives  40.4 us (2%)
    all_gather x4, waiting for transfers between devices, carried_in(): gathered = jax.tree.map(lambda a: lax.all_gather(a, axis), part)  650 us
    psum x1, waiting for transfers between devices, shards(): lax.psum((grad_norm1_gain, grad_query_w, grad_key_w, grad_value_w, grad_g...  478 us
    another operation x5, other arithmetic, span_apply(): jax.scipy.linalg.solve_triangular(system, right_side, lower=True, unit_di...  84.3 us
    dot_general x27, matrix products, exact(): return jnp.matmul(left, right, precision=lax.Precision.HIGHEST)  78.7 us
    psum x1, waiting for transfers between devices, shards(): attention = lax.psum(project(mixed, w_out), 'tensor')  77.7 us
    psum x1, waiting for transfers between devices, shards(): ffn = lax.psum(project(inner, w_ffn_down), 'tensor')  64.6 us
    psum x1, waiting for transfers between devices, shards(): lax.psum(back_project(grad_fgate, w_ffn_gate) + back_project(grad_fup, w_...  49 us
    psum x1, blocking collectives, shards(): lax.psum((grad_norm1_gain, grad_query_w, grad_key_w, grad_value_w, grad_g...  40.4 us
  transfers between devices with their start and end apart: 10, of which 9 were waited for; matrix products, arithmetic and copies ran while one was open for 5% of the time, Pallas kernels for 0%

commit v1 on v0

--- a/solution.py
+++ b/solution.py
@@ -1,8 +1,11 @@
+import functools
 from functools import partial
 
 import jax
 import jax.numpy as jnp
 from jax import lax
+from jax.experimental import pallas as pl
+from jax.experimental.pallas import tpu as pltpu
 from jax.sharding import PartitionSpec as P
 
 SPAN = 64
@@ -331,6 +334,639 @@
     )
 
 
+HALO = 8
+
+
+def mm(left, right):
+    return lax.dot_general(
+        left, right, (((1,), (0,)), ((), ())),
+        precision=lax.Precision.HIGHEST, preferred_element_type=jnp.float32,
+    )
+
+
+def mm_nt(left, right):
+    return lax.dot_general(
+        left, right, (((1,), (1,)), ((), ())),
+        precision=lax.Precision.HIGHEST, preferred_element_type=jnp.float32,
+    )
+
+
+def mm_tn(left, right):
+    return lax.dot_general(
+        left, right, (((0,), (0,)), ((), ())),
+        precision=lax.Precision.HIGHEST, preferred_element_type=jnp.float32,
+    )
+
+
+def grids(count):
+    rows = lax.broadcasted_iota(jnp.int32, (count, count), 0)
+    cols = lax.broadcasted_iota(jnp.int32, (count, count), 1)
+    return rows, cols
+
+
+def unit_inverse(lower, rows, cols):
+    count = lower.shape[0]
+    near = (rows // 2 == cols // 2) & (rows > cols)
+    inverse = jnp.where(rows == cols, 1.0, jnp.where(near, -lower, 0.0))
+    block = 2
+    while block < count:
+        cross = (rows // (2 * block) == cols // (2 * block)) & (rows // block > cols // block)
+        inverse = inverse - mm(mm(inverse, jnp.where(cross, lower, 0.0)), inverse)
+        block *= 2
+    return inverse
+
+
+def conv_window(halo_block, taps, span):
+    reach = taps.shape[0] - 1
+    total = None
+    for offset in range(reach + 1):
+        start = HALO - reach + offset
+        term = taps[offset : offset + 1] * halo_block[start : start + span]
+        total = term if total is None else total + term
+    return total
+
+
+def sigmoid(value):
+    return 1.0 / (1.0 + jnp.exp(-value))
+
+
+def softplus(value):
+    return jnp.maximum(value, 0.0) + jnp.log(1.0 + jnp.exp(-jnp.abs(value)))
+
+
+def gates_of(small, rate, heads, rows, cols):
+    beta = sigmoid(small)
+    slope = softplus(small)
+    logdecay = -rate * slope
+    cumul = mm(jnp.where(cols <= rows, 1.0, 0.0), logdecay)
+    return beta, slope, logdecay, cumul
+
+
+def chunk_terms(query, key, beta_col, beta_row, cum_col, cum_row, rows, cols):
+    within = cols <= rows
+    decays = jnp.where(within, jnp.exp(jnp.where(within, cum_col - cum_row, 0.0)), 0.0)
+    scaled = decays * beta_row
+    key_key = mm_nt(key, key)
+    query_key = mm_nt(query, key)
+    lower = jnp.where(cols < rows, scaled * key_key, 0.0)
+    attend = scaled * query_key
+    return decays, scaled, key_key, query_key, lower, attend
+
+
+def forward_kernel(heads, key_dim, value_dim, pre_ref, gate_ref, small_ref, taps_ref, rate_ref, gain_ref,
+                   mixed_ref, core_ref, update_ref, state_ref, inverse_ref, pad_ref, now_ref):
+    length, width = pre_ref.shape
+    span = SPAN
+    chunks = length // span
+    rows, cols = grids(span)
+    qk = heads * key_dim
+    pad_ref[0:HALO] = jnp.zeros((HALO, width), jnp.float32)
+    for head in range(heads):
+        now_ref[head] = jnp.zeros((key_dim, value_dim), jnp.float32)
+
+    def chunk(index, carry):
+        start = pl.multiple_of(index * span, span)
+        here = pl.ds(start, span)
+        pad_ref[HALO : HALO + span] = pre_ref[here, :]
+        total = conv_window(pad_ref[...], taps_ref[...], span)
+        pad_ref[0:HALO] = pad_ref[span : span + HALO]
+        active = total * sigmoid(total)
+        beta, _, _, cumul = gates_of(small_ref[here, :], rate_ref[...], heads, rows, cols)
+        beta_t = jnp.transpose(beta)
+        cumul_t = jnp.transpose(cumul)
+        gate = gate_ref[here, :]
+        gated = gate * sigmoid(gate) * gain_ref[...]
+        for head in range(heads):
+            query = active[:, head * key_dim : (head + 1) * key_dim]
+            query = query * (lax.rsqrt(jnp.sum(query * query, -1, keepdims=True) + EPS) * key_dim ** (-0.5))
+            key = active[:, qk + head * key_dim : qk + (head + 1) * key_dim]
+            key = key * lax.rsqrt(jnp.sum(key * key, -1, keepdims=True) + EPS)
+            value = active[:, 2 * qk + head * value_dim : 2 * qk + (head + 1) * value_dim]
+            beta_col = beta[:, head : head + 1]
+            beta_row = beta_t[head : head + 1]
+            cum_col = cumul[:, heads + head : heads + head + 1]
+            cum_row = cumul_t[heads + head : heads + head + 1]
+            _, _, _, _, lower, attend = chunk_terms(query, key, beta_col, beta_row, cum_col, cum_row, rows, cols)
+            inverse = unit_inverse(lower, rows, cols)
+            state = now_ref[head]
+            state_ref[index, head] = state
+            rise = jnp.exp(cum_col)
+            last = cum_col[span - 1 : span]
+            update = mm(inverse, value) - mm(mm(inverse, rise * key), state)
+            core = mm(rise * query, state) + mm(attend, update)
+            tail = jnp.exp(last - cum_col) * beta_col
+            now_ref[head] = jnp.exp(last) * state + mm_tn(key * tail, update)
+            inverse_ref[index, head] = inverse
+            wide = slice(head * value_dim, (head + 1) * value_dim)
+            update_ref[here, wide] = update
+            core_ref[here, wide] = core
+            normed = core * lax.rsqrt(jnp.mean(core * core, -1, keepdims=True) + EPS)
+            mixed_ref[here, wide] = (normed * gated[:, wide]).astype(mixed_ref.dtype)
+        return carry
+
+    lax.fori_loop(0, chunks, chunk, 0)
+
+
+def delta_forward(pre, gate, small, taps, rate, gain, heads, key_dim, value_dim):
+    length, width = pre.shape
+    chunks = length // SPAN
+    out_shape = (
+        jax.ShapeDtypeStruct((length, heads * value_dim), jnp.bfloat16),
+        jax.ShapeDtypeStruct((length, heads * value_dim), jnp.float32),
+        jax.ShapeDtypeStruct((length, heads * value_dim), jnp.float32),
+        jax.ShapeDtypeStruct((chunks, heads, key_dim, value_dim), jnp.float32),
+        jax.ShapeDtypeStruct((chunks, heads, SPAN, SPAN), jnp.float32),
+    )
+    return pl.pallas_call(
+        functools.partial(forward_kernel, heads, key_dim, value_dim),
+        out_shape=out_shape,
+        scratch_shapes=[
+            pltpu.VMEM((HALO + SPAN, width), jnp.float32),
+            pltpu.VMEM((heads, key_dim, value_dim), jnp.float32),
+        ],
+        compiler_params=pltpu.CompilerParams(vmem_limit_bytes=56 << 20),
+        name="delta_forward",
+    )(pre, gate, small, taps, rate, gain)
+
+
+def backward_kernel(heads, key_dim, value_dim, pre_ref, gate_ref, small_ref, taps_ref, rate_ref, gain_ref,
+                    core_ref, update_ref, state_ref, inverse_ref, grad_ref,
+                    low_ref, gate_low_ref, small_low_ref, taps_grad_ref, gain_grad_ref, rate_grad_ref,
+                    ahead_ref, pad_ref, now_ref):
+    length, width = pre_ref.shape
+    span = SPAN
+    chunks = length // span
+    rows, cols = grids(span)
+    qk = heads * key_dim
+    reach = taps_ref.shape[0] - 1
+    lanes = small_ref.shape[1]
+    lane = lax.broadcasted_iota(jnp.int32, (span, lanes), 1)
+    for head in range(heads):
+        now_ref[head] = jnp.zeros((key_dim, value_dim), jnp.float32)
+    pad_ref[span : span + HALO] = jnp.zeros((HALO, width), jnp.float32)
+    taps_grad_ref[...] = jnp.zeros_like(taps_grad_ref)
+    gain_grad_ref[...] = jnp.zeros_like(gain_grad_ref)
+    rate_grad_ref[...] = jnp.zeros_like(rate_grad_ref)
+
+    def chunk(turn, carry):
+        index = chunks - 1 - turn
+        start = pl.multiple_of(index * span, span)
+        here = pl.ds(start, span)
+        before = pl.ds(pl.multiple_of(jnp.maximum(start - HALO, 0), HALO), HALO)
+        ahead_ref[0:HALO] = pre_ref[before, :] * jnp.where(index > 0, 1.0, 0.0)
+        ahead_ref[HALO : HALO + span] = pre_ref[here, :]
+        total = conv_window(ahead_ref[...], taps_ref[...], span)
+        gain_of = sigmoid(total)
+        active = total * gain_of
+        bend = gain_of * (1.0 + total * (1.0 - gain_of))
+        small = small_ref[here, :]
+        beta, slope, _, cumul = gates_of(small, rate_ref[...], heads, rows, cols)
+        beta_t = jnp.transpose(beta)
+        cumul_t = jnp.transpose(cumul)
+        gate = gate_ref[here, :]
+        gate_sig = sigmoid(gate)
+        gate_silu = gate * gate_sig
+        gate_bend = gate_sig * (1.0 + gate * (1.0 - gate_sig))
+        small_grad = jnp.zeros((span, lanes), jnp.float32)
+        for head in range(heads):
+            wide = slice(head * value_dim, (head + 1) * value_dim)
+            core = core_ref[here, wide]
+            grad_mixed = grad_ref[here, wide]
+            gain = gain_ref[:, wide]
+            scale = lax.rsqrt(jnp.mean(core * core, -1, keepdims=True) + EPS)
+            normed = core * scale
+            gate_low_ref[here, wide] = (grad_mixed * normed * gain * gate_bend[:, wide]).astype(gate_low_ref.dtype)
+            with_gate = grad_mixed * gate_silu[:, wide]
+            gain_grad_ref[:, wide] += jnp.sum(with_gate * normed, 0, keepdims=True)
+            grad_normed = with_gate * gain
+            grad_core = scale * (grad_normed - normed * jnp.mean(grad_normed * normed, -1, keepdims=True))
+            query_act = active[:, head * key_dim : (head + 1) * key_dim]
+            query_scale = lax.rsqrt(jnp.sum(query_act * query_act, -1, keepdims=True) + EPS)
+            query = query_act * (query_scale * key_dim ** (-0.5))
+            key_act = active[:, qk + head * key_dim : qk + (head + 1) * key_dim]
+            key_scale = lax.rsqrt(jnp.sum(key_act * key_act, -1, keepdims=True) + EPS)
+            key = key_act * key_scale
+            beta_col = beta[:, head : head + 1]
+            beta_row = beta_t[head : head + 1]
+            cum_col = cumul[:, heads + head : heads + head + 1]
+            cum_row = cumul_t[heads + head : heads + head + 1]
+            decays, scaled, key_key, query_key, lower, attend = chunk_terms(
+                query, key, beta_col, beta_row, cum_col, cum_row, rows, cols
+            )
+            state = state_ref[index, head]
+            update = update_ref[here, wide]
+            inverse = inverse_ref[index, head]
+            grad_state = now_ref[head]
+            rise = jnp.exp(cum_col)
+            last = cum_col[span - 1 : span]
+            fall = jnp.exp(last - cum_col)
+            tail = fall * beta_col
+            rise_query = rise * query
+            rise_key = rise * key
+            grad_update = mm_tn(attend, grad_core) + mm(key * tail, grad_state)
+            grad_right = mm_tn(inverse, grad_update)
+            now_ref[head] = jnp.exp(last) * grad_state + mm_tn(rise_query, grad_core) - mm_tn(rise_key, grad_right)
+            grad_attend = jnp.where(cols <= rows, mm_nt(grad_core, update), 0.0)
+            grad_lower = jnp.where(cols < rows, -mm_nt(grad_right, update), 0.0)
+            core_state = mm_nt(grad_core, state)
+            right_state = mm_nt(grad_right, state)
+            grad_tail_key = mm_nt(update, grad_state)
+            pair_query = grad_attend * scaled
+            pair_key = grad_lower * scaled
+            grad_query = rise * core_state + mm(pair_query, key)
+            grad_key = (
+                grad_tail_key * tail - rise * right_state + mm_tn(pair_query, query)
+                + mm(pair_key, key) + mm_tn(pair_key, key)
+            )
+            grad_tail = jnp.sum(grad_tail_key * key, -1, keepdims=True)
+            moved = grad_attend * query_key + grad_lower * key_key
+            spread = moved * scaled
+            by_row = jnp.sum(spread, -1, keepdims=True)
+            sums = mm_tn(
+                jnp.concatenate([moved * decays, spread], 1), jnp.ones((span, lanes), jnp.float32)
+            )
+            grad_beta = sums[:span, 0:1] + grad_tail * fall
+            through_tail = grad_tail * tail
+            grad_cum = (
+                by_row - sums[span:, 0:1] - through_tail
+                + rise * (jnp.sum(core_state * query, -1, keepdims=True) - jnp.sum(right_state * key, -1, keepdims=True))
+            )
+            end_grad = jnp.sum(through_tail, 0, keepdims=True) + jnp.exp(last) * jnp.sum(
+                jnp.sum(state * grad_state, -1, keepdims=True), 0, keepdims=True
+            )
+            grad_cum = grad_cum + jnp.where(rows[:, 0:1] == span - 1, end_grad, 0.0)
+            small_grad = small_grad + jnp.where(lane == head, grad_beta, 0.0)
+            small_grad = small_grad + jnp.where(lane == heads + head, grad_cum, 0.0)
+            grad_query = grad_query * key_dim ** (-0.5)
+            unit = query_act * query_scale
+            grad_query = query_scale * (grad_query - unit * jnp.sum(grad_query * unit, -1, keepdims=True))
+            grad_key = key_scale * (grad_key - key * jnp.sum(grad_key * key, -1, keepdims=True))
+            at = slice(head * key_dim, (head + 1) * key_dim)
+            pad_ref[0:span, at] = grad_query * bend[:, at]
+            at = slice(qk + head * key_dim, qk + (head + 1) * key_dim)
+            pad_ref[0:span, at] = grad_key * bend[:, at]
+            at = slice(2 * qk + head * value_dim, 2 * qk + (head + 1) * value_dim)
+            pad_ref[0:span, at] = grad_right * bend[:, at]
+        summed = mm(jnp.where(cols >= rows, 1.0, 0.0), small_grad)
+        is_beta = lane < heads
+        rate_grad_ref[...] += jnp.sum(jnp.where(is_beta, 0.0, -slope * summed), 0, keepdims=True)
+        sig = beta
+        small_low_ref[here, :] = jnp.where(
+            is_beta, small_grad * sig * (1.0 - sig), -rate_ref[...] * sig * summed
+        ).astype(small_low_ref.dtype)
+        outer = pad_ref[...]
+        dense = outer[0:span]
+        block = ahead_ref[...]
+        grad_pre = None
+        for offset in range(reach + 1):
+            behind = reach - offset
+            taps_grad_ref[offset : offset + 1] += jnp.sum(
+                dense * block[HALO - behind : HALO - behind + span], 0, keepdims=True
+            )
+            term = taps_ref[offset : offset + 1] * outer[behind : behind + span]
+            grad_pre = term if grad_pre is None else grad_pre + term
+        low_ref[here, :] = grad_pre.astype(low_ref.dtype)
+        pad_ref[span : span + HALO] = pad_ref[0:HALO]
+        return carry
+
+    lax.fori_loop(0, chunks, chunk, 0)
+
+
+def delta_backward(pre, gate, small, taps, rate, gain, core, update, state, inverse, grad, heads, key_dim, value_dim):
+    length, width = pre.shape
+    lanes = small.shape[1]
+    out_shape = (
+        jax.ShapeDtypeStruct((length, width), jnp.bfloat16),
+        jax.ShapeDtypeStruct((length, heads * value_dim), jnp.bfloat16),
+        jax.ShapeDtypeStruct((length, lanes), jnp.bfloat16),
+        jax.ShapeDtypeStruct(taps.shape, jnp.float32),
+        jax.ShapeDtypeStruct((1, heads * value_dim), jnp.float32),
+        jax.ShapeDtypeStruct((1, lanes), jnp.float32),
+    )
+    return pl.pallas_call(
+        functools.partial(backward_kernel, heads, key_dim, value_dim),
+        out_shape=out_shape,
+        scratch_shapes=[
+            pltpu.VMEM((HALO + SPAN, width), jnp.float32),
+            pltpu.VMEM((HALO + SPAN, width), jnp.float32),
+            pltpu.VMEM((heads, key_dim, value_dim), jnp.float32),
+        ],
+        compiler_params=pltpu.CompilerParams(vmem_limit_bytes=56 << 20),
+        name="delta_backward",
+    )(pre, gate, small, taps, rate, gain, core, update, state, inverse, grad)
+
+
+MESH = pl.DeviceIdType.MESH
+VM = pl.BlockSpec(memory_space=pltpu.VMEM)
+
+
+def greet(peers):
+    barrier = pltpu.get_barrier_semaphore()
+    for peer in peers:
+        pl.semaphore_signal(barrier, inc=1, device_id=peer, device_id_type=MESH)
+    pl.semaphore_wait(barrier, len(peers))
+
+
+def remote(src, dst, send, recv, peer):
+    return pltpu.make_async_remote_copy(
+        src_ref=src, dst_ref=dst, send_sem=send, recv_sem=recv, device_id=peer, device_id_type=MESH
+    )
+
+
+def tensor_peers():
+    dp = lax.axis_index("dp")
+    t = lax.axis_index("tensor")
+    core = lax.rem(t, 2)
+    mate = (dp, t + 1 - 2 * core)
+    across = (dp, lax.rem(t + 2, 4))
+    return core, mate, across
+
+
+def psum_kernel(blocks, part_ref, out_ref, land_mate, land_across, half, send, recv):
+    core, mate, across = tensor_peers()
+    greet((mate, across))
+    rows = part_ref.shape[0] // blocks
+    part = rows // 2
+    first = []
+    for b in range(blocks):
+        theirs = pl.ds(pl.multiple_of(b * rows + (1 - core) * part, part), part)
+        copy = remote(part_ref.at[theirs], land_mate.at[pl.ds(b * part, part)], send.at[0, b], recv.at[0, b], mate)
+        copy.start()
+        first.append(copy)
+    second = []
+    for b in range(blocks):
+        mine = pl.ds(pl.multiple_of(b * rows + core * part, part), part)
+        slot = pl.ds(b * part, part)
+        first[b].wait_recv()
+        half[slot] = part_ref[mine] + land_mate[slot]
+        copy = remote(half.at[slot], land_across.at[slot], send.at[1, b], recv.at[1, b], across)
+        copy.start()
+        second.append(copy)
+    third = []
+    for b in range(blocks):
+        mine = pl.ds(pl.multiple_of(b * rows + core * part, part), part)
+        slot = pl.ds(b * part, part)
+        second[b].wait_recv()
+        out_ref[mine] = half[slot] + land_across[slot]
+        copy = remote(out_ref.at[mine], out_ref.at[mine], send.at[2, b], recv.at[2, b], mate)
+        copy.start()
+        third.append(copy)
+    for b in range(blocks):
+        third[b].wait_recv()
+    for b in range(blocks):
+        first[b].wait_send()
+        second[b].wait_send()
+        third[b].wait_send()
+
+
+def tensor_sum(part, collective_id, blocks=8):
+    rows, width = part.shape
+    return pl.pallas_call(
+        functools.partial(psum_kernel, blocks),
+        out_shape=jax.ShapeDtypeStruct(part.shape, part.dtype),
+        in_specs=[VM],
+        out_specs=VM,
+        scratch_shapes=[pltpu.VMEM((rows // 2, width), part.dtype)] * 3
+        + [pltpu.SemaphoreType.DMA((3, blocks))] * 2,
+        compiler_params=pltpu.CompilerParams(
+            collective_id=collective_id, has_side_effects=True, vmem_limit_bytes=40 << 20
+        ),
+        name="tensor_sum",
+    )(part)
+
+
+def swap_kernel(count, narrow, *refs):
+    sources, results = refs[:count], refs[count : 2 * count]
+    staged, send, recv, close_send, close_recv = refs[2 * count :]
+    n = lax.axis_size("dp")
+    me = lax.axis_index("dp")
+    t = lax.axis_index("tensor")
+    core, mate, across = tensor_peers()
+    ranks = lax.axis_size("tensor")
+    others = [lax.rem(me + k, n) for k in range(1, n)]
+    greet([(other, t) for other in others] + [mate, across])
+    seg = results[0].shape[0] // n
+    part = seg // ranks
+    far = lax.rem(t + 2, ranks)
+
+    def at(place, rank):
+        return pl.ds(pl.multiple_of(place * seg + rank * part, part), part)
+
+    outgoing = []
+    for i in range(count):
+        for k in range(n):
+            other = lax.rem(me + k, n)
+            if k == 0:
+                results[i][at(me, t)] = sources[i][at(me, t)].astype(jnp.float32)
+                continue
+            if narrow[i]:
+                staged[i, k] = sources[i][at(other, t)].astype(jnp.float32)
+                src = staged.at[i, k]
+            else:
+                src = sources[i].at[at(other, t)]
+            copy = remote(src, results[i].at[at(me, t)], send.at[i, k], recv.at[i, k], (other, t))
+            copy.start()
+            outgoing.append(copy)
+    close = []
+    for i in range(count):
+        for k in range(n):
+            source = lax.rem(me + n - k, n)
+            here = results[i].at[at(source, t)]
+            if k:
+                remote(here, here, send.at[i, k], recv.at[i, k], (source, t)).wait_recv()
+            over = remote(here, here, close_send.at[0, i, k], close_recv.at[0, i, k], across)
+            over.start()
+            beside = remote(here, here, close_send.at[1, i, k], close_recv.at[1, i, k], mate)
+            beside.start()
+            close += [over, beside]
+    last = []
+    for i in range(count):
+        for k in range(n):
+            source = lax.rem(me + n - k, n)
+            there = results[i].at[at(source, far)]
+            remote(there, there, close_send.at[0, i, k], close_recv.at[0, i, k], across).wait_recv()
+            copy = remote(there, there, close_send.at[2, i, k], close_recv.at[2, i, k], mate)
+            copy.start()
+            last.append(copy)
+    for copy in outgoing:
+        copy.wait_send()
+    for j, copy in enumerate(close):
+        copy.wait_send()
+        if j % 2:
+            copy.wait_recv()
+    for copy in last:
+        copy.wait()
+
+
+def swap(arrays, n, collective_id):
+    count = len(arrays)
+    rows, width = arrays[0].shape
+    narrow = [a.dtype != jnp.float32 for a in arrays]
+    out = pl.pallas_call(
+        functools.partial(swap_kernel, count, narrow),
+        out_shape=[jax.ShapeDtypeStruct((rows, width), jnp.float32)] * count,
+        in_specs=[VM] * count,
+        out_specs=[VM] * count,
+        scratch_shapes=[pltpu.VMEM((count, n, rows // n // 4, width), jnp.float32)]
+        + [pltpu.SemaphoreType.DMA((count, n))] * 2
+        + [pltpu.SemaphoreType.DMA((3, count, n))] * 2,
+        compiler_params=pltpu.CompilerParams(
+            collective_id=collective_id, has_side_effects=True, vmem_limit_bytes=40 << 20
+        ),
+        name="swap",
+    )(*arrays)
+    return out
+
+
+def lane_pad(array, lanes):
+    return jnp.pad(array, ((0, 0), (0, lanes - array.shape[1])))
+
+
+def whole_sequences(
+    inputs,
+    norm1_gain,
+    w_query,
+    w_key,
+    w_value,
+    w_gate,
+    w_beta,
+    w_decay,
+    decay_rate,
+    conv_query,
+    conv_key,
+    conv_value,
+    head_gain,
+    w_out,
+    norm2_gain,
+    w_ffn_gate,
+    w_ffn_up,
+    w_ffn_down,
+    cotangent,
+):
+    batch, seg, width = inputs.shape
+    count = batch * seg
+    heads = decay_rate.shape[0]
+    key_dim = w_query.shape[1] // heads
+    value_dim = w_value.shape[1] // heads
+    qk_width = heads * key_dim
+    lanes = 128
+    bf = jnp.bfloat16
+    places = lax.axis_size("dp")
+    resid, upstream = swap(
+        [inputs.reshape(count, width), cotangent.reshape(count, width)], places, 1
+    )
+    upstream_low = upstream.astype(bf)
+    normed1, norm1_back = jax.vjp(rms_apply, resid, norm1_gain)
+    hidden1 = normed1.astype(bf)
+    w_mix = jnp.concatenate([w_query, w_key, w_value], axis=1)
+    w_small = lane_pad(jnp.concatenate([w_beta, w_decay], axis=1), lanes)
+    pre = project(hidden1, w_mix)
+    gate_pre = project(hidden1, w_gate)
+    small = project(hidden1, w_small)
+    taps = jnp.concatenate([conv_query, conv_key, conv_value], axis=1)
+    rate = lane_pad(jnp.pad(decay_rate, (heads, 0))[None], lanes)
+    gain = head_gain[None]
+    mixed, core, update, states, inverses = delta_forward(
+        pre, gate_pre, small, taps, rate, gain, heads, key_dim, value_dim
+    )
+    attention = tensor_sum(project(mixed, w_out), 2)
+    resid1 = resid + attention
+    normed2, norm2_back = jax.vjp(rms_apply, resid1, norm2_gain)
+    hidden2 = normed2.astype(bf)
+    ffn_gate = project(hidden2, w_ffn_gate)
+    ffn_up = project(hidden2, w_ffn_up)
+    inner_full, swiglu_back = jax.vjp(swiglu, ffn_gate, ffn_up)
+    inner = inner_full.astype(bf)
+    grad_inner = back_project(upstream_low, w_ffn_down)
+    grad_fgate, grad_fup = swiglu_back(grad_inner)
+    grad_fgate = grad_fgate.astype(bf)
+    grad_fup = grad_fup.astype(bf)
+    grad_hidden2 = tensor_sum(
+        back_project(grad_fgate, w_ffn_gate) + back_project(grad_fup, w_ffn_up), 3
+    )
+    ffn = tensor_sum(project(inner, w_ffn_down), 4)
+    grad_down = contract_rows(inner, upstream_low)
+    grad_ffn_gate_w = contract_rows(hidden2, grad_fgate)
+    grad_ffn_up_w = contract_rows(hidden2, grad_fup)
+    grad_from_norm2, grad_norm2_gain = norm2_back(grad_hidden2)
+    grad_resid1 = upstream + grad_from_norm2
+    grad_resid1_low = grad_resid1.astype(bf)
+    grad_out_w = contract_rows(mixed, grad_resid1_low)
+    grad_mixed = back_project(grad_resid1_low, w_out)
+    low, gate_low, small_low, grad_taps, grad_head, grad_rate = delta_backward(
+        pre, gate_pre, small, taps, rate, gain, core, update, states, inverses, grad_mixed,
+        heads, key_dim, value_dim,
+    )
+    partial_hidden1 = (
+        back_project(low, w_mix) + back_project(gate_low, w_gate) + back_project(small_low, w_small)
+    )
+    grad_hidden1 = tensor_sum(partial_hidden1, 5)
+    grad_from_norm1, grad_norm1_gain = norm1_back(grad_hidden1)
+    output, grad_inputs = swap([resid1 + ffn, grad_resid1 + grad_from_norm1], places, 6)
+    output = output.reshape(batch, seg, width).astype(bf)
+    grad_inputs = grad_inputs.reshape(batch, seg, width)
+    grad_mix_w = contract_rows(hidden1, low)
+    grad_gate_w = contract_rows(hidden1, gate_low)
+    grad_small_w = contract_rows(hidden1, small_low)
+    (
+        grad_norm1_gain,
+        grad_mix_w,
+        grad_gate_w,
+        grad_small_w,
+        grad_rate,
+        grad_taps,
+        grad_head,
+        grad_out_w,
+        grad_norm2_gain,
+        grad_ffn_gate_w,
+        grad_ffn_up_w,
+        grad_down,
+    ) = lax.psum(
+        (
+            grad_norm1_gain,
+            grad_mix_w,
+            grad_gate_w,
+            grad_small_w,
+            grad_rate,
+            grad_taps,
+            grad_head,
+            grad_out_w,
+            grad_norm2_gain,
+            grad_ffn_gate_w,
+            grad_ffn_up_w,
+            grad_down,
+        ),
+        "dp",
+    )
+    return (
+        output,
+        grad_inputs,
+        grad_norm1_gain,
+        grad_mix_w[:, :qk_width],
+        grad_mix_w[:, qk_width : 2 * qk_width],
+        grad_mix_w[:, 2 * qk_width :],
+        grad_gate_w,
+        grad_small_w[:, :heads],
+        grad_small_w[:, heads : 2 * heads],
+        grad_rate[0, heads : 2 * heads],
+        grad_taps[:, :qk_width],
+        grad_taps[:, qk_width : 2 * qk_width],
+        grad_taps[:, 2 * qk_width :],
+        grad_head[0],
+        grad_out_w,
+        grad_norm2_gain,
+        grad_ffn_gate_w,
+        grad_ffn_up_w,
+        grad_down,
+    )
+
+
+def fits_whole(mesh, args):
+    batch, length, _ = args[0].shape
+    places, ranks = mesh.shape["dp"], mesh.shape["tensor"]
+    return batch == places and ranks == 4 and length % (places * ranks * 16) == 0 and length % SPAN == 0
+
+
 def solution(mesh):
     placed = (
         P(None, "dp", None),
@@ -353,8 +989,13 @@
         P("tensor", None),
         P(None, "dp", None),
     )
-    return jax.shard_map(
-        shards,
+    def step(*args):
+        body = whole_sequences if fits_whole(mesh, args) else shards
+        return placed_step(body)(*args)
+
+    def placed_step(body):
+      return jax.shard_map(
+        body,
         mesh=mesh,
         in_specs=placed,
         out_specs=(
@@ -380,3 +1021,5 @@
         ),
         check_vma=False,
     )
+
+    return step

time: 1760 us -> 848 us (0.48)
  waiting for transfers between devices: 1320 us -> 412 us
  Pallas kernels: 0 us -> 288 us
  other arithmetic: 137 us -> 6.19 us
  matrix products: 132 us -> 37.6 us
  local copies, waits for them, and re-layouts: 92.1 us -> 38 us
    all_gather x4 -> x0, waiting for transfers between devices: 650 us -> none  [carried_in(): gathered = jax.tree.map(lambda a: lax.all_gather(a, axis), part)]
    pallas_call x0 -> x8, Pallas kernels: none -> 288 us  [the longest x4 113 us: tensor_sum(): pl.pallas_call(functools.partial(psum_kernel, blocks), out_shape=jax.Shap...]
    psum x4 -> x1, waiting for transfers between devices: 669 us -> 412 us  [whole_sequences(): lax.psum((grad_norm1_gain, grad_mix_w, grad_gate_w, grad_small_w, grad_ra...]
    another operation x8 -> x0, other arithmetic: 86 us -> none  [the longest x5 84.3 us: span_apply(): jax.scipy.linalg.solve_triangular(system, right_side, lower=True, unit_di...]
    dot_general x28 -> x0, matrix products: 79.8 us -> none  [the longest x27 78.7 us: exact(): return jnp.matmul(left, right, precision=lax.Precision.HIGHEST)]
    unnamed x303 -> x96, local copies, waits for them, and re-layouts: 36.6 us -> 29.1 us
  transfers between devices with their start and end apart: 10 -> 1, of which waited for: 9 -> 1; matrix products, arithmetic and copies ran while one was open for 5% -> 1% of each run, Pallas kernels for 0% -> 10%
where the time goes in v1:
time: 848 us
  waiting for transfers between devices  412 us (49%)
  Pallas kernels  288 us (34%)
  blocking collectives  51.5 us (6%)
  local copies, waits for them, and re-layouts  38 us (4%)
  matrix products  37.6 us (4%)
  between operations  14.5 us (2%)
    psum x1, waiting for transfers between devices, whole_sequences(): lax.psum((grad_norm1_gain, grad_mix_w, grad_gate_w, grad_small_w, grad_ra...  412 us
    pallas_call x4, Pallas kernels, tensor_sum(): pl.pallas_call(functools.partial(psum_kernel, blocks), out_shape=jax.Shap...  113 us
    pallas_call x2, Pallas kernels, swap(): pl.pallas_call(functools.partial(swap_kernel, count, narrow), out_shape=[...  91.8 us
    psum x1, blocking collectives, whole_sequences(): lax.psum((grad_norm1_gain, grad_mix_w, grad_gate_w, grad_small_w, grad_ra...  51.5 us
    pallas_call x1, Pallas kernels, delta_forward(): pl.pallas_call(functools.partial(forward_kernel, heads, key_dim, value_di...  47.2 us
    pallas_call x1, Pallas kernels, delta_backward(): pl.pallas_call(functools.partial(backward_kernel, heads, key_dim, value_d...  36.4 us
    unnamed x96, local copies, waits for them, and re-layouts  29.1 us
    dot_general x7, matrix products, contract_rows(): jnp.einsum('ra,rb->ab', left, right, preferred_element_type=jnp.float32)  18.2 us
  transfers between devices with their start and end apart: 1, of which 1 were waited for; matrix products, arithmetic and copies ran while one was open for 1% of the time, Pallas kernels for 10%

profile of v1, /device:TPU:0, one launch (start us, length us, event | category | flops | bytes accessed | tf_op | source)
XLA Modules:
  0.0 847.6 jit_solution(13335741987421669214)
XLA Ops:
  8.8 1.1 constant_dynamic-update-slice_fusion.2
  9.9 1.2 copy-done.3
  11.1 1.2 copy-done.4
  12.3 36.4 %swap.2 = (f32[512,1024]{1,0:T(8,128)S(1)}, f32[512,1024]{1,0:T(8,128)S(1)}) custom-call(bf16[512,1024]{1,0:T(8,128)(2,1)S(1)} %bitcast.47, bf16[512,1024]{1,0:T(8,128)(2,1)S(1)} %bitcast.48), custom_call_target="tpu_custom_call" | custom-call | tf_op jit(solution)/shard_map/swap/pallas_call | solution.py:805
  50.4 1.7 copy-done.19
  52.1 1.7 fusion.35.gate_ref
  53.8 2.6 fusion.34.pre_ref
  57.0 1.1 fusion.17.small_ref
  58.1 47.2 %delta_forward.1 = (bf16[512,512]{1,0:T(8,128)(2,1)}, f32[512,512]{1,0:T(8,128)}, f32[512,512]{1,0:T(8,128)}, f32[8,2,128,256]{3,2,1,0:T(8,128)}, f32[8,2,64,64]{3,2,1,0:T(8,128)}) custom-call(f32[512,1024]{1,0:T(8,128)} %fusion.34.pre_ref, f32[512,512]{1,0:T(8,128)} %fusion.35.gate_ref, f32[512,128]{1,0:T(8,128)} %fusion.17.small_ref, ...), custom_call_target="tpu_custom_call" | custom-call | tf_op jit(solution)/shard_map/delta_forward/pallas_call | solution.py:480
  105.4 1.8 fusion.36.part_ref
  107.1 28.2 %tensor_sum.4 = f32[512,1024]{1,0:T(8,128)S(1)} custom-call(f32[512,1024]{1,0:T(8,128)S(1)} %fusion.36.part_ref), custom_call_target="tpu_custom_call" | custom-call | tf_op jit(solution)/shard_map/tensor_sum/pallas_call | solution.py:724
  139.3 1.4 multiply_convert_fusion.2
  141.8 2.5 fusion.12
  144.3 1.0 fusion.40
  145.3 1.0 convolution_add_fusion.part_ref
  146.3 28.2 %tensor_sum.6 = f32[512,1024]{1,0:T(8,128)S(1)} custom-call(f32[512,1024]{1,0:T(8,128)S(1)} %convolution_add_fusion.part_ref), custom_call_target="tpu_custom_call" | custom-call | tf_op jit(solution)/shard_map/tensor_sum/pallas_call | solution.py:724
  175.1 28.2 %tensor_sum.5 = f32[512,1024]{1,0:T(8,128)S(1)} custom-call(f32[512,1024]{1,0:T(8,128)S(1)} %fusion.39.part_ref), custom_call_target="tpu_custom_call" | custom-call | tf_op jit(solution)/shard_map/tensor_sum/pallas_call | solution.py:724
  203.2 1.9 fusion
  205.1 1.7 fusion.10.grad_ref
  206.9 2.1 fusion.8
  208.9 2.5 fusion.46
  211.4 2.5 fusion.45
  213.9 36.4 %delta_backward.1 = (bf16[512,1024]{1,0:T(8,128)(2,1)}, bf16[512,512]{1,0:T(8,128)(2,1)}, bf16[512,128]{1,0:T(8,128)(2,1)}, f32[4,1024]{1,0:T(4,128)}, f32[1,512]{1,0:T(1,128)}, /*index=5*/f32[1,128]{1,0:T(1,128)}) custom-call(f32[512,1024]{1,0:T(8,128)} %fusion.34.pre_ref, f32[512,512]{1,0:T(8,128)} %fusion.35.gate_ref, f32[512,128]{1,0:T(8,128)} %fusion.17.small_ref, ...), custom_call_target="tpu_custom_call" | custom-call | tf_op jit(solution)/shard_map/delta_backward/pallas_call | solution.py:646
  250.3 2.2 fusion.44
  252.4 3.2 fusion.43
  255.6 3.3 fusion.42
  261.1 3.0 fusion.41
  264.9 28.2 %tensor_sum.7 = f32[512,1024]{1,0:T(8,128)S(1)} custom-call(f32[512,1024]{1,0:T(8,128)S(1)} %add_add_fusion.2.part_ref), custom_call_target="tpu_custom_call" | custom-call | tf_op jit(solution)/shard_map/tensor_sum/pallas_call | solution.py:724
  293.1 1.1 multiply_reduce_fusion.1
  295.2 1.2 copy-done.2
  296.3 55.4 %swap.3 = (f32[512,1024]{1,0:T(8,128)S(1)}, f32[512,1024]{1,0:T(8,128)S(1)}) custom-call(f32[512,1024]{1,0:T(8,128)S(1)} %copy-done.2, f32[512,1024]{1,0:T(8,128)S(1)} %fusion.1.refs_1_), custom_call_target="tpu_custom_call" | custom-call | tf_op jit(solution)/shard_map/swap/pallas_call | solution.py:805
  351.8 1.1 convert_element_type.40
  352.9 51.5 %all-reduce.3 = (f32[1024]{0:T(1024)}, f32[1,128]{1,0:T(1,128)S(1)}, f32[4,1024]{1,0:T(4,128)S(1)}, f32[512]{0:T(512)}, f32[1024]{0:T(1024)}) all-reduce(f32[1024]{0:T(1024)S(1)} %copy-done.30, f32[1,128]{1,0:T(1,128)S(1)} %copy-done.39, f32[4,1024]{1,0:T(4,128)S(1)} %copy-done.31, ...), channel_id=1, replica_groups=mesh['dp'=8,'tensor'=4] {'dp'}, use_global_device_ids=true, to_apply=%region_5.6 | all-reduce | flops 6784 | bytes 54272 | tf_op jit(solution)/shard_map/psum | solution.py:924
  406.2 411.7 %all-reduce.7.cloned.1.call-done = (f32[1024,1024]{1,0:T(8,128)}, f32[1024,512]{1,0:T(8,128)}, f32[1024,128]{1,0:T(8,128)}, f32[512,1024]{1,0:T(8,128)}, f32[102...) async-done(((f32[1024,1024]{1,0:T(8,128)}, f32[1024,512]{1,0:T(8,128)}, f32[1024,128]{1,0:T(8,128)}, f32[512,1024]{1,0:T(8,128)}, f32[1024,704]{0,1:T(8,128)}, ...) | async-done | bytes 17563664 | tf_op jit(solution)/shard_map/psum | solution.py:924
  817.9 3.2 slice.38
  821.1 1.5 fusion.31
  823.6 1.8 copy.39
  826.2 1.3 copy.52
  827.5 1.0 copy-done.16
  828.5 1.3 copy.53
  829.9 1.0 copy-done.15
  830.9 1.3 copy.54
  832.2 1.3 copy-done.13
  833.5 1.6 copy.55
  835.0 1.3 copy-done.12
  836.3 1.6 copy.56
  837.9 1.3 copy-done.11
  839.2 1.6 copy.57
  (104 shorter events, 16.7 us)
Async XLA Ops:
  7.2 132.1 %copy-start = (bf16[704,1024]{1,0:T(8,128)(2,1)S(1)}, bf16[704,1024]{1,0:T(8,128)(2,1)}, u32[]{:S(2)}) copy-start(bf16[704,1024]{1,0:T(8,128)(2,1)} %param.36) | copy-start | bytes 4325380
  7.2 810.7 %all-reduce.7.cloned.1.call-start = ((), (), s32[]{:S(2)}) async-start(), calls=%async_computation | async-start | bytes 35127296 | tf_op jit(solution)/shard_map/psum | solution.py:924
  9.9 1.2 copy-start.3
  11.1 1.2 copy-start.4
  12.3 36.7 %copy-start.24 = (bf16[1024,256]{1,0:T(8,128)(2,1)S(1)}, bf16[1024,256]{1,0:T(8,128)(2,1)}, u32[]{:S(2)}) copy-start(bf16[1024,256]{1,0:T(8,128)(2,1)} %param.22) | copy-start | bytes 1572868
  48.8 1.2 copy-start.21
  49.0 1.1 copy-start.28
  50.1 3.7 copy-start.26
  50.1 2.0 copy-start.19
  52.1 4.8 copy-start.7
  53.8 3.1 copy-start.37
  53.8 3.1 copy-start.32
  53.8 3.2 copy-start.33
  53.8 3.2 copy-start.35
  57.0 1.1 copy-start.27
  58.1 47.3 %copy-start.10 = (bf16[512,1024]{1,0:T(8,128)(2,1)S(1)}, bf16[512,1024]{1,0:T(8,128)(2,1)}, u32[]{:S(2)}) copy-start(bf16[512,1024]{1,0:T(8,128)(2,1)} %param.32) | copy-start | bytes 3145732
  135.3 0.7 copy-start.29
  135.6 1.4 copy-start.41
  137.0 1.4 copy-start.40
  205.1 1.7 copy-start.5
  205.1 1.7 copy-start.14
  213.9 36.4 %copy-start.8 = (bf16[512,1024]{1,0:T(8,128)(2,1)S(1)}, bf16[512,1024]{1,0:T(8,128)(2,1)}, u32[]{:S(2)}) copy-start(bf16[512,1024]{1,0:T(8,128)(2,1)} %copy-done.7) | copy-start | bytes 3145732
  252.4 3.2 copy-start.22
  259.0 0.9 copy-start.25
  259.0 0.9 copy-start.34
  259.0 0.9 copy-start.36
  259.9 1.2 copy-start.23
  261.1 3.0 copy-start.18
  261.1 3.0 copy-start.20
  293.1 1.6 copy-start.6
  294.7 1.7 copy-start.2
  351.7 1.2 copy-start.30
  351.7 1.2 copy-start.31
  351.7 1.2 copy-start.38
  351.7 1.2 copy-start.39
  817.9 3.2 copy-start.9
  821.1 1.5 copy-start.17
  826.2 2.3 copy-start.16
  828.5 2.3 copy-start.15
  830.9 2.6 copy-start.13
  833.5 2.9 copy-start.12
  836.3 2.9 copy-start.11
  836.3 4.4 copy-start.1
Sparse Core Ops, SparseCore 0:
  259.1 558.7 all-reduce.6

commit v2 on v1

--- a/solution.py
+++ b/solution.py
@@ -489,171 +489,145 @@
     )(pre, gate, small, taps, rate, gain)
 
 
-def backward_kernel(heads, key_dim, value_dim, pre_ref, gate_ref, small_ref, taps_ref, rate_ref, gain_ref,
-                    core_ref, update_ref, state_ref, inverse_ref, grad_ref,
-                    low_ref, gate_low_ref, small_low_ref, taps_grad_ref, gain_grad_ref, rate_grad_ref,
-                    ahead_ref, pad_ref, now_ref):
-    length, width = pre_ref.shape
+def backward_start(refs, span):
+    (_, _, _, _, _, _, _, _, _, _, _, _, _, _, taps_grad_ref, gain_grad_ref, rate_grad_ref,
+     _, pad_ref, now_ref) = refs
+    now_ref[...] = jnp.zeros_like(now_ref)
+    pad_ref[span : span + HALO] = jnp.zeros((HALO, pad_ref.shape[1]), jnp.float32)
+    taps_grad_ref[...] = jnp.zeros_like(taps_grad_ref)
+    gain_grad_ref[...] = jnp.zeros_like(gain_grad_ref)
+    rate_grad_ref[...] = jnp.zeros_like(rate_grad_ref)
+
+
+def backward_chunk(heads, key_dim, value_dim, index, refs):
+    (pre_ref, gate_ref, small_ref, taps_ref, rate_ref, gain_ref,
+     core_ref, update_ref, state_ref, inverse_ref, grad_ref,
+     low_ref, gate_low_ref, small_low_ref, taps_grad_ref, gain_grad_ref, rate_grad_ref,
+     ahead_ref, pad_ref, now_ref) = refs
+    width = taps_ref.shape[1]
     span = SPAN
-    chunks = length // span
     rows, cols = grids(span)
     qk = heads * key_dim
     reach = taps_ref.shape[0] - 1
     lanes = small_ref.shape[1]
     lane = lax.broadcasted_iota(jnp.int32, (span, lanes), 1)
+    start = pl.multiple_of(index * span, span)
+    here = pl.ds(start, span)
+    before = pl.ds(pl.multiple_of(jnp.maximum(start - HALO, 0), HALO), HALO)
+    ahead_ref[0:HALO] = pre_ref[before, :] * jnp.where(index > 0, 1.0, 0.0)
+    ahead_ref[HALO : HALO + span] = pre_ref[here, :]
+    total = conv_window(ahead_ref[...], taps_ref[...], span)
+    gain_of = sigmoid(total)
+    active = total * gain_of
+    bend = gain_of * (1.0 + total * (1.0 - gain_of))
+    small = small_ref[here, :]
+    beta, slope, _, cumul = gates_of(small, rate_ref[...], heads, rows, cols)
+    beta_t = jnp.transpose(beta)
+    cumul_t = jnp.transpose(cumul)
+    gate = gate_ref[here, :]
+    gate_sig = sigmoid(gate)
+    gate_silu = gate * gate_sig
+    gate_bend = gate_sig * (1.0 + gate * (1.0 - gate_sig))
+    small_grad = jnp.zeros((span, lanes), jnp.float32)
     for head in range(heads):
-        now_ref[head] = jnp.zeros((key_dim, value_dim), jnp.float32)
-    pad_ref[span : span + HALO] = jnp.zeros((HALO, width), jnp.float32)
-    taps_grad_ref[...] = jnp.zeros_like(taps_grad_ref)
-    gain_grad_ref[...] = jnp.zeros_like(gain_grad_ref)
-    rate_grad_ref[...] = jnp.zeros_like(rate_grad_ref)
-
-    def chunk(turn, carry):
-        index = chunks - 1 - turn
-        start = pl.multiple_of(index * span, span)
-        here = pl.ds(start, span)
-        before = pl.ds(pl.multiple_of(jnp.maximum(start - HALO, 0), HALO), HALO)
-        ahead_ref[0:HALO] = pre_ref[before, :] * jnp.where(index > 0, 1.0, 0.0)
-        ahead_ref[HALO : HALO + span] = pre_ref[here, :]
-        total = conv_window(ahead_ref[...], taps_ref[...], span)
-        gain_of = sigmoid(total)
-        active = total * gain_of
-        bend = gain_of * (1.0 + total * (1.0 - gain_of))
-        small = small_ref[here, :]
-        beta, slope, _, cumul = gates_of(small, rate_ref[...], heads, rows, cols)
-        beta_t = jnp.transpose(beta)
-        cumul_t = jnp.transpose(cumul)
-        gate = gate_ref[here, :]
-        gate_sig = sigmoid(gate)
-        gate_silu = gate * gate_sig
-        gate_bend = gate_sig * (1.0 + gate * (1.0 - gate_sig))
-        small_grad = jnp.zeros((span, lanes), jnp.float32)
-        for head in range(heads):
-            wide = slice(head * value_dim, (head + 1) * value_dim)
-            core = core_ref[here, wide]
-            grad_mixed = grad_ref[here, wide]
-            gain = gain_ref[:, wide]
-            scale = lax.rsqrt(jnp.mean(core * core, -1, keepdims=True) + EPS)
-            normed = core * scale
-            gate_low_ref[here, wide] = (grad_mixed * normed * gain * gate_bend[:, wide]).astype(gate_low_ref.dtype)
-            with_gate = grad_mixed * gate_silu[:, wide]
-            gain_grad_ref[:, wide] += jnp.sum(with_gate * normed, 0, keepdims=True)
-            grad_normed = with_gate * gain
-            grad_core = scale * (grad_normed - normed * jnp.mean(grad_normed * normed, -1, keepdims=True))
-            query_act = active[:, head * key_dim : (head + 1) * key_dim]
-            query_scale = lax.rsqrt(jnp.sum(query_act * query_act, -1, keepdims=True) + EPS)
-            query = query_act * (query_scale * key_dim ** (-0.5))
-            key_act = active[:, qk + head * key_dim : qk + (head + 1) * key_dim]
-            key_scale = lax.rsqrt(jnp.sum(key_act * key_act, -1, keepdims=True) + EPS)
-            key = key_act * key_scale
-            beta_col = beta[:, head : head + 1]
-            beta_row = beta_t[head : head + 1]
-            cum_col = cumul[:, heads + head : heads + head + 1]
-            cum_row = cumul_t[heads + head : heads + head + 1]
-            decays, scaled, key_key, query_key, lower, attend = chunk_terms(
-                query, key, beta_col, beta_row, cum_col, cum_row, rows, cols
-            )
-            state = state_ref[index, head]
-            update = update_ref[here, wide]
-            inverse = inverse_ref[index, head]
-            grad_state = now_ref[head]
-            rise = jnp.exp(cum_col)
-            last = cum_col[span - 1 : span]
-            fall = jnp.exp(last - cum_col)
-            tail = fall * beta_col
-            rise_query = rise * query
-            rise_key = rise * key
-            grad_update = mm_tn(attend, grad_core) + mm(key * tail, grad_state)
-            grad_right = mm_tn(inverse, grad_update)
-            now_ref[head] = jnp.exp(last) * grad_state + mm_tn(rise_query, grad_core) - mm_tn(rise_key, grad_right)
-            grad_attend = jnp.where(cols <= rows, mm_nt(grad_core, update), 0.0)
-            grad_lower = jnp.where(cols < rows, -mm_nt(grad_right, update), 0.0)
-            core_state = mm_nt(grad_core, state)
-            right_state = mm_nt(grad_right, state)
-            grad_tail_key = mm_nt(update, grad_state)
-            pair_query = grad_attend * scaled
-            pair_key = grad_lower * scaled
-            grad_query = rise * core_state + mm(pair_query, key)
-            grad_key = (
-                grad_tail_key * tail - rise * right_state + mm_tn(pair_query, query)
-                + mm(pair_key, key) + mm_tn(pair_key, key)
-            )
-            grad_tail = jnp.sum(grad_tail_key * key, -1, keepdims=True)
-            moved = grad_attend * query_key + grad_lower * key_key
-            spread = moved * scaled
-            by_row = jnp.sum(spread, -1, keepdims=True)
-            sums = mm_tn(
-                jnp.concatenate([moved * decays, spread], 1), jnp.ones((span, lanes), jnp.float32)
-            )
-            grad_beta = sums[:span, 0:1] + grad_tail * fall
-            through_tail = grad_tail * tail
-            grad_cum = (
-                by_row - sums[span:, 0:1] - through_tail
-                + rise * (jnp.sum(core_state * query, -1, keepdims=True) - jnp.sum(right_state * key, -1, keepdims=True))
-            )
-            end_grad = jnp.sum(through_tail, 0, keepdims=True) + jnp.exp(last) * jnp.sum(
-                jnp.sum(state * grad_state, -1, keepdims=True), 0, keepdims=True
-            )
-            grad_cum = grad_cum + jnp.where(rows[:, 0:1] == span - 1, end_grad, 0.0)
-            small_grad = small_grad + jnp.where(lane == head, grad_beta, 0.0)
-            small_grad = small_grad + jnp.where(lane == heads + head, grad_cum, 0.0)
-            grad_query = grad_query * key_dim ** (-0.5)
-            unit = query_act * query_scale
-            grad_query = query_scale * (grad_query - unit * jnp.sum(grad_query * unit, -1, keepdims=True))
-            grad_key = key_scale * (grad_key - key * jnp.sum(grad_key * key, -1, keepdims=True))
-            at = slice(head * key_dim, (head + 1) * key_dim)
-            pad_ref[0:span, at] = grad_query * bend[:, at]
-            at = slice(qk + head * key_dim, qk + (head + 1) * key_dim)
-            pad_ref[0:span, at] = grad_key * bend[:, at]
-            at = slice(2 * qk + head * value_dim, 2 * qk + (head + 1) * value_dim)
-            pad_ref[0:span, at] = grad_right * bend[:, at]
-        summed = mm(jnp.where(cols >= rows, 1.0, 0.0), small_grad)
-        is_beta = lane < heads
-        rate_grad_ref[...] += jnp.sum(jnp.where(is_beta, 0.0, -slope * summed), 0, keepdims=True)
-        sig = beta
-        small_low_ref[here, :] = jnp.where(
-            is_beta, small_grad * sig * (1.0 - sig), -rate_ref[...] * sig * summed
-        ).astype(small_low_ref.dtype)
-        outer = pad_ref[...]
-        dense = outer[0:span]
-        block = ahead_ref[...]
-        grad_pre = None
-        for offset in range(reach + 1):
-            behind = reach - offset
-            taps_grad_ref[offset : offset + 1] += jnp.sum(
-                dense * block[HALO - behind : HALO - behind + span], 0, keepdims=True
-            )
-            term = taps_ref[offset : offset + 1] * outer[behind : behind + span]
-            grad_pre = term if grad_pre is None else grad_pre + term
-        low_ref[here, :] = grad_pre.astype(low_ref.dtype)
-        pad_ref[span : span + HALO] = pad_ref[0:HALO]
-        return carry
-
-    lax.fori_loop(0, chunks, chunk, 0)
-
-
-def delta_backward(pre, gate, small, taps, rate, gain, core, update, state, inverse, grad, heads, key_dim, value_dim):
-    length, width = pre.shape
-    lanes = small.shape[1]
-    out_shape = (
-        jax.ShapeDtypeStruct((length, width), jnp.bfloat16),
-        jax.ShapeDtypeStruct((length, heads * value_dim), jnp.bfloat16),
-        jax.ShapeDtypeStruct((length, lanes), jnp.bfloat16),
-        jax.ShapeDtypeStruct(taps.shape, jnp.float32),
-        jax.ShapeDtypeStruct((1, heads * value_dim), jnp.float32),
-        jax.ShapeDtypeStruct((1, lanes), jnp.float32),
-    )
-    return pl.pallas_call(
-        functools.partial(backward_kernel, heads, key_dim, value_dim),
-        out_shape=out_shape,
-        scratch_shapes=[
-            pltpu.VMEM((HALO + SPAN, width), jnp.float32),
-            pltpu.VMEM((HALO + SPAN, width), jnp.float32),
-            pltpu.VMEM((heads, key_dim, value_dim), jnp.float32),
-        ],
-        compiler_params=pltpu.CompilerParams(vmem_limit_bytes=56 << 20),
-        name="delta_backward",
-    )(pre, gate, small, taps, rate, gain, core, update, state, inverse, grad)
+        wide = slice(head * value_dim, (head + 1) * value_dim)
+        core = core_ref[here, wide]
+        grad_mixed = grad_ref[here, wide]
+        gain = gain_ref[:, wide]
+        scale = lax.rsqrt(jnp.mean(core * core, -1, keepdims=True) + EPS)
+        normed = core * scale
+        gate_low_ref[here, wide] = (grad_mixed * normed * gain * gate_bend[:, wide]).astype(gate_low_ref.dtype)
+        with_gate = grad_mixed * gate_silu[:, wide]
+        gain_grad_ref[:, wide] += jnp.sum(with_gate * normed, 0, keepdims=True)
+        grad_normed = with_gate * gain
+        grad_core = scale * (grad_normed - normed * jnp.mean(grad_normed * normed, -1, keepdims=True))
+        query_act = active[:, head * key_dim : (head + 1) * key_dim]
+        query_scale = lax.rsqrt(jnp.sum(query_act * query_act, -1, keepdims=True) + EPS)
+        query = query_act * (query_scale * key_dim ** (-0.5))
+        key_act = active[:, qk + head * key_dim : qk + (head + 1) * key_dim]
+        key_scale = lax.rsqrt(jnp.sum(key_act * key_act, -1, keepdims=True) + EPS)
+        key = key_act * key_scale
+        beta_col = beta[:, head : head + 1]
+        beta_row = beta_t[head : head + 1]
+        cum_col = cumul[:, heads + head : heads + head + 1]
+        cum_row = cumul_t[heads + head : heads + head + 1]
+        decays, scaled, key_key, query_key, lower, attend = chunk_terms(
+            query, key, beta_col, beta_row, cum_col, cum_row, rows, cols
+        )
+        state = state_ref[index, head]
+        update = update_ref[here, wide]
+        inverse = inverse_ref[index, head]
+        grad_state = now_ref[head]
+        rise = jnp.exp(cum_col)
+        last = cum_col[span - 1 : span]
+        fall = jnp.exp(last - cum_col)
+        tail = fall * beta_col
+        rise_query = rise * query
+        rise_key = rise * key
+        grad_update = mm_tn(attend, grad_core) + mm(key * tail, grad_state)
+        grad_right = mm_tn(inverse, grad_update)
+        now_ref[head] = jnp.exp(last) * grad_state + mm_tn(rise_query, grad_core) - mm_tn(rise_key, grad_right)
+        grad_attend = jnp.where(cols <= rows, mm_nt(grad_core, update), 0.0)
+        grad_lower = jnp.where(cols < rows, -mm_nt(grad_right, update), 0.0)
+        core_state = mm_nt(grad_core, state)
+        right_state = mm_nt(grad_right, state)
+        grad_tail_key = mm_nt(update, grad_state)
+        pair_query = grad_attend * scaled
+        pair_key = grad_lower * scaled
+        grad_query = rise * core_state + mm(pair_query, key)
+        grad_key = (
+            grad_tail_key * tail - rise * right_state + mm_tn(pair_query, query)
+            + mm(pair_key, key) + mm_tn(pair_key, key)
+        )
+        grad_tail = jnp.sum(grad_tail_key * key, -1, keepdims=True)
+        moved = grad_attend * query_key + grad_lower * key_key
+        spread = moved * scaled
+        by_row = jnp.sum(spread, -1, keepdims=True)
+        sums = mm_tn(
+            jnp.concatenate([moved * decays, spread], 1), jnp.ones((span, lanes), jnp.float32)
+        )
+        grad_beta = sums[:span, 0:1] + grad_tail * fall
+        through_tail = grad_tail * tail
+        grad_cum = (
+            by_row - sums[span:, 0:1] - through_tail
+            + rise * (jnp.sum(core_state * query, -1, keepdims=True) - jnp.sum(right_state * key, -1, keepdims=True))
+        )
+        end_grad = jnp.sum(through_tail, 0, keepdims=True) + jnp.exp(last) * jnp.sum(
+            jnp.sum(state * grad_state, -1, keepdims=True), 0, keepdims=True
+        )
+        grad_cum = grad_cum + jnp.where(rows[:, 0:1] == span - 1, end_grad, 0.0)
+        small_grad = small_grad + jnp.where(lane == head, grad_beta, 0.0)
+        small_grad = small_grad + jnp.where(lane == heads + head, grad_cum, 0.0)
+        grad_query = grad_query * key_dim ** (-0.5)
+        unit = query_act * query_scale
+        grad_query = query_scale * (grad_query - unit * jnp.sum(grad_query * unit, -1, keepdims=True))
+        grad_key = key_scale * (grad_key - key * jnp.sum(grad_key * key, -1, keepdims=True))
+        at = slice(head * key_dim, (head + 1) * key_dim)
+        pad_ref[0:span, at] = grad_query * bend[:, at]
+        at = slice(qk + head * key_dim, qk + (head + 1) * key_dim)
+        pad_ref[0:span, at] = grad_key * bend[:, at]
+        at = slice(2 * qk + head * value_dim, 2 * qk + (head + 1) * value_dim)
+        pad_ref[0:span, at] = grad_right * bend[:, at]
+    summed = mm(jnp.where(cols >= rows, 1.0, 0.0), small_grad)
+    is_beta = lane < heads
+    rate_grad_ref[...] += jnp.sum(jnp.where(is_beta, 0.0, -slope * summed), 0, keepdims=True)
+    sig = beta
+    small_low_ref[here, :] = jnp.where(
+        is_beta, small_grad * sig * (1.0 - sig), -rate_ref[...] * sig * summed
+    ).astype(small_low_ref.dtype)
+    outer = pad_ref[...]
+    dense = outer[0:span]
+    block = ahead_ref[...]
+    grad_pre = None
+    for offset in range(reach + 1):
+        behind = reach - offset
+        taps_grad_ref[offset : offset + 1] += jnp.sum(
+            dense * block[HALO - behind : HALO - behind + span], 0, keepdims=True
+        )
+        term = taps_ref[offset : offset + 1] * outer[behind : behind + span]
+        grad_pre = term if grad_pre is None else grad_pre + term
+    low_ref[here, :] = grad_pre.astype(low_ref.dtype)
+    pad_ref[span : span + HALO] = pad_ref[0:HALO]
 
 
 MESH = pl.DeviceIdType.MESH
@@ -818,6 +792,669 @@
     return out
 
 
+SLOT = 64
+DEPTH = 12
+LAG = 1
+
+
+def grid_place():
+    n = lax.axis_size("dp")
+    me = lax.axis_index("dp")
+    t = lax.axis_index("tensor")
+    lines = n // 2
+    z = lax.div(me, 2)
+    x = lax.rem(me, 2)
+    return n, lines, me, t, z, x
+
+
+def grid_greet(extra=()):
+    n, lines, me, t, z, x = grid_place()
+    barrier = pltpu.get_barrier_semaphore()
+    pl.semaphore_signal(barrier, inc=1, device_id=(me + 1 - 2 * x, t), device_id_type=MESH)
+    for peer in extra:
+        pl.semaphore_signal(barrier, inc=1, device_id=peer, device_id_type=MESH)
+
+    @pl.when(z > 0)
+    def _():
+        pl.semaphore_signal(barrier, inc=1, device_id=(me - 2, t), device_id_type=MESH)
+
+    @pl.when(z < lines - 1)
+    def _():
+        pl.semaphore_signal(barrier, inc=1, device_id=(me + 2, t), device_id_type=MESH)
+
+    pl.semaphore_wait(
+        barrier, 1 + len(extra) + jnp.where(z > 0, 1, 0) + jnp.where(z < lines - 1, 1, 0)
+    )
+
+
+def reduce_slot(slot, chunks, data, land_x, land_z, outgo, aside, sems):
+    n, lines, me, t, z, x = grid_place()
+    mate = (me + 1 - 2 * x, t)
+    send_x, recv_x, send_z, recv_z, send_d, recv_d, send_p, recv_p = [sems.at[i] for i in range(8)]
+    top = lines - 1
+
+    def ring(chunk):
+        return lax.rem(chunk, DEPTH)
+
+    def within(chunk):
+        return (chunk >= 0) & (chunk < chunks)
+
+    for stream in range(4):
+        split = stream < 2
+        up = stream % 2 == 0
+        level = z if up else top - z
+        after = (me + 2, t) if up else (me - 2, t)
+        prior = (me - 2, t) if up else (me + 2, t)
+        size = 8 if split else 16
+        offset = 16 * stream
+
+        def rows(chunk, side):
+            base = chunk * SLOT + offset + (side * 8 if split else 0)
+            return pl.ds(pl.multiple_of(base, 8), size)
+
+        def spot(ref, chunk):
+            return ref.at[stream, ring(chunk), 0:size]
+
+        def to_mate(chunk, src):
+            return remote(
+                src, spot(land_x, chunk), send_x.at[stream, ring(chunk)], recv_x.at[stream, ring(chunk)], mate
+            )
+
+        def to_after(chunk):
+            return remote(
+                spot(outgo, chunk), spot(land_z, chunk),
+                send_z.at[stream, ring(chunk)], recv_z.at[stream, ring(chunk)], after,
+            )
+
+        def to_prior(chunk):
+            here = data.at[rows(chunk, x)]
+            return remote(here, here, send_d.at[stream, ring(chunk)], recv_d.at[stream, ring(chunk)], prior)
+
+        def from_after(chunk):
+            here = data.at[rows(chunk, x)]
+            return remote(here, here, send_d.at[stream, ring(chunk)], recv_d.at[stream, ring(chunk)], after)
+
+        def close(chunk, side):
+            here = data.at[rows(chunk, side)]
+            return remote(here, here, send_p.at[stream, ring(chunk)], recv_p.at[stream, ring(chunk)], mate)
+
+        def give_back(chunk):
+            @pl.when(level > 0)
+            def _():
+                to_prior(chunk).start()
+
+            if split:
+                close(chunk, x).start()
+
+        if split:
+            @pl.when(slot < chunks)
+            def _():
+                aside[stream, ring(slot)] = data[rows(slot, 1 - x)]
+                to_mate(slot, aside.at[stream, ring(slot)]).start()
+
+        rise = slot - LAG * (1 + level)
+
+        @pl.when(within(rise))
+        def _():
+            here = rows(rise, x)
+            if split:
+                to_mate(rise, aside.at[stream, ring(rise)]).wait_recv()
+
+            def first():
+                own = data[here]
+                return own + land_x[stream, ring(rise), 0:size] if split else own
+
+            @pl.when(level > 0)
+            def _():
+                to_after(rise).wait_recv()
+                outgo[stream, ring(rise), 0:size] = first() + land_z[stream, ring(rise), 0:size]
+
+            @pl.when(level == 0)
+            def _():
+                outgo[stream, ring(rise), 0:size] = first()
+
+            @pl.when(level < top)
+            def _():
+                to_after(rise).start()
+
+            @pl.when(level == top)
+            def _():
+                if split:
+                    data[here] = outgo[stream, ring(rise), 0:size]
+                    give_back(rise)
+                else:
+                    to_mate(rise, spot(outgo, rise)).start()
+
+        if not split:
+            meet = slot - LAG * (2 + top)
+
+            @pl.when(within(meet) & (level == top))
+            def _():
+                to_mate(meet, spot(outgo, meet)).wait_recv()
+                data[rows(meet, x)] = outgo[stream, ring(meet), 0:size] + land_x[stream, ring(meet), 0:size]
+                give_back(meet)
+
+        extra = 0 if split else 1
+        fall = slot - LAG * (1 + extra + 2 * top - level)
+
+        @pl.when(within(fall) & (level < top))
+        def _():
+            from_after(fall).wait_recv()
+            to_after(fall).wait_send()
+            give_back(fall)
+
+        done = fall - LAG
+
+        @pl.when(within(done))
+        def _():
+            @pl.when(level > 0)
+            def _():
+                to_prior(done).wait_send()
+
+            if split:
+                close(done, x).wait_send()
+                close(done, 1 - x).wait_recv()
+                to_mate(done, aside.at[stream, ring(done)]).wait_send()
+            else:
+                @pl.when(level == top)
+                def _():
+                    to_mate(done, spot(outgo, done)).wait_send()
+
+
+def slots_of(chunks, lines):
+    return chunks + LAG * (2 * lines + 1)
+
+
+def reduce_scratch(width):
+    return [
+        pltpu.VMEM((4, DEPTH, 16, width), jnp.float32),
+        pltpu.VMEM((4, DEPTH, 16, width), jnp.float32),
+        pltpu.VMEM((4, DEPTH, 16, width), jnp.float32),
+        pltpu.VMEM((2, DEPTH, 8, width), jnp.float32),
+        pltpu.SemaphoreType.DMA((8, 4, DEPTH)),
+    ]
+
+
+def reduce_kernel(part_ref, out_ref, land_x, land_z, outgo, aside, sems):
+    grid_greet()
+    chunks = part_ref.shape[0] // SLOT
+
+    def take(i, carry):
+        at = pl.ds(pl.multiple_of(i * SLOT, SLOT), SLOT)
+        out_ref[at] = part_ref[at]
+        return carry
+
+    lax.fori_loop(0, chunks, take, 0)
+
+    def step(slot, carry):
+        reduce_slot(slot, chunks, out_ref, land_x, land_z, outgo, aside, sems)
+        return carry
+
+    lax.fori_loop(0, slots_of(chunks, lax.axis_size("dp") // 2), step, 0)
+
+
+def plane_sum(part, collective_id):
+    rows, width = part.shape
+    return pl.pallas_call(
+        reduce_kernel,
+        out_shape=jax.ShapeDtypeStruct(part.shape, part.dtype),
+        in_specs=[VM],
+        out_specs=VM,
+        scratch_shapes=reduce_scratch(width),
+        compiler_params=pltpu.CompilerParams(
+            collective_id=collective_id, has_side_effects=True, vmem_limit_bytes=60 << 20
+        ),
+        name="plane_sum",
+    )(part)
+
+
+BLOCKS = 8
+
+
+def dot_plain(left, right):
+    return lax.dot_general(left, right, (((1,), (0,)), ((), ())), preferred_element_type=jnp.float32)
+
+
+def dot_nt(left, right):
+    return lax.dot_general(left, right, (((1,), (1,)), ((), ())), preferred_element_type=jnp.float32)
+
+
+def dot_tn(left, right):
+    return lax.dot_general(left, right, (((0,), (0,)), ((), ())), preferred_element_type=jnp.float32)
+
+
+def aligned(start, size):
+    return pl.ds(pl.multiple_of(start, size), size)
+
+
+class TensorSum:
+    def __init__(self, part, total, land_mate, land_across, half, send, recv):
+        self.core, self.mate, self.across = tensor_peers()
+        self.part, self.total, self.half = part, total, half
+        self.land_mate, self.land_across = land_mate, land_across
+        self.send, self.recv = send, recv
+        self.rows = part.shape[0] // BLOCKS
+        self.size = self.rows // 2
+
+    def span(self, block, side):
+        return aligned(block * self.rows + side * self.size, self.size)
+
+    def slot(self, block):
+        return aligned(block * self.size, self.size)
+
+    def first(self, block):
+        return remote(
+            self.part.at[self.span(block, 1 - self.core)], self.land_mate.at[self.slot(block)],
+            self.send.at[0, block], self.recv.at[0, block], self.mate,
+        )
+
+    def second(self, block):
+        return remote(
+            self.half.at[self.slot(block)], self.land_across.at[self.slot(block)],
+            self.send.at[1, block], self.recv.at[1, block], self.across,
+        )
+
+    def third(self, block):
+        mine = self.total.at[self.span(block, self.core)]
+        return remote(mine, mine, self.send.at[2, block], self.recv.at[2, block], self.mate)
+
+    def start(self):
+        for block in range(BLOCKS):
+            self.first(block).start()
+
+    def cross(self, block):
+        self.first(block).wait_recv()
+        slot = self.slot(block)
+        self.half[slot] = self.part[self.span(block, self.core)] + self.land_mate[slot]
+        self.second(block).start()
+
+    def share(self, block):
+        self.second(block).wait_recv()
+        slot = self.slot(block)
+        self.total[self.span(block, self.core)] = self.half[slot] + self.land_across[slot]
+        self.third(block).start()
+
+    def finish(self):
+        for block in range(BLOCKS):
+            self.third(block).wait_recv()
+        for block in range(BLOCKS):
+            self.first(block).wait_send()
+            self.second(block).wait_send()
+            self.third(block).wait_send()
+
+
+class Swap:
+    def __init__(self, source, result, send, recv, close_send, close_recv):
+        self.n = lax.axis_size("dp")
+        self.me = lax.axis_index("dp")
+        self.t = lax.axis_index("tensor")
+        self.ranks = lax.axis_size("tensor")
+        _, self.mate, self.across = tensor_peers()
+        self.source, self.result = source, result
+        self.sems = send, recv, close_send, close_recv
+        self.seg = result.shape[0] // self.n
+        self.part = self.seg // self.ranks
+
+    def at(self, place, rank):
+        return aligned(place * self.seg + rank * self.part, self.part)
+
+    def out(self, k):
+        other = lax.rem(self.me + k, self.n)
+        return remote(
+            self.source.at[self.at(other, self.t)], self.result.at[self.at(self.me, self.t)],
+            self.sems[0].at[k], self.sems[1].at[k], (other, self.t),
+        )
+
+    def close(self, k, leg):
+        origin = lax.rem(self.me + self.n - k, self.n)
+        rank = lax.rem(self.t + 2, self.ranks) if leg == 2 else self.t
+        here = self.result.at[self.at(origin, rank)]
+        return remote(
+            here, here, self.sems[2].at[leg, k], self.sems[3].at[leg, k], self.across if leg == 0 else self.mate
+        )
+
+    def start(self):
+        mine = self.at(self.me, self.t)
+        self.result[mine] = self.source[mine]
+        for k in range(1, self.n):
+            self.out(k).start()
+
+    def gather(self, k):
+        @pl.when(k > 0)
+        def _():
+            self.out(k).wait_recv()
+
+        self.close(k, 0).start()
+        self.close(k, 1).start()
+
+    def forward(self, k):
+        self.close(k, 0).wait_recv()
+        self.close(k, 2).start()
+
+    def finish(self):
+        for k in range(self.n):
+            if k:
+                self.out(k).wait_send()
+            self.close(k, 0).wait_send()
+            self.close(k, 1).wait()
+            self.close(k, 2).wait()
+
+
+def tail_kernel(
+    heads, key_dim, value_dim, ranges, chunks,
+    part2_hbm, ffn_hbm, wide_hbm, rest_hbm, down_hbm, pre_hbm, core_hbm, update_hbm,
+    resid1_ref, upstream_ref, resid_ref, mixed_ref, hidden1_ref,
+    w_out_ref, w_mix_ref, w_gate_ref, w_small_ref, norm1_ref, norm2_ref,
+    gate_ref, small_ref, taps_ref, rate_ref, gain_ref, state_ref, inverse_ref,
+    output_ref, inputs_grad_ref, wide_out, rest_out, down_out, out_out, gate_out,
+    query_out, key_out, value_out, small_out,
+    data, land_x, land_z, outgo, aside, sems,
+    part, total, half, land_mate, land_across, sum_send, sum_recv,
+    resid1_grad, resid1_low, mixed_grad, low, gate_low, small_low,
+    taps_grad, gain_grad, rate_grad, norm1_grad, norm2_grad, ahead, pad, now,
+    shuffled, swap_send, swap_recv, close_send, close_recv, load_sem, out_sem,
+):
+    n, lines, me, t, z, x = grid_place()
+    _, mate, across = tensor_peers()
+    length, width = resid1_ref.shape
+    qk = heads * key_dim
+    values = heads * value_dim
+    at_wide, at_rest, at_down, at_out, at_gate, at_mix, at_small, rows_all = ranges
+    loads = [
+        (part2_hbm, part),
+        (wide_hbm, data.at[pl.ds(at_wide, at_rest - at_wide)]),
+        (rest_hbm, data.at[pl.ds(at_rest, at_down - at_rest)]),
+        (down_hbm, data.at[pl.ds(at_down, at_out - at_down)]),
+        (pre_hbm, data.at[pl.ds(at_mix, length)]),
+        (core_hbm, data.at[pl.ds(at_mix + length, length), pl.ds(0, values)]),
+        (update_hbm, data.at[pl.ds(at_mix + length, length), pl.ds(values, values)]),
+    ]
+    loads = [pltpu.make_async_copy(src, dst, load_sem.at[i]) for i, (src, dst) in enumerate(loads)]
+    load_ffn = pltpu.make_async_copy(ffn_hbm, part, load_sem.at[len(loads)])
+    for load in loads:
+        load.start()
+    greet([(lax.rem(me + k, n), t) for k in range(1, n)] + [mate, across])
+    refs = (
+        data.at[pl.ds(at_mix, length)], gate_ref, small_ref, taps_ref, rate_ref, gain_ref,
+        data.at[pl.ds(at_mix + length, length), pl.ds(0, values)],
+        data.at[pl.ds(at_mix + length, length), pl.ds(values, values)],
+        state_ref, inverse_ref, mixed_grad, low, gate_low, small_low, taps_grad, gain_grad, rate_grad,
+        ahead, pad, now,
+    )
+    sums = [
+        TensorSum(part, total, land_mate, land_across.at[i % 2], half, sum_send.at[i], sum_recv.at[i]) for i in range(3)
+    ]
+    swaps = [
+        Swap(source, result, swap_send.at[i], swap_recv.at[i], close_send.at[i], close_recv.at[i])
+        for i, (source, result) in enumerate([(total, shuffled), (resid1_grad, inputs_grad_ref)])
+    ]
+    norm1_grad[...] = jnp.zeros_like(norm1_grad)
+    norm2_grad[...] = jnp.zeros_like(norm2_grad)
+    backward_start(refs, SPAN)
+    loads[0].wait()
+    sums[0].start()
+    for load in loads[1:]:
+        load.wait()
+
+    def norm_back(value, grad, gain, gain_grad_ref):
+        scale = lax.rsqrt(jnp.mean(value * value, -1, keepdims=True) + EPS)
+        normed = value * scale
+        gain_grad_ref[...] += jnp.sum(grad * normed, 0, keepdims=True)
+        scaled = grad * gain
+        return scale * (scaled - normed * jnp.mean(scaled * normed, -1, keepdims=True))
+
+    def norm2_piece(i):
+        here = aligned(i * 64, 64)
+        grad = upstream_ref[here].astype(jnp.float32) + norm_back(
+            resid1_ref[here], total[here], norm2_ref[...], norm2_grad
+        )
+        resid1_grad[here] = grad
+        resid1_low[here] = grad.astype(jnp.bfloat16)
+
+    def mixed_piece(i):
+        tile = aligned(i * 256, 256)
+        mixed_grad[:, tile] = dot_nt(resid1_low[...], w_out_ref[tile])
+
+    def out_piece(i):
+        tile = aligned(i * 256, 256)
+        data[pl.ds(pl.multiple_of(at_out + i * 256, 64), 256)] = dot_tn(
+            mixed_ref[:, tile], resid1_low[...]
+        )
+
+    def gate_piece(i):
+        tile = aligned(i * 256, 256)
+        half_rows = width // 2
+        data[pl.ds(pl.multiple_of(at_gate + i * 256, 64), 256), 0:values] = dot_tn(hidden1_ref[:, tile], gate_low[...])
+        other = aligned(half_rows + i * 256, 256)
+        data[pl.ds(pl.multiple_of(at_gate + i * 256, 64), 256), values : 2 * values] = dot_tn(
+            hidden1_ref[:, other], gate_low[...]
+        )
+
+    def mix_piece(i):
+        tile = aligned(i * 256, 256)
+        data[pl.ds(pl.multiple_of(at_mix + i * 256, 64), 256)] = dot_tn(hidden1_ref[:, tile], low[...])
+
+    def hidden_piece(i):
+        tile = aligned(i * 256, 256)
+        part[:, tile] = (
+            dot_nt(low[...], w_mix_ref[tile]) + dot_nt(gate_low[...], w_gate_ref[tile])
+            + dot_nt(small_low[...], w_small_ref[tile])
+        )
+
+    def output_piece(i):
+        here = aligned(i * 64, 64)
+        total[here] = total[here] + resid1_ref[here]
+
+    def round_piece(i):
+        here = aligned(i * 64, 64)
+        output_ref[here] = shuffled[here].astype(output_ref.dtype)
+
+    def norm1_piece(i):
+        here = aligned(i * 64, 64)
+        resid1_grad[here] = resid1_grad[here] + norm_back(
+            resid_ref[here].astype(jnp.float32), total[here], norm1_ref[...], norm1_grad
+        )
+
+    def small_piece():
+        base = at_small
+        data[base : rows_all] = jnp.zeros((rows_all - base, width), jnp.float32)
+        data[base : base + 4] = taps_grad[...]
+        data[base + 4 : base + 5] = norm1_grad[...]
+        data[base + 5 : base + 6] = norm2_grad[...]
+        data[base + 6 : base + 7, 0:values] = gain_grad[...]
+        data[base + 6 : base + 7, values : values + rate_grad.shape[1]] = rate_grad[...]
+        data[base + 8 : base + 16] = dot_tn(small_low[...], hidden1_ref[...])[0:8]
+
+    def start_ffn():
+        load_ffn.start()
+        load_ffn.wait()
+        sums[1].start()
+
+    pieces = []
+
+    def plan(first, count, each, run):
+        pieces.append((first, count, each, run))
+        return first + -(-count // each)
+
+    at = plan(0, BLOCKS, 2, sums[0].cross)
+    at = plan(at, BLOCKS, 2, sums[0].share)
+    at = plan(at, 1, 1, lambda i: sums[0].finish())
+    at = plan(at, length // 64, 2, norm2_piece)
+    at = plan(at, values // 256, 1, mixed_piece)
+    side = at
+    at = plan(at, values // 256, 1, out_piece)
+    at_ready_out = at
+    at = plan(at, length // SPAN, 1, lambda i: backward_chunk(heads, key_dim, value_dim, length // SPAN - 1 - i, refs))
+    side = plan(side, 1, 1, lambda i: start_ffn())
+    side = plan(side, BLOCKS, 2, sums[1].cross)
+    side = plan(side, BLOCKS, 2, sums[1].share)
+    side = plan(side, 1, 1, lambda i: sums[1].finish())
+    part_free = side
+    side = plan(side, length // 64, 4, output_piece)
+    side = plan(side, 1, 1, lambda i: swaps[0].start())
+    side = plan(side, n, 2, swaps[0].gather)
+    side = plan(side, n, 2, swaps[0].forward)
+    side = plan(side, 1, 1, lambda i: swaps[0].finish())
+    side = plan(side, length // 64, 4, round_piece)
+    at = plan(at, width // 512, 1, gate_piece)
+    at_ready_gate = at
+    at = plan(at, width // 256, 1, mix_piece)
+    at_ready_mix = at
+    at = plan(max(at, part_free), width // 256, 1, hidden_piece)
+    at = plan(max(at, side), 1, 1, lambda i: sums[2].start())
+    at = plan(at, BLOCKS, 2, sums[2].cross)
+    at = plan(at, BLOCKS, 2, sums[2].share)
+    at = plan(at, 1, 1, lambda i: sums[2].finish())
+    at = plan(at, length // 64, 2, norm1_piece)
+    at = plan(at, 1, 1, lambda i: small_piece())
+    at_ready_small = at
+    at = plan(at, 1, 1, lambda i: swaps[1].start())
+    at = plan(at, n, 2, swaps[1].gather)
+    at = plan(at, n, 2, swaps[1].forward)
+    at = plan(at, 1, 1, lambda i: swaps[1].finish())
+    assert at_ready_out <= at_out // SLOT and at_ready_gate <= at_gate // SLOT
+    assert at_ready_mix <= at_mix // SLOT and at_ready_small <= at_small // SLOT
+    delay = 2 * lines + 1
+    last = max(chunks + delay + 1, at)
+
+    def writes(chunk, act):
+        row = chunk * SLOT
+
+        def put(sem, src_cols, dst, start):
+            rows = pl.ds(pl.multiple_of(row, SLOT), SLOT)
+            src = data.at[rows] if src_cols is None else data.at[rows, pl.ds(*src_cols)]
+            copy = pltpu.make_async_copy(src, dst.at[pl.ds(pl.multiple_of(row - start, SLOT), SLOT)], out_sem.at[sem])
+            copy.start() if act == "start" else copy.wait()
+
+        def segment(low_row, high_row, run):
+            @pl.when((row >= low_row) & (row < high_row))
+            def _():
+                run()
+
+        segment(at_wide, at_rest, lambda: put(0, None, wide_out, at_wide))
+        segment(at_rest, at_down, lambda: put(0, None, rest_out, at_rest))
+        segment(at_down, at_out, lambda: put(0, None, down_out, at_down))
+        segment(at_out, at_gate, lambda: put(0, None, out_out, at_out))
+
+        def gates():
+            put(0, (0, values), gate_out, at_gate)
+            put(1, (values, values), gate_out, at_gate - width // 2)
+
+        segment(at_gate, at_mix, gates)
+
+        def mixes():
+            put(0, (0, qk), query_out, at_mix)
+            put(1, (qk, qk), key_out, at_mix)
+            put(2, (2 * qk, values), value_out, at_mix)
+
+        segment(at_mix, at_small, mixes)
+        segment(at_small, rows_all, lambda: put(0, None, small_out, at_small))
+
+    def step(slot, carry):
+        reduce_slot(slot, chunks, data, land_x, land_z, outgo, aside, sems)
+        writes(slot - delay - 1, "wait")
+        writes(slot - delay, "start")
+        for first, count, each, run in pieces:
+            steps = -(-count // each)
+
+            @pl.when((slot >= first) & (slot < first + steps))
+            def _(first=first, each=each, run=run):
+                if each == 1:
+                    run(slot - first)
+                else:
+                    def inner(i, carry):
+                        run((slot - first) * each + i)
+                        return carry
+
+                    lax.fori_loop(0, each, inner, 0)
+
+        return carry
+
+    lax.fori_loop(0, last + 1, step, 0)
+
+
+def tail(
+    part2, ffn, wide, rest, down, pre, core, update, resid1, upstream, resid, mixed, hidden1,
+    w_out, w_mix, w_gate, w_small, norm1, norm2, gate, small, taps, rate, gain, states, inverses,
+    heads, key_dim, value_dim, places, collective_id,
+):
+    length, width = resid1.shape
+    values = heads * value_dim
+    qk = heads * key_dim
+    lanes = small.shape[1]
+    heights = [wide.shape[0], rest.shape[0], down.shape[0], values, values, width, SLOT]
+    ranges = [0]
+    for height in heights:
+        ranges.append(ranges[-1] + height)
+    rows_all = ranges[-1]
+    chunks = rows_all // SLOT
+    f32, bf = jnp.float32, jnp.bfloat16
+    shape = jax.ShapeDtypeStruct
+    out_shape = [
+        shape((length, width), bf),
+        shape((length, width), f32),
+        shape(wide.shape, f32),
+        shape(rest.shape, f32),
+        shape(down.shape, f32),
+        shape((values, width), f32),
+        shape((width, values), f32),
+        shape((width, qk), f32),
+        shape((width, qk), f32),
+        shape((width, values), f32),
+        shape((SLOT, width), f32),
+    ]
+    vmem, any_ = VM, pl.BlockSpec(memory_space=pl.ANY)
+    dma = pltpu.SemaphoreType.DMA
+    scratch = (
+        [pltpu.VMEM((rows_all, width), f32)]
+        + reduce_scratch(width)
+        + [
+            pltpu.VMEM((length, width), f32),
+            pltpu.VMEM((length, width), f32),
+            pltpu.VMEM((length // 2, width), f32),
+            pltpu.VMEM((length // 2, width), f32),
+            pltpu.VMEM((2, length // 2, width), f32),
+            dma((3, 3, BLOCKS)),
+            dma((3, 3, BLOCKS)),
+            pltpu.VMEM((length, width), f32),
+            pltpu.VMEM((length, width), bf),
+            pltpu.VMEM((length, values), f32),
+            pltpu.VMEM((length, width), bf),
+            pltpu.VMEM((length, values), bf),
+            pltpu.VMEM((length, lanes), bf),
+            pltpu.VMEM(taps.shape, f32),
+            pltpu.VMEM((1, values), f32),
+            pltpu.VMEM((1, lanes), f32),
+            pltpu.VMEM((1, width), f32),
+            pltpu.VMEM((1, width), f32),
+            pltpu.VMEM((HALO + SPAN, width), f32),
+            pltpu.VMEM((HALO + SPAN, width), f32),
+            pltpu.VMEM((heads, key_dim, value_dim), f32),
+            pltpu.VMEM((length, width), f32),
+            dma((2, places)),
+            dma((2, places)),
+            dma((2, 3, places)),
+            dma((2, 3, places)),
+            dma((8,)),
+            dma((3,)),
+        ]
+    )
+    return pl.pallas_call(
+        functools.partial(tail_kernel, heads, key_dim, value_dim, tuple(ranges[:7]) + (rows_all,), chunks),
+        out_shape=out_shape,
+        in_specs=[any_] * 8 + [vmem] * 18,
+        out_specs=[vmem] * 2 + [any_] * 9,
+        scratch_shapes=scratch,
+        compiler_params=pltpu.CompilerParams(
+            collective_id=collective_id, has_side_effects=True, vmem_limit_bytes=67043328
+        ),
+        name="tail",
+    )(
+        part2, ffn, wide, rest, down, pre, core, update, resid1, upstream, resid, mixed, hidden1,
+        w_out, w_mix, w_gate, w_small, norm1, norm2, gate, small, taps, rate, gain, states, inverses,
+    )
+
+
 def lane_pad(array, lanes):
     return jnp.pad(array, ((0, 0), (0, lanes - array.shape[1])))
 
@@ -881,90 +1518,60 @@
     grad_fgate, grad_fup = swiglu_back(grad_inner)
     grad_fgate = grad_fgate.astype(bf)
     grad_fup = grad_fup.astype(bf)
-    grad_hidden2 = tensor_sum(
-        back_project(grad_fgate, w_ffn_gate) + back_project(grad_fup, w_ffn_up), 3
-    )
-    ffn = tensor_sum(project(inner, w_ffn_down), 4)
-    grad_down = contract_rows(inner, upstream_low)
-    grad_ffn_gate_w = contract_rows(hidden2, grad_fgate)
-    grad_ffn_up_w = contract_rows(hidden2, grad_fup)
-    grad_from_norm2, grad_norm2_gain = norm2_back(grad_hidden2)
-    grad_resid1 = upstream + grad_from_norm2
-    grad_resid1_low = grad_resid1.astype(bf)
-    grad_out_w = contract_rows(mixed, grad_resid1_low)
-    grad_mixed = back_project(grad_resid1_low, w_out)
-    low, gate_low, small_low, grad_taps, grad_head, grad_rate = delta_backward(
-        pre, gate_pre, small, taps, rate, gain, core, update, states, inverses, grad_mixed,
-        heads, key_dim, value_dim,
-    )
-    partial_hidden1 = (
-        back_project(low, w_mix) + back_project(gate_low, w_gate) + back_project(small_low, w_small)
-    )
-    grad_hidden1 = tensor_sum(partial_hidden1, 5)
-    grad_from_norm1, grad_norm1_gain = norm1_back(grad_hidden1)
-    output, grad_inputs = swap([resid1 + ffn, grad_resid1 + grad_from_norm1], places, 6)
-    output = output.reshape(batch, seg, width).astype(bf)
-    grad_inputs = grad_inputs.reshape(batch, seg, width)
-    grad_mix_w = contract_rows(hidden1, low)
-    grad_gate_w = contract_rows(hidden1, gate_low)
-    grad_small_w = contract_rows(hidden1, small_low)
+    grad_wide = jnp.concatenate([grad_fgate, grad_fup], axis=1)
+    units = inner.shape[1]
+    part2 = back_project(grad_wide, jnp.concatenate([w_ffn_gate, w_ffn_up], axis=1))
+    wide = contract_rows(hidden2, grad_wide[:, :width])
+    rest = contract_rows(grad_wide[:, width:], hidden2)
+    down = contract_rows(inner, upstream_low)
+    ffn = project(inner, w_ffn_down)
     (
-        grad_norm1_gain,
-        grad_mix_w,
+        output, grad_inputs, wide, rest, grad_down, grad_out_w, grad_gate_w,
+        grad_query_w, grad_key_w, grad_value_w, rows,
+    ) = tail(
+        part2, ffn, wide, rest, down, pre, core, update, resid1, upstream_low, resid.astype(bf), mixed, hidden1,
+        w_out, w_mix, w_gate, w_small, norm1_gain[None], norm2_gain[None],
+        gate_pre, small, taps, rate, gain, states, inverses,
+        heads, key_dim, value_dim, places, 7,
+    )
+    grad_taps = rows[0:4]
+    grad_small_w = rows[8 : 8 + 2 * heads]
+    wide_full = jnp.concatenate([wide, rest.T], axis=1)
+    return (
+        output.reshape(batch, seg, width),
+        grad_inputs.reshape(batch, seg, width),
+        rows[4],
+        grad_query_w,
+        grad_key_w,
+        grad_value_w,
         grad_gate_w,
-        grad_small_w,
-        grad_rate,
-        grad_taps,
-        grad_head,
-        grad_out_w,
-        grad_norm2_gain,
-        grad_ffn_gate_w,
-        grad_ffn_up_w,
-        grad_down,
-    ) = lax.psum(
-        (
-            grad_norm1_gain,
-            grad_mix_w,
-            grad_gate_w,
-            grad_small_w,
-            grad_rate,
-            grad_taps,
-            grad_head,
-            grad_out_w,
-            grad_norm2_gain,
-            grad_ffn_gate_w,
-            grad_ffn_up_w,
-            grad_down,
-        ),
-        "dp",
-    )
-    return (
-        output,
-        grad_inputs,
-        grad_norm1_gain,
-        grad_mix_w[:, :qk_width],
-        grad_mix_w[:, qk_width : 2 * qk_width],
-        grad_mix_w[:, 2 * qk_width :],
-        grad_gate_w,
-        grad_small_w[:, :heads],
-        grad_small_w[:, heads : 2 * heads],
-        grad_rate[0, heads : 2 * heads],
+        grad_small_w[:heads].T,
+        grad_small_w[heads:].T,
+        rows[6, heads * value_dim + heads : heads * value_dim + 2 * heads],
         grad_taps[:, :qk_width],
         grad_taps[:, qk_width : 2 * qk_width],
         grad_taps[:, 2 * qk_width :],
-        grad_head[0],
+        rows[6, : heads * value_dim],
         grad_out_w,
-        grad_norm2_gain,
-        grad_ffn_gate_w,
-        grad_ffn_up_w,
+        rows[5],
+        wide_full[:, :units],
+        wide_full[:, units:],
         grad_down,
     )
 
 
 def fits_whole(mesh, args):
-    batch, length, _ = args[0].shape
+    batch, length, width = args[0].shape
     places, ranks = mesh.shape["dp"], mesh.shape["tensor"]
-    return batch == places and ranks == 4 and length % (places * ranks * 16) == 0 and length % SPAN == 0
+    heads = args[8].shape[0] // ranks
+    qk = args[2].shape[1] // ranks
+    values = args[4].shape[1] // ranks
+    units = args[15].shape[1] // ranks
+    return (
+        batch == places and places == 8 and ranks == 4 and length == places * SPAN and heads <= 4
+        and width == 2 * qk + values and width == 2 * values and width % 512 == 0 and length % 256 == 0
+        and 2 * units > width and (2 * units - width) % SLOT == 0 and units % SLOT == 0 and values % 256 == 0
+    )
 
 
 def solution(mesh):

time: 848 us -> 542 us (0.64)
  waiting for transfers between devices: 412 us -> 0 us
  Pallas kernels: 288 us -> 467 us
  blocking collectives: 51.5 us -> 0 us
  matrix products: 37.6 us -> 23.6 us
  between operations: 14.5 us -> 0.91 us
    psum x1 -> x0, waiting for transfers between devices: 412 us -> none  [whole_sequences(): lax.psum((grad_norm1_gain, grad_mix_w, grad_gate_w, grad_small_w, grad_ra...]
    pallas_call x1, Pallas kernels: 36.4 us -> 355 us  [tail(): pl.pallas_call(functools.partial(tail_kernel, heads, key_dim, value_dim,...]
    pallas_call x4 -> x1, Pallas kernels: 113 us -> 28.2 us  [tensor_sum(): pl.pallas_call(functools.partial(psum_kernel, blocks), out_shape=jax.Shap...]
    pallas_call x2 -> x1, Pallas kernels: 91.8 us -> 36.4 us  [swap(): pl.pallas_call(functools.partial(swap_kernel, count, narrow), out_shape=[...]
    psum x1 -> x0, blocking collectives: 51.5 us -> none  [whole_sequences(): lax.psum((grad_norm1_gain, grad_mix_w, grad_gate_w, grad_small_w, grad_ra...]
    dot_general x7 -> x3, matrix products: 18.2 us -> 7.58 us  [contract_rows(): jnp.einsum('ra,rb->ab', left, right, preferred_element_type=jnp.float32)]
    unnamed x96 -> x60, local copies, waits for them, and re-layouts: 29.1 us -> 26.5 us
  transfers between devices with their start and end apart: 1 -> 0, of which waited for: 1 -> 0; matrix products, arithmetic and copies ran while one was open for 1% -> 0% of each run, Pallas kernels for 10% -> 0%
where the time goes in v2:
time: 542 us; the launch traced here: 541 us
  Pallas kernels  467 us (86%)
  local copies, waits for them, and re-layouts  40.7 us (8%)
  matrix products  23.6 us (4%)
  other arithmetic  8.49 us (2%)
    pallas_call x1, Pallas kernels, tail(): pl.pallas_call(functools.partial(tail_kernel, heads, key_dim, value_dim,...  355 us
    pallas_call x1, Pallas kernels, delta_forward(): pl.pallas_call(functools.partial(forward_kernel, heads, key_dim, value_di...  47.4 us
    pallas_call x1, Pallas kernels, swap(): pl.pallas_call(functools.partial(swap_kernel, count, narrow), out_shape=[...  36.4 us
    pallas_call x1, Pallas kernels, tensor_sum(): pl.pallas_call(functools.partial(psum_kernel, blocks), out_shape=jax.Shap...  28.2 us
    unnamed x60, local copies, waits for them, and re-layouts  26.5 us
    dot_general x7, matrix products, project(): return jnp.dot(left, right, preferred_element_type=jnp.float32)  11.9 us

profile of v2, /device:TPU:0, one launch (start us, length us, event | category | flops | bytes accessed | tf_op | source)
XLA Modules:
  0.0 540.8 jit_solution(2542027029280153497)
XLA Ops:
  0.7 0.8 pad_bitcast_fusion
  1.5 0.5 pad.14.rate_ref
  2.0 0.7 pad_maximum_fusion.1
  2.8 0.7 constant_dynamic-update-slice_fusion.5
  3.4 0.7 constant_dynamic-update-slice_fusion.4
  4.1 0.7 constant_dynamic-update-slice_fusion.3.taps_ref
  5.1 0.8 pad.12.w_small_ref
  5.8 1.2 constant_dynamic-update-slice_fusion.2
  7.5 36.4 %swap.1 = (f32[512,1024]{1,0:T(8,128)S(1)}, f32[512,1024]{1,0:T(8,128)S(1)}) custom-call(bf16[512,1024]{1,0:T(8,128)(2,1)S(1)} %bitcast.38, bf16[512,1024]{1,0:T(8,128)(2,1)S(1)} %bitcast.39), custom_call_target="tpu_custom_call" | custom-call | tf_op jit(solution)/shard_map/swap/pallas_call | solution.py:779
  44.9 1.2 fusion.19.small_ref
  46.1 1.7 fusion.26.gate_ref
  47.7 0.9 fusion.24
  48.7 2.6 fusion.25.pre_ref.pre_hbm
  51.3 47.4 %delta_forward.1 = (bf16[512,512]{1,0:T(8,128)(2,1)}, f32[512,512]{1,0:T(8,128)}, f32[512,512]{1,0:T(8,128)}, f32[8,2,128,256]{3,2,1,0:T(8,128)}, f32[8,2,64,64]{3,2,1,0:T(8,128)}) custom-call(f32[512,1024]{1,0:T(8,128)} %fusion.25.pre_ref.pre_hbm, f32[512,512]{1,0:T(8,128)} %fusion.26.gate_ref, f32[512,128]{1,0:T(8,128)} %fusion.19.small_ref, ...), custom_call_target="tpu_custom_call" | custom-call | tf_op jit(solution)/shard_map/delta_forward/pallas_call | solution.py:480
  98.7 1.8 fusion.27.part_ref
  100.5 28.2 %tensor_sum.1 = f32[512,1024]{1,0:T(8,128)S(1)} custom-call(f32[512,1024]{1,0:T(8,128)S(1)} %fusion.27.part_ref), custom_call_target="tpu_custom_call" | custom-call | tf_op jit(solution)/shard_map/tensor_sum/pallas_call | solution.py:698
  128.7 1.3 multiply_reduce_fusion
  130.3 1.9 copy-done.22
  132.1 0.9 fusion.28
  133.5 1.5 multiply_convert_fusion.2
  135.0 1.7 fusion.15.rest_hbm
  136.7 2.3 fusion.29.ffn_hbm
  139.1 3.2 fusion.part2_hbm
  142.2 3.3 fusion.11.wide_hbm
  145.6 2.5 fusion.30.down_hbm
  148.1 355.0 %tail.1 = (bf16[512,1024]{1,0:T(8,128)(2,1)}, f32[512,1024]{1,0:T(8,128)}, f32[1024,1024]{1,0:T(8,128)}, f32[384,1024]{1,0:T(8,128)}, f32[704,1024]{1,0:T(8,128)...) custom-call(f32[512,1024]{1,0:T(8,128)} %fusion.part2_hbm, ...), custom_call_target="tpu_custom_call" | custom-call | tf_op jit(solution)/shard_map/tail/pallas_call | solution.py:1442
  503.1 1.3 slice_bitcast_fusion.2
  504.4 1.3 slice.55
  505.6 1.3 slice.54
  507.0 1.3 fusion.22
  508.3 1.4 fusion.21
  509.7 1.4 slice_bitcast_fusion
  511.2 3.0 copy.44
  514.2 5.6 %pad_maximum_fusion = (f32[1024,704]{1,0:T(8,128)}, f32[1024,704]{1,0:T(8,128)S(1)}) fusion(f32[1024,384]{1,0:T(8,128)} %copy.44, f32[1024,1024]{1,0:T(8,128)} %get-tuple-element.52), kind=kLoop, calls=%fused_computation | loop fusion | flops 720896 | bytes 14680064 | tf_op jit(solution)/shard_map/concatenate | solution.py:1539
  519.8 3.4 copy.46
  523.2 2.2 copy.45
  525.4 2.4 copy.59
  527.9 1.3 copy.60
  529.2 0.6 copy-done.15
  529.8 1.0 copy.61
  530.8 1.0 copy.62
  531.9 1.3 copy.63
  533.2 1.0 copy-done.9
  534.3 1.3 copy.64
  535.6 1.0 copy-done.8
  536.6 1.3 copy.65
  537.9 1.3 copy-done.7
  539.2 1.6 copy.66
  (50 shorter events, 2.3 us)
Async XLA Ops:
  0.7 6.5 %copy-start.13 = (bf16[1024,512]{1,0:T(8,128)(2,1)S(1)}, bf16[1024,512]{1,0:T(8,128)(2,1)}, u32[]{:S(2)}) copy-start(bf16[1024,512]{1,0:T(8,128)(2,1)} %param.23) | copy-start | bytes 3145732
  0.7 6.4 %copy-start.16 = (bf16[1024,256]{1,0:T(8,128)(2,1)S(1)}, bf16[1024,256]{1,0:T(8,128)(2,1)}, u32[]{:S(2)}) copy-start(bf16[1024,256]{1,0:T(8,128)(2,1)} %param.22) | copy-start | bytes 1572868
  4.8 2.5 copy-start.17
  5.8 1.5 copy-start
  5.8 1.7 copy-start.1
  7.5 41.2 %copy-start.6 = (bf16[1024,1024]{1,0:T(8,128)(2,1)}, bf16[1024,1024]{1,0:T(8,128)(2,1)S(1)}, u32[]{:S(2)}) copy-start(bf16[1024,1024]{1,0:T(8,128)(2,1)S(1)} %constant_dynamic-update-slice_fusion.w_mix_ref) | copy-start | bytes 6291460
  44.0 0.7 copy-start.18
  44.1 101.4 %copy-start.4 = (bf16[512,1024]{1,0:T(8,128)(2,1)}, bf16[512,1024]{1,0:T(8,128)(2,1)S(1)}, u32[]{:S(2)}) copy-start(bf16[512,1024]{1,0:T(8,128)(2,1)S(1)} %convert_element_type.27.upstream_ref) | copy-start | bytes 3145732
  44.6 1.4 copy-start.12
  44.9 3.8 copy-start.3
  46.1 1.7 copy-start.20
  51.3 47.4 %copy-start.5 = (bf16[512,1024]{1,0:T(8,128)(2,1)S(1)}, bf16[512,1024]{1,0:T(8,128)(2,1)}, u32[]{:S(2)}) copy-start(bf16[512,1024]{1,0:T(8,128)(2,1)} %w_out_ref.1) | copy-start | bytes 3145732
  128.7 1.4 copy-start.19
  130.0 3.1 copy-start.2
  130.0 2.1 copy-start.22
  132.1 1.4 copy-start.21
  525.4 2.4 copy-start.11
  527.9 2.0 copy-start.15
  527.9 2.9 copy-start.14
  529.8 2.1 copy-start.10
  531.9 2.3 copy-start.9
  534.3 2.3 copy-start.8
  536.6 2.6 copy-start.7

commit v3 on v2

--- a/solution.py
+++ b/solution.py
@@ -402,6 +402,15 @@
     return beta, slope, logdecay, cumul
 
 
+def state_place(index, head, heads, key_dim, value_dim, width):
+    across = width // value_dim
+    turn = index * heads + head
+    return (
+        pl.ds(pl.multiple_of(lax.div(turn, across) * key_dim, key_dim), key_dim),
+        pl.ds(pl.multiple_of(lax.rem(turn, across) * value_dim, value_dim), value_dim),
+    )
+
+
 def chunk_terms(query, key, beta_col, beta_row, cum_col, cum_row, rows, cols):
     within = cols <= rows
     decays = jnp.where(within, jnp.exp(jnp.where(within, cum_col - cum_row, 0.0)), 0.0)
@@ -449,7 +458,7 @@
             _, _, _, _, lower, attend = chunk_terms(query, key, beta_col, beta_row, cum_col, cum_row, rows, cols)
             inverse = unit_inverse(lower, rows, cols)
             state = now_ref[head]
-            state_ref[index, head] = state
+            state_ref[state_place(index, head, heads, key_dim, value_dim, width)] = state
             rise = jnp.exp(cum_col)
             last = cum_col[span - 1 : span]
             update = mm(inverse, value) - mm(mm(inverse, rise * key), state)
@@ -474,7 +483,7 @@
         jax.ShapeDtypeStruct((length, heads * value_dim), jnp.bfloat16),
         jax.ShapeDtypeStruct((length, heads * value_dim), jnp.float32),
         jax.ShapeDtypeStruct((length, heads * value_dim), jnp.float32),
-        jax.ShapeDtypeStruct((chunks, heads, key_dim, value_dim), jnp.float32),
+        jax.ShapeDtypeStruct((chunks * heads * key_dim * value_dim // width, width), jnp.float32),
         jax.ShapeDtypeStruct((chunks, heads, SPAN, SPAN), jnp.float32),
     )
     return pl.pallas_call(
@@ -554,7 +563,7 @@
         decays, scaled, key_key, query_key, lower, attend = chunk_terms(
             query, key, beta_col, beta_row, cum_col, cum_row, rows, cols
         )
-        state = state_ref[index, head]
+        state = state_ref[state_place(index, head, heads, key_dim, value_dim, width)]
         update = update_ref[here, wide]
         inverse = inverse_ref[index, head]
         grad_state = now_ref[head]
@@ -827,7 +836,7 @@
     )
 
 
-def reduce_slot(slot, chunks, data, land_x, land_z, outgo, aside, sems):
+def reduce_slot(slot, chunks, data, split_rings, whole_rings, aside, sems):
     n, lines, me, t, z, x = grid_place()
     mate = (me + 1 - 2 * x, t)
     send_x, recv_x, send_z, recv_z, send_d, recv_d, send_p, recv_p = [sems.at[i] for i in range(8)]
@@ -846,6 +855,8 @@
         after = (me + 2, t) if up else (me - 2, t)
         prior = (me - 2, t) if up else (me + 2, t)
         size = 8 if split else 16
+        land_x, land_z, outgo = (split_rings if split else whole_rings)
+        lane = stream % 2
         offset = 16 * stream
 
         def rows(chunk, side):
@@ -853,7 +864,7 @@
             return pl.ds(pl.multiple_of(base, 8), size)
 
         def spot(ref, chunk):
-            return ref.at[stream, ring(chunk), 0:size]
+            return ref.at[lane, ring(chunk)]
 
         def to_mate(chunk, src):
             return remote(
@@ -902,16 +913,16 @@
 
             def first():
                 own = data[here]
-                return own + land_x[stream, ring(rise), 0:size] if split else own
+                return own + land_x[lane, ring(rise)] if split else own
 
             @pl.when(level > 0)
             def _():
                 to_after(rise).wait_recv()
-                outgo[stream, ring(rise), 0:size] = first() + land_z[stream, ring(rise), 0:size]
+                outgo[lane, ring(rise)] = first() + land_z[lane, ring(rise)]
 
             @pl.when(level == 0)
             def _():
-                outgo[stream, ring(rise), 0:size] = first()
+                outgo[lane, ring(rise)] = first()
 
             @pl.when(level < top)
             def _():
@@ -920,7 +931,7 @@
             @pl.when(level == top)
             def _():
                 if split:
-                    data[here] = outgo[stream, ring(rise), 0:size]
+                    data[here] = outgo[lane, ring(rise)]
                     give_back(rise)
                 else:
                     to_mate(rise, spot(outgo, rise)).start()
@@ -931,7 +942,7 @@
             @pl.when(within(meet) & (level == top))
             def _():
                 to_mate(meet, spot(outgo, meet)).wait_recv()
-                data[rows(meet, x)] = outgo[stream, ring(meet), 0:size] + land_x[stream, ring(meet), 0:size]
+                data[rows(meet, x)] = outgo[lane, ring(meet)] + land_x[lane, ring(meet)]
                 give_back(meet)
 
         extra = 0 if split else 1
@@ -966,46 +977,11 @@
 
 
 def reduce_scratch(width):
-    return [
-        pltpu.VMEM((4, DEPTH, 16, width), jnp.float32),
-        pltpu.VMEM((4, DEPTH, 16, width), jnp.float32),
-        pltpu.VMEM((4, DEPTH, 16, width), jnp.float32),
-        pltpu.VMEM((2, DEPTH, 8, width), jnp.float32),
-        pltpu.SemaphoreType.DMA((8, 4, DEPTH)),
-    ]
-
-
-def reduce_kernel(part_ref, out_ref, land_x, land_z, outgo, aside, sems):
-    grid_greet()
-    chunks = part_ref.shape[0] // SLOT
-
-    def take(i, carry):
-        at = pl.ds(pl.multiple_of(i * SLOT, SLOT), SLOT)
-        out_ref[at] = part_ref[at]
-        return carry
-
-    lax.fori_loop(0, chunks, take, 0)
-
-    def step(slot, carry):
-        reduce_slot(slot, chunks, out_ref, land_x, land_z, outgo, aside, sems)
-        return carry
-
-    lax.fori_loop(0, slots_of(chunks, lax.axis_size("dp") // 2), step, 0)
-
-
-def plane_sum(part, collective_id):
-    rows, width = part.shape
-    return pl.pallas_call(
-        reduce_kernel,
-        out_shape=jax.ShapeDtypeStruct(part.shape, part.dtype),
-        in_specs=[VM],
-        out_specs=VM,
-        scratch_shapes=reduce_scratch(width),
-        compiler_params=pltpu.CompilerParams(
-            collective_id=collective_id, has_side_effects=True, vmem_limit_bytes=60 << 20
-        ),
-        name="plane_sum",
-    )(part)
+    return (
+        [pltpu.VMEM((2, DEPTH, 8, width), jnp.float32)] * 3
+        + [pltpu.VMEM((2, DEPTH, 16, width), jnp.float32)] * 3
+        + [pltpu.VMEM((2, DEPTH, 8, width), jnp.float32), pltpu.SemaphoreType.DMA((8, 4, DEPTH))]
+    )
 
 
 BLOCKS = 8
@@ -1142,13 +1118,13 @@
 
 def tail_kernel(
     heads, key_dim, value_dim, ranges, chunks,
-    part2_hbm, ffn_hbm, wide_hbm, rest_hbm, down_hbm, pre_hbm, core_hbm, update_hbm,
+    part2_hbm, ffn_hbm, fgate_hbm, fup_hbm, down_hbm, pre_hbm, core_hbm, update_hbm, state_hbm,
     resid1_ref, upstream_ref, resid_ref, mixed_ref, hidden1_ref,
     w_out_ref, w_mix_ref, w_gate_ref, w_small_ref, norm1_ref, norm2_ref,
-    gate_ref, small_ref, taps_ref, rate_ref, gain_ref, state_ref, inverse_ref,
-    output_ref, inputs_grad_ref, wide_out, rest_out, down_out, out_out, gate_out,
+    gate_ref, small_ref, taps_ref, rate_ref, gain_ref, inverse_ref,
+    output_ref, inputs_grad_ref, fgate_out, fup_out, down_out, out_out, gate_out,
     query_out, key_out, value_out, small_out,
-    data, land_x, land_z, outgo, aside, sems,
+    data, split_x, split_z, split_out, whole_x, whole_z, whole_out, aside, sems,
     part, total, half, land_mate, land_across, sum_send, sum_recv,
     resid1_grad, resid1_low, mixed_grad, low, gate_low, small_low,
     taps_grad, gain_grad, rate_grad, norm1_grad, norm2_grad, ahead, pad, now,
@@ -1159,15 +1135,16 @@
     length, width = resid1_ref.shape
     qk = heads * key_dim
     values = heads * value_dim
-    at_wide, at_rest, at_down, at_out, at_gate, at_mix, at_small, rows_all = ranges
+    at_fgate, at_fup, at_down, at_out, at_gate, at_mix, at_small, rows_all = ranges
     loads = [
         (part2_hbm, part),
-        (wide_hbm, data.at[pl.ds(at_wide, at_rest - at_wide)]),
-        (rest_hbm, data.at[pl.ds(at_rest, at_down - at_rest)]),
+        (fgate_hbm, data.at[pl.ds(at_fgate, at_fup - at_fgate)]),
+        (fup_hbm, data.at[pl.ds(at_fup, at_down - at_fup)]),
         (down_hbm, data.at[pl.ds(at_down, at_out - at_down)]),
         (pre_hbm, data.at[pl.ds(at_mix, length)]),
         (core_hbm, data.at[pl.ds(at_mix + length, length), pl.ds(0, values)]),
         (update_hbm, data.at[pl.ds(at_mix + length, length), pl.ds(values, values)]),
+        (state_hbm, data.at[pl.ds(at_gate, state_hbm.shape[0])]),
     ]
     loads = [pltpu.make_async_copy(src, dst, load_sem.at[i]) for i, (src, dst) in enumerate(loads)]
     load_ffn = pltpu.make_async_copy(ffn_hbm, part, load_sem.at[len(loads)])
@@ -1178,7 +1155,7 @@
         data.at[pl.ds(at_mix, length)], gate_ref, small_ref, taps_ref, rate_ref, gain_ref,
         data.at[pl.ds(at_mix + length, length), pl.ds(0, values)],
         data.at[pl.ds(at_mix + length, length), pl.ds(values, values)],
-        state_ref, inverse_ref, mixed_grad, low, gate_low, small_low, taps_grad, gain_grad, rate_grad,
+        data.at[pl.ds(at_gate, state_hbm.shape[0])], inverse_ref, mixed_grad, low, gate_low, small_low, taps_grad, gain_grad, rate_grad,
         ahead, pad, now,
     )
     sums = [
@@ -1314,7 +1291,7 @@
     at = plan(at, 1, 1, lambda i: swaps[1].finish())
     assert at_ready_out <= at_out // SLOT and at_ready_gate <= at_gate // SLOT
     assert at_ready_mix <= at_mix // SLOT and at_ready_small <= at_small // SLOT
-    delay = 2 * lines + 1
+    delay = LAG * (2 * lines + 1)
     last = max(chunks + delay + 1, at)
 
     def writes(chunk, act):
@@ -1331,8 +1308,8 @@
             def _():
                 run()
 
-        segment(at_wide, at_rest, lambda: put(0, None, wide_out, at_wide))
-        segment(at_rest, at_down, lambda: put(0, None, rest_out, at_rest))
+        segment(at_fgate, at_fup, lambda: put(0, None, fgate_out, at_fgate))
+        segment(at_fup, at_down, lambda: put(0, None, fup_out, at_fup))
         segment(at_down, at_out, lambda: put(0, None, down_out, at_down))
         segment(at_out, at_gate, lambda: put(0, None, out_out, at_out))
 
@@ -1351,7 +1328,9 @@
         segment(at_small, rows_all, lambda: put(0, None, small_out, at_small))
 
     def step(slot, carry):
-        reduce_slot(slot, chunks, data, land_x, land_z, outgo, aside, sems)
+        reduce_slot(
+            slot, chunks, data, (split_x, split_z, split_out), (whole_x, whole_z, whole_out), aside, sems
+        )
         writes(slot - delay - 1, "wait")
         writes(slot - delay, "start")
         for first, count, each, run in pieces:
@@ -1374,15 +1353,15 @@
 
 
 def tail(
-    part2, ffn, wide, rest, down, pre, core, update, resid1, upstream, resid, mixed, hidden1,
-    w_out, w_mix, w_gate, w_small, norm1, norm2, gate, small, taps, rate, gain, states, inverses,
+    part2, ffn, fgate, fup, down, pre, core, update, states, resid1, upstream, resid, mixed, hidden1,
+    w_out, w_mix, w_gate, w_small, norm1, norm2, gate, small, taps, rate, gain, inverses,
     heads, key_dim, value_dim, places, collective_id,
 ):
     length, width = resid1.shape
     values = heads * value_dim
     qk = heads * key_dim
     lanes = small.shape[1]
-    heights = [wide.shape[0], rest.shape[0], down.shape[0], values, values, width, SLOT]
+    heights = [fgate.shape[0], fup.shape[0], down.shape[0], values, values, width, SLOT]
     ranges = [0]
     for height in heights:
         ranges.append(ranges[-1] + height)
@@ -1393,8 +1372,8 @@
     out_shape = [
         shape((length, width), bf),
         shape((length, width), f32),
-        shape(wide.shape, f32),
-        shape(rest.shape, f32),
+        shape(fgate.shape, f32),
+        shape(fup.shape, f32),
         shape(down.shape, f32),
         shape((values, width), f32),
         shape((width, values), f32),
@@ -1435,14 +1414,14 @@
             dma((2, places)),
             dma((2, 3, places)),
             dma((2, 3, places)),
-            dma((8,)),
+            dma((9,)),
             dma((3,)),
         ]
     )
     return pl.pallas_call(
         functools.partial(tail_kernel, heads, key_dim, value_dim, tuple(ranges[:7]) + (rows_all,), chunks),
         out_shape=out_shape,
-        in_specs=[any_] * 8 + [vmem] * 18,
+        in_specs=[any_] * 9 + [vmem] * 17,
         out_specs=[vmem] * 2 + [any_] * 9,
         scratch_shapes=scratch,
         compiler_params=pltpu.CompilerParams(
@@ -1450,9 +1429,254 @@
         ),
         name="tail",
     )(
-        part2, ffn, wide, rest, down, pre, core, update, resid1, upstream, resid, mixed, hidden1,
-        w_out, w_mix, w_gate, w_small, norm1, norm2, gate, small, taps, rate, gain, states, inverses,
-    )
+        part2, ffn, fgate, fup, down, pre, core, update, states, resid1, upstream, resid, mixed, hidden1,
+        w_out, w_mix, w_gate, w_small, norm1, norm2, gate, small, taps, rate, gain, inverses,
+    )
+
+
+def finish_kernel(count, heads, qk, values, *refs):
+    sources, rows = refs[:count], refs[count]
+    results = refs[count + 1 : 2 * count + 1]
+    norm1, norm2, head, rate, beta, decay, query, key, value = refs[2 * count + 1 : 2 * count + 10]
+    held, sems = refs[2 * count + 10 : 3 * count + 10], refs[-1]
+    loads = [pltpu.make_async_copy(sources[i], held[i], sems.at[0, i]) for i in range(count)]
+    stores = [pltpu.make_async_copy(held[i], results[i], sems.at[1, i]) for i in range(count)]
+    for load in loads:
+        load.start()
+    norm1[...] = rows[4:5]
+    norm2[...] = rows[5:6]
+    head[...] = rows[6:7, 0:values]
+    rate[...] = rows[6:7, values : values + 2 * heads][:, heads:]
+    beta[...] = rows[8 : 8 + heads]
+    decay[...] = rows[8 + heads : 8 + 2 * heads]
+    query[...] = rows[0:4, 0:qk]
+    key[...] = rows[0:4, qk : 2 * qk]
+    value[...] = rows[0:4, 2 * qk :]
+    for load, store in zip(loads, stores):
+        load.wait()
+        store.start()
+    for store in stores:
+        store.wait()
+
+
+def finish(arrays, rows, heads, qk, values):
+    count = len(arrays)
+    width = rows.shape[1]
+    any_ = pl.BlockSpec(memory_space=pl.ANY)
+    f32 = jnp.float32
+    smalls = [(1, width), (1, width), (1, values), (1, heads), (heads, width), (heads, width), (4, qk), (4, qk), (4, values)]
+    return pl.pallas_call(
+        functools.partial(finish_kernel, count, heads, qk, values),
+        out_shape=[jax.ShapeDtypeStruct(a.shape, a.dtype) for a in arrays]
+        + [jax.ShapeDtypeStruct(shape, f32) for shape in smalls],
+        in_specs=[any_] * count + [VM],
+        out_specs=[any_] * count + [VM] * len(smalls),
+        scratch_shapes=[pltpu.VMEM(a.shape, a.dtype) for a in arrays] + [pltpu.SemaphoreType.DMA((2, count))],
+        compiler_params=pltpu.CompilerParams(vmem_limit_bytes=67043328),
+        name="finish",
+    )(*arrays, rows)
+
+
+PAIR = 2
+
+
+def unit_inverses(lowers, rows, cols):
+    count = lowers[0].shape[0]
+    near = (rows // 2 == cols // 2) & (rows > cols)
+    inverses = [jnp.where(rows == cols, 1.0, jnp.where(near, -lower, 0.0)) for lower in lowers]
+    block = 2
+    while block < count:
+        cross = (rows // (2 * block) == cols // (2 * block)) & (rows // block > cols // block)
+        steps = [mm(inverse, jnp.where(cross, lower, 0.0)) for inverse, lower in zip(inverses, lowers)]
+        inverses = [inverse - mm(step, inverse) for inverse, step in zip(inverses, steps)]
+        block *= 2
+    return inverses
+
+
+def head_kernel(
+    heads, key_dim, value_dim,
+    pre_ref, gate_ref, small_ref, taps_ref, rate_ref, gain_ref, w_out_ref, resid_ref, cotangent_ref,
+    mixed_ref, core_ref, update_ref, state_ref, inverse_ref, resid1_ref, upstream_ref,
+    pad, now, solved_key, rise_query, key_tail, attend_all, ends,
+    part, land_mate, land_across, half, sum_send, sum_recv,
+    staged, arrived, swap_send, swap_recv, close_send, close_recv,
+):
+    length, width = pre_ref.shape
+    span = SPAN
+    chunks = length // span
+    rows, cols = grids(span)
+    qk = heads * key_dim
+    n, _, me, t, _, _ = grid_place()
+    _, mate, across = tensor_peers()
+    greet([(lax.rem(me + k, n), t) for k in range(1, n)] + [mate, across])
+    total = TensorSum(part, resid1_ref, land_mate, land_across, half, sum_send, sum_recv)
+    swap = Swap(staged, arrived, swap_send, swap_recv, close_send, close_recv)
+    for place in range(n):
+        mine = swap.at(place, t)
+        staged[mine] = cotangent_ref[mine].astype(jnp.float32)
+    swap.start()
+    pad[0:HALO] = jnp.zeros((HALO, width), jnp.float32)
+    now[...] = jnp.zeros_like(now)
+
+    def prepare_pair(turn, carry):
+        items = []
+        for k in range(PAIR):
+            index = turn * PAIR + k
+            here = aligned(index * span, span)
+            pad[HALO : HALO + span] = pre_ref[here, :]
+            total_pre = conv_window(pad[...], taps_ref[...], span)
+            pad[0:HALO] = pad[span : span + HALO]
+            active = total_pre * sigmoid(total_pre)
+            beta, _, _, cumul = gates_of(small_ref[here, :], rate_ref[...], heads, rows, cols)
+            beta_t = jnp.transpose(beta)
+            cumul_t = jnp.transpose(cumul)
+            for head in range(heads):
+                query = active[:, head * key_dim : (head + 1) * key_dim]
+                query = query * (lax.rsqrt(jnp.sum(query * query, -1, keepdims=True) + EPS) * key_dim ** (-0.5))
+                key = active[:, qk + head * key_dim : qk + (head + 1) * key_dim]
+                key = key * lax.rsqrt(jnp.sum(key * key, -1, keepdims=True) + EPS)
+                value = active[:, 2 * qk + head * value_dim : 2 * qk + (head + 1) * value_dim]
+                beta_col = beta[:, head : head + 1]
+                cum_col = cumul[:, heads + head : heads + head + 1]
+                cum_row = cumul_t[heads + head : heads + head + 1]
+                within = cols <= rows
+                decays = jnp.where(within, jnp.exp(jnp.where(within, cum_col - cum_row, 0.0)), 0.0)
+                scaled = decays * beta_t[head : head + 1]
+                products = mm_nt(jnp.concatenate([query, key], 0), key)
+                lower = jnp.where(cols < rows, scaled * products[span:], 0.0)
+                attend = scaled * products[:span]
+                last = cum_col[span - 1 : span]
+                rise = jnp.exp(cum_col)
+                narrow = slice(head * key_dim, (head + 1) * key_dim)
+                attend_all[index, head] = attend
+                rise_query[here, narrow] = rise * query
+                key_tail[here, narrow] = key * (jnp.exp(last - cum_col) * beta_col)
+                ends[index, head] = jnp.broadcast_to(jnp.exp(last), (8, 128))
+                items.append((index, head, here, lower, jnp.concatenate([value, rise * key], 1)))
+        inverses = unit_inverses([item[3] for item in items], rows, cols)
+        solved = [mm(inverse, item[4]) for inverse, item in zip(inverses, items)]
+        for (index, head, here, _, _), inverse, solution_ in zip(items, inverses, solved):
+            inverse_ref[index, head] = inverse
+            update_ref[here, head * value_dim : (head + 1) * value_dim] = solution_[:, :value_dim]
+            solved_key[here, head * key_dim : (head + 1) * key_dim] = solution_[:, value_dim:]
+        for k in range(PAIR):
+            swap.gather(turn * PAIR + k)
+        return carry
+
+    lax.fori_loop(0, chunks // PAIR, prepare_pair, 0)
+
+    def project_out(index):
+        here = aligned(index * span, span)
+        part[here] = dot_plain(mixed_ref[here], w_out_ref[...])
+        total.first(index).start()
+
+    def chain(index, carry):
+        @pl.when(index > 0)
+        def _():
+            project_out(index - 1)
+
+        @pl.when(index > 1)
+        def _():
+            total.cross(index - 2)
+
+        @pl.when(index > 3)
+        def _():
+            total.share(index - 4)
+
+        here = aligned(index * span, span)
+        gate = gate_ref[here, :]
+        gated = gate * sigmoid(gate) * gain_ref[...]
+        for head in range(heads):
+            narrow = slice(head * key_dim, (head + 1) * key_dim)
+            wide = slice(head * value_dim, (head + 1) * value_dim)
+            state = now[head]
+            state_ref[state_place(index, head, heads, key_dim, value_dim, width)] = state
+            both = mm(jnp.concatenate([solved_key[here, narrow], rise_query[here, narrow]], 0), state)
+            update = update_ref[here, wide] - both[:span]
+            now[head] = ends[index, head][0:1, 0:1] * state + mm_tn(key_tail[here, narrow], update)
+            core = both[span:] + mm(attend_all[index, head], update)
+            update_ref[here, wide] = update
+            core_ref[here, wide] = core
+            normed = core * lax.rsqrt(jnp.mean(core * core, -1, keepdims=True) + EPS)
+            mixed_ref[here, wide] = (normed * gated[:, wide]).astype(mixed_ref.dtype)
+        swap.forward(index)
+        return carry
+
+    lax.fori_loop(0, chunks, chain, 0)
+    project_out(chunks - 1)
+    total.cross(chunks - 2)
+    total.share(chunks - 4)
+    total.cross(chunks - 1)
+    total.share(chunks - 3)
+    total.share(chunks - 2)
+    total.share(chunks - 1)
+    swap.finish()
+
+    def turn_low(i, carry):
+        here = aligned(i * 64, 64)
+        upstream_ref[here] = arrived[here].astype(upstream_ref.dtype)
+        return carry
+
+    lax.fori_loop(0, length // 64, turn_low, 0)
+    total.finish()
+
+    def add_resid(i, carry):
+        here = aligned(i * 64, 64)
+        resid1_ref[here] = resid1_ref[here] + resid_ref[here]
+        return carry
+
+    lax.fori_loop(0, length // 64, add_resid, 0)
+
+
+def head_part(
+    pre, gate, small, taps, rate, gain, w_out, resid, cotangent, heads, key_dim, value_dim, places, collective_id
+):
+    length, width = pre.shape
+    values = heads * value_dim
+    qk = heads * key_dim
+    chunks = length // SPAN
+    f32, bf = jnp.float32, jnp.bfloat16
+    shape = jax.ShapeDtypeStruct
+    dma = pltpu.SemaphoreType.DMA
+    return pl.pallas_call(
+        functools.partial(head_kernel, heads, key_dim, value_dim),
+        out_shape=[
+            shape((length, values), bf),
+            shape((length, values), f32),
+            shape((length, values), f32),
+            shape((chunks * heads * key_dim * value_dim // width, width), f32),
+            shape((chunks, heads, SPAN, SPAN), f32),
+            shape((length, width), f32),
+            shape((length, width), bf),
+        ],
+        in_specs=[VM] * 9,
+        out_specs=[VM] * 7,
+        scratch_shapes=[
+            pltpu.VMEM((HALO + SPAN, width), f32),
+            pltpu.VMEM((heads, key_dim, value_dim), f32),
+            pltpu.VMEM((length, qk), f32),
+            pltpu.VMEM((length, qk), f32),
+            pltpu.VMEM((length, qk), f32),
+            pltpu.VMEM((chunks, heads, SPAN, SPAN), f32),
+            pltpu.VMEM((chunks, heads, 8, 128), f32),
+            pltpu.VMEM((length, width), f32),
+            pltpu.VMEM((length // 2, width), f32),
+            pltpu.VMEM((length // 2, width), f32),
+            pltpu.VMEM((length // 2, width), f32),
+            dma((3, BLOCKS)),
+            dma((3, BLOCKS)),
+            pltpu.VMEM((length, width), f32),
+            pltpu.VMEM((length, width), f32),
+            dma((places,)),
+            dma((places,)),
+            dma((3, places)),
+            dma((3, places)),
+        ],
+        compiler_params=pltpu.CompilerParams(
+            collective_id=collective_id, has_side_effects=True, vmem_limit_bytes=56 << 20
+        ),
+        name="head",
+    )(pre, gate, small, taps, rate, gain, w_out, resid, cotangent)
 
 
 def lane_pad(array, lanes):
@@ -1489,12 +1713,8 @@
     lanes = 128
     bf = jnp.bfloat16
     places = lax.axis_size("dp")
-    resid, upstream = swap(
-        [inputs.reshape(count, width), cotangent.reshape(count, width)], places, 1
-    )
-    upstream_low = upstream.astype(bf)
-    normed1, norm1_back = jax.vjp(rms_apply, resid, norm1_gain)
-    hidden1 = normed1.astype(bf)
+    resid, = swap([inputs.reshape(count, width)], places, 1)
+    hidden1 = rms_apply(resid, norm1_gain).astype(bf)
     w_mix = jnp.concatenate([w_query, w_key, w_value], axis=1)
     w_small = lane_pad(jnp.concatenate([w_beta, w_decay], axis=1), lanes)
     pre = project(hidden1, w_mix)
@@ -1503,59 +1723,54 @@
     taps = jnp.concatenate([conv_query, conv_key, conv_value], axis=1)
     rate = lane_pad(jnp.pad(decay_rate, (heads, 0))[None], lanes)
     gain = head_gain[None]
-    mixed, core, update, states, inverses = delta_forward(
-        pre, gate_pre, small, taps, rate, gain, heads, key_dim, value_dim
-    )
-    attention = tensor_sum(project(mixed, w_out), 2)
-    resid1 = resid + attention
-    normed2, norm2_back = jax.vjp(rms_apply, resid1, norm2_gain)
-    hidden2 = normed2.astype(bf)
+    mixed, core, update, states, inverses, resid1, upstream = head_part(
+        pre, gate_pre, small, taps, rate, gain, w_out, resid, cotangent.reshape(count, width),
+        heads, key_dim, value_dim, places, 2,
+    )
+    hidden2 = rms_apply(resid1, norm2_gain).astype(bf)
     ffn_gate = project(hidden2, w_ffn_gate)
     ffn_up = project(hidden2, w_ffn_up)
     inner_full, swiglu_back = jax.vjp(swiglu, ffn_gate, ffn_up)
     inner = inner_full.astype(bf)
-    grad_inner = back_project(upstream_low, w_ffn_down)
+    grad_inner = back_project(upstream, w_ffn_down)
     grad_fgate, grad_fup = swiglu_back(grad_inner)
     grad_fgate = grad_fgate.astype(bf)
     grad_fup = grad_fup.astype(bf)
-    grad_wide = jnp.concatenate([grad_fgate, grad_fup], axis=1)
-    units = inner.shape[1]
-    part2 = back_project(grad_wide, jnp.concatenate([w_ffn_gate, w_ffn_up], axis=1))
-    wide = contract_rows(hidden2, grad_wide[:, :width])
-    rest = contract_rows(grad_wide[:, width:], hidden2)
-    down = contract_rows(inner, upstream_low)
+    part2 = back_project(grad_fgate, w_ffn_gate) + back_project(grad_fup, w_ffn_up)
+    fgate = contract_rows(grad_fgate, hidden2)
+    fup = contract_rows(grad_fup, hidden2)
+    down = contract_rows(inner, upstream)
     ffn = project(inner, w_ffn_down)
+    *arrays, rows = tail(
+        part2, ffn, fgate, fup, down, pre, core, update, states, resid1, upstream, resid.astype(bf), mixed, hidden1,
+        w_out, w_mix, w_gate, w_small, norm1_gain[None], norm2_gain[None],
+        gate_pre, small, taps, rate, gain, inverses,
+        heads, key_dim, value_dim, places, 7,
+    )
     (
-        output, grad_inputs, wide, rest, grad_down, grad_out_w, grad_gate_w,
-        grad_query_w, grad_key_w, grad_value_w, rows,
-    ) = tail(
-        part2, ffn, wide, rest, down, pre, core, update, resid1, upstream_low, resid.astype(bf), mixed, hidden1,
-        w_out, w_mix, w_gate, w_small, norm1_gain[None], norm2_gain[None],
-        gate_pre, small, taps, rate, gain, states, inverses,
-        heads, key_dim, value_dim, places, 7,
-    )
-    grad_taps = rows[0:4]
-    grad_small_w = rows[8 : 8 + 2 * heads]
-    wide_full = jnp.concatenate([wide, rest.T], axis=1)
+        output, grad_inputs, fgate, fup, grad_down, grad_out_w, grad_gate_w, grad_query_w, grad_key_w, grad_value_w,
+        grad_norm1_gain, grad_norm2_gain, grad_head, grad_rate, grad_beta_w, grad_decay_w,
+        grad_convq, grad_convk, grad_convv,
+    ) = finish(arrays, rows, heads, qk_width, heads * value_dim)
     return (
         output.reshape(batch, seg, width),
         grad_inputs.reshape(batch, seg, width),
-        rows[4],
+        grad_norm1_gain[0],
         grad_query_w,
         grad_key_w,
         grad_value_w,
         grad_gate_w,
-        grad_small_w[:heads].T,
-        grad_small_w[heads:].T,
-        rows[6, heads * value_dim + heads : heads * value_dim + 2 * heads],
-        grad_taps[:, :qk_width],
-        grad_taps[:, qk_width : 2 * qk_width],
-        grad_taps[:, 2 * qk_width :],
-        rows[6, : heads * value_dim],
+        grad_beta_w.T,
+        grad_decay_w.T,
+        grad_rate[0],
+        grad_convq,
+        grad_convk,
+        grad_convv,
+        grad_head[0],
         grad_out_w,
-        rows[5],
-        wide_full[:, :units],
-        wide_full[:, units:],
+        grad_norm2_gain[0],
+        fgate.T,
+        fup.T,
         grad_down,
     )
 
@@ -1568,9 +1783,10 @@
     values = args[4].shape[1] // ranks
     units = args[15].shape[1] // ranks
     return (
-        batch == places and places == 8 and ranks == 4 and length == places * SPAN and heads <= 4
+        batch == places and places == 8 and ranks == 4 and length == places * SPAN and BLOCKS == places and heads <= 4
         and width == 2 * qk + values and width == 2 * values and width % 512 == 0 and length % 256 == 0
-        and 2 * units > width and (2 * units - width) % SLOT == 0 and units % SLOT == 0 and values % 256 == 0
+        and units % SLOT == 0 and values % 256 == 0
+        and length // SPAN * args[2].shape[1] // ranks * (values // heads) <= values * width
     )
 
 

time: 542 us -> 487 us (0.90)
  local copies, waits for them, and re-layouts: 40.7 us -> 9.5 us
  Pallas kernels: 467 us -> 450 us
    unnamed x60 -> x36, local copies, waits for them, and re-layouts: 26.5 us -> 6.43 us
    pallas_call x1, Pallas kernels: 36.4 us -> 24.3 us  [swap(): pl.pallas_call(functools.partial(swap_kernel, count, narrow), out_shape=[...]
    concatenate x1 -> x0, other arithmetic: 5.58 us -> none  [whole_sequences(): wide_full = jnp.concatenate([wide, rest.T], axis=1)]
    dot_general x7 -> x6, matrix products: 11.9 us -> 10.2 us  [project(): return jnp.dot(left, right, preferred_element_type=jnp.float32)]
where the time goes in v3:
time: 487 us
  Pallas kernels  450 us (92%)
  matrix products  21.9 us (4%)
  local copies, waits for them, and re-layouts  9.5 us (2%)
    pallas_call x1, Pallas kernels, tail(): pl.pallas_call(functools.partial(tail_kernel, heads, key_dim, value_dim,...  353 us
    pallas_call x1, Pallas kernels, head_part(): pl.pallas_call(functools.partial(head_kernel, heads, key_dim, value_dim),...  55.7 us
    pallas_call x1, Pallas kernels, swap(): pl.pallas_call(functools.partial(swap_kernel, count, narrow), out_shape=[...  24.3 us
    pallas_call x1, Pallas kernels, finish(): pl.pallas_call(functools.partial(finish_kernel, count, heads, qk, values)...  16.4 us
    dot_general x6, matrix products, project(): return jnp.dot(left, right, preferred_element_type=jnp.float32)  10.2 us

profile of v3, /device:TPU:0, one launch (start us, length us, event | category | flops | bytes accessed | tf_op | source)
XLA Modules:
  0.0 486.5 jit_solution(10287253865413187864)
XLA Ops:
  0.7 0.7 pad_bitcast_fusion
  1.4 0.5 pad.14.rate_ref
  1.9 0.7 pad_maximum_fusion
  2.6 0.7 constant_dynamic-update-slice_fusion.5
  3.3 0.7 constant_dynamic-update-slice_fusion.4
  4.0 0.7 constant_dynamic-update-slice_fusion.3.taps_ref
  4.7 0.2 copy.40
  4.9 0.8 pad.12.w_small_ref
  5.7 1.2 copy-done.1
  6.9 24.3 %swap.1.resid_ref = f32[512,1024]{1,0:T(8,128)S(1)} custom-call(bf16[512,1024]{1,0:T(8,128)(2,1)S(1)} %bitcast.40), custom_call_target="tpu_custom_call" | custom-call | tf_op jit(solution)/shard_map/swap/pallas_call | solution.py:788
  31.3 0.0 copy-start
  31.3 0.2 multiply_reduce_fusion.1
  31.5 0.0 copy-done.10
  31.5 0.0 copy-start.6
  31.5 1.4 fusion.6
  32.9 0.0 copy-done
  32.9 1.1 fusion.4.small_ref
  34.1 0.0 copy-done.6
  34.1 1.7 fusion.9.gate_ref
  35.8 0.0 copy-done.8
  35.8 0.1 constant_dynamic-update-slice_fusion.2
  35.9 0.1 constant_dynamic-update-slice_fusion.1
  35.9 0.1 constant_dynamic-update-slice_fusion.w_mix_ref
  36.1 0.0 copy-done.3
  36.1 0.0 copy-start.5
  36.1 1.3 copy-done.5
  37.4 2.6 fusion.8.pre_ref.pre_hbm
  40.0 55.7 %head.1 = (bf16[512,512]{1,0:T(8,128)(2,1)}, f32[512,512]{1,0:T(8,128)}, f32[512,512]{1,0:T(8,128)}, f32[512,1024]{1,0:T(8,128)}, f32[8,2,64,64]{3,2,1,0:T(8,128...) custom-call(f32[512,1024]{1,0:T(8,128)} %fusion.8.pre_ref.pre_hbm, f32[512,512]{1,0:T(8,128)} %fusion.9.gate_ref, ...), custom_call_target="tpu_custom_call" | custom-call | tf_op jit(solution)/shard_map/head/pallas_call | solution.py:1641
  95.8 0.0 copy-start.2
  95.8 0.0 copy-start.12
  95.8 1.9 multiply_reduce_fusion
  97.7 0.2 copy-done.2
  98.0 0.2 multiply_convert_fusion
  98.2 0.9 copy-done.14
  99.2 0.9 fusion.11
  100.1 0.3 copy-done.4
  100.4 0.5 copy-done.13
  100.8 0.9 fusion.10
  101.8 0.4 copy-done.15
  102.2 1.5 multiply_convert_fusion.2
  103.7 2.3 fusion.13.ffn_hbm
  106.0 1.0 fusion.12
  107.0 2.3 convolution_add_fusion.part2_hbm
  109.4 2.5 fusion.15.fup_hbm
  111.9 2.5 fusion.14.fgate_hbm
  114.3 2.5 fusion.16.down_hbm
  116.8 353.1 %tail.1 = (bf16[512,1024]{1,0:T(8,128)(2,1)}, f32[512,1024]{1,0:T(8,128)}, f32[704,1024]{1,0:T(8,128)}, f32[704,1024]{1,0:T(8,128)}, f32[704,1024]{1,0:T(8,128)}...) custom-call(f32[512,1024]{1,0:T(8,128)} %convolution_add_fusion.part, ...), custom_call_target="tpu_custom_call" | custom-call | tf_op jit(solution)/shard_map/tail/pallas_call | solution.py:1421
  470.0 16.4 %finish.1 = (bf16[512,1024]{1,0:T(8,128)(2,1)}, f32[512,1024]{1,0:T(8,128)}, f32[704,1024]{1,0:T(8,128)}, f32[704,1024]{1,0:T(8,128)}, f32[704,1024]{1,0:T(8,128...) custom-call(bf16[512,1024]{1,0:T(8,128)(2,1)} %get-tuple-element.63., ...), custom_call_target="tpu_custom_call" | custom-call | tf_op jit(solution)/shard_map/finish/pallas_call | solution.py:1468
  (17 shorter events, 0.0 us)
Async XLA Ops:
  4.7 26.8 %copy-start.10 = (f32[4,1024]{1,0:T(4,128)}, f32[4,1024]{1,0:T(4,128)S(1)}, u32[]{:S(2)}) copy-start(f32[4,1024]{1,0:T(4,128)S(1)} %constant_dynamic-update-slice_fusion.3.taps_ref) | copy-start | bytes 49156
  5.7 1.2 copy-start.1
  6.9 24.6 %copy-start.11 = (f32[1024]{0:T(1024)S(1)}, f32[1024]{0:T(1024)}, u32[]{:S(2)}) copy-start(f32[1024]{0:T(1024)} %param.20) | copy-start | bytes 12292
  31.3 1.7 copy-start
  31.5 2.6 copy-start.6
  32.9 3.2 copy-start.3
  34.1 1.7 copy-start.8
  34.1 1.8 copy-start.9
  34.1 1.8 copy-start.7
  36.1 1.3 copy-start.5
  95.8 2.2 copy-start.2
  95.8 2.2 copy-start.12
  97.7 1.4 copy-start.14
  99.1 1.2 copy-start.4
  99.2 1.7 copy-start.13
  100.8 1.4 copy-start.15

commit v4 on v3

--- a/solution.py
+++ b/solution.py
@@ -801,9 +801,10 @@
     return out
 
 
-SLOT = 64
-DEPTH = 12
-LAG = 1
+SLOT = 80
+DEPTH = 10
+SPLIT = 3
+WHOLE = 2
 
 
 def grid_place():
@@ -816,31 +817,12 @@
     return n, lines, me, t, z, x
 
 
-def grid_greet(extra=()):
-    n, lines, me, t, z, x = grid_place()
-    barrier = pltpu.get_barrier_semaphore()
-    pl.semaphore_signal(barrier, inc=1, device_id=(me + 1 - 2 * x, t), device_id_type=MESH)
-    for peer in extra:
-        pl.semaphore_signal(barrier, inc=1, device_id=peer, device_id_type=MESH)
-
-    @pl.when(z > 0)
-    def _():
-        pl.semaphore_signal(barrier, inc=1, device_id=(me - 2, t), device_id_type=MESH)
-
-    @pl.when(z < lines - 1)
-    def _():
-        pl.semaphore_signal(barrier, inc=1, device_id=(me + 2, t), device_id_type=MESH)
-
-    pl.semaphore_wait(
-        barrier, 1 + len(extra) + jnp.where(z > 0, 1, 0) + jnp.where(z < lines - 1, 1, 0)
-    )
-
-
-def reduce_slot(slot, chunks, data, split_rings, whole_rings, aside, sems):
+def reduce_slot(slot, chunks, data, split_rings, whole_rings, sems):
     n, lines, me, t, z, x = grid_place()
     mate = (me + 1 - 2 * x, t)
-    send_x, recv_x, send_z, recv_z, send_d, recv_d, send_p, recv_p = [sems.at[i] for i in range(8)]
+    send_x, recv_x, send_z, recv_z, send_d, recv_d, send_p, recv_p, send_s, recv_s = [sems.at[i] for i in range(10)]
     top = lines - 1
+    finish = slot - 2 * lines - 1
 
     def ring(chunk):
         return lax.rem(chunk, DEPTH)
@@ -848,81 +830,65 @@
     def within(chunk):
         return (chunk >= 0) & (chunk < chunks)
 
-    for stream in range(4):
-        split = stream < 2
+    for stream in range(SPLIT):
+        land_x, land_z, outgo, aside = split_rings
         up = stream % 2 == 0
         level = z if up else top - z
         after = (me + 2, t) if up else (me - 2, t)
         prior = (me - 2, t) if up else (me + 2, t)
-        size = 8 if split else 16
-        land_x, land_z, outgo = (split_rings if split else whole_rings)
-        lane = stream % 2
-        offset = 16 * stream
 
         def rows(chunk, side):
-            base = chunk * SLOT + offset + (side * 8 if split else 0)
-            return pl.ds(pl.multiple_of(base, 8), size)
+            return pl.ds(pl.multiple_of(chunk * SLOT + 16 * stream + 8 * side, 8), 8)
 
         def spot(ref, chunk):
-            return ref.at[lane, ring(chunk)]
-
-        def to_mate(chunk, src):
-            return remote(
-                src, spot(land_x, chunk), send_x.at[stream, ring(chunk)], recv_x.at[stream, ring(chunk)], mate
-            )
+            return ref.at[stream, ring(chunk)]
+
+        def copy(kind_send, kind_recv, chunk, src, dst, peer):
+            at = (stream, ring(chunk))
+            return remote(src, dst, kind_send.at[at], kind_recv.at[at], peer)
+
+        def to_mate(chunk):
+            return copy(send_x, recv_x, chunk, spot(aside, chunk), spot(land_x, chunk), mate)
 
         def to_after(chunk):
-            return remote(
-                spot(outgo, chunk), spot(land_z, chunk),
-                send_z.at[stream, ring(chunk)], recv_z.at[stream, ring(chunk)], after,
-            )
-
-        def to_prior(chunk):
+            return copy(send_z, recv_z, chunk, spot(outgo, chunk), spot(land_z, chunk), after)
+
+        def result(chunk, peer):
             here = data.at[rows(chunk, x)]
-            return remote(here, here, send_d.at[stream, ring(chunk)], recv_d.at[stream, ring(chunk)], prior)
-
-        def from_after(chunk):
-            here = data.at[rows(chunk, x)]
-            return remote(here, here, send_d.at[stream, ring(chunk)], recv_d.at[stream, ring(chunk)], after)
+            return copy(send_d, recv_d, chunk, here, here, peer)
 
         def close(chunk, side):
             here = data.at[rows(chunk, side)]
-            return remote(here, here, send_p.at[stream, ring(chunk)], recv_p.at[stream, ring(chunk)], mate)
+            return copy(send_p, recv_p, chunk, here, here, mate)
 
         def give_back(chunk):
             @pl.when(level > 0)
             def _():
-                to_prior(chunk).start()
-
-            if split:
-                close(chunk, x).start()
-
-        if split:
-            @pl.when(slot < chunks)
-            def _():
-                aside[stream, ring(slot)] = data[rows(slot, 1 - x)]
-                to_mate(slot, aside.at[stream, ring(slot)]).start()
-
-        rise = slot - LAG * (1 + level)
+                result(chunk, prior).start()
+
+            close(chunk, x).start()
+
+        @pl.when(slot < chunks)
+        def _():
+            aside[stream, ring(slot)] = data[rows(slot, 1 - x)]
+            to_mate(slot).start()
+
+        rise = slot - 1 - level
 
         @pl.when(within(rise))
         def _():
             here = rows(rise, x)
-            if split:
-                to_mate(rise, aside.at[stream, ring(rise)]).wait_recv()
-
-            def first():
-                own = data[here]
-                return own + land_x[lane, ring(rise)] if split else own
+            at = ring(rise)
+            to_mate(rise).wait_recv()
 
             @pl.when(level > 0)
             def _():
                 to_after(rise).wait_recv()
-                outgo[lane, ring(rise)] = first() + land_z[lane, ring(rise)]
+                outgo[stream, at] = data[here] + land_x[stream, at] + land_z[stream, at]
 
             @pl.when(level == 0)
             def _():
-                outgo[lane, ring(rise)] = first()
+                outgo[stream, at] = data[here] + land_x[stream, at]
 
             @pl.when(level < top)
             def _():
@@ -930,57 +896,163 @@
 
             @pl.when(level == top)
             def _():
-                if split:
-                    data[here] = outgo[lane, ring(rise)]
-                    give_back(rise)
-                else:
-                    to_mate(rise, spot(outgo, rise)).start()
-
-        if not split:
-            meet = slot - LAG * (2 + top)
-
-            @pl.when(within(meet) & (level == top))
-            def _():
-                to_mate(meet, spot(outgo, meet)).wait_recv()
-                data[rows(meet, x)] = outgo[lane, ring(meet)] + land_x[lane, ring(meet)]
-                give_back(meet)
-
-        extra = 0 if split else 1
-        fall = slot - LAG * (1 + extra + 2 * top - level)
+                data[here] = outgo[stream, at]
+                give_back(rise)
+
+        fall = slot - 1 - 2 * top + level
 
         @pl.when(within(fall) & (level < top))
         def _():
-            from_after(fall).wait_recv()
+            result(fall, after).wait_recv()
             to_after(fall).wait_send()
             give_back(fall)
 
-        done = fall - LAG
-
-        @pl.when(within(done))
+        @pl.when(within(finish))
         def _():
             @pl.when(level > 0)
             def _():
-                to_prior(done).wait_send()
-
-            if split:
-                close(done, x).wait_send()
-                close(done, 1 - x).wait_recv()
-                to_mate(done, aside.at[stream, ring(done)]).wait_send()
-            else:
-                @pl.when(level == top)
+                result(finish, prior).wait_send()
+
+            close(finish, x).wait_send()
+            close(finish, 1 - x).wait_recv()
+            to_mate(finish).wait_send()
+
+    for stream in range(WHOLE):
+        land_x, land_z, land_s, outgo = whole_rings
+        line = z if stream == 0 else top - z
+        step = 2 if stream == 0 else -2
+        inner, outer = (me - step, t), (me + step, t)
+
+        def rows(chunk):
+            return pl.ds(pl.multiple_of(chunk * SLOT + 16 * (SPLIT + stream), 8), 16)
+
+        def spot(ref, chunk):
+            return ref.at[stream, ring(chunk)]
+
+        def copy(kind_send, kind_recv, chunk, src, dst, peer):
+            at = (ring(chunk),)
+            return remote(
+                src, dst, kind_send.at[SPLIT + stream, ring(chunk)], kind_recv.at[SPLIT + stream, ring(chunk)], peer
+            )
+
+        def inward(chunk):
+            return copy(send_z, recv_z, chunk, spot(outgo, chunk), spot(land_z, chunk), inner)
+
+        def outward(chunk):
+            return copy(send_z, recv_s, chunk, spot(outgo, chunk), spot(land_s, chunk), outer)
+
+        def to_mate(chunk):
+            return copy(send_x, recv_x, chunk, spot(outgo, chunk), spot(land_x, chunk), mate)
+
+        def result_out(chunk):
+            here = data.at[rows(chunk)]
+            return copy(send_d, recv_d, chunk, here, here, outer)
+
+        def result_in(chunk):
+            here = data.at[rows(chunk)]
+            return copy(send_s, recv_d, chunk, here, here, inner)
+
+        rise = slot - 1 - (top - line)
+        root = lax.rem(jnp.maximum(rise, 0), 2)
+
+        @pl.when(within(rise) & (line >= root))
+        def _():
+            here = rows(rise)
+            at = ring(rise)
+
+            @pl.when(line < top)
+            def _():
+                inward(rise).wait_recv()
+
+            is_fork = (line == root) & (root > 0)
+
+            @pl.when(is_fork)
+            def _():
+                outward(rise).wait_recv()
+                outgo[stream, at] = data[here] + land_z[stream, at] + land_s[stream, at]
+
+            @pl.when((line < top) & jnp.logical_not(is_fork))
+            def _():
+                outgo[stream, at] = data[here] + land_z[stream, at]
+
+            @pl.when(line == top)
+            def _():
+                outgo[stream, at] = data[here]
+
+            @pl.when(line > root)
+            def _():
+                inward(rise).start()
+
+            @pl.when(line == root)
+            def _():
+                to_mate(rise).start()
+
+        leaf = slot - 1
+
+        @pl.when(within(leaf) & (line == 0) & (lax.rem(jnp.maximum(leaf, 0), 2) > 0))
+        def _():
+            outgo[stream, ring(leaf)] = data[rows(leaf)]
+            outward(leaf).start()
+
+        meet = slot - 2 - (top - line)
+        meet_root = lax.rem(jnp.maximum(meet, 0), 2)
+
+        @pl.when(within(meet) & (line == meet_root))
+        def _():
+            at = ring(meet)
+            to_mate(meet).wait_recv()
+            data[rows(meet)] = outgo[stream, at] + land_x[stream, at]
+            result_out(meet).start()
+
+            @pl.when(meet_root > 0)
+            def _():
+                result_in(meet).start()
+
+        for parity in range(2):
+            fall = slot - 2 - (top - parity) - (line - parity)
+
+            @pl.when(within(fall) & (lax.rem(jnp.maximum(fall, 0), 2) == parity) & (line > parity))
+            def _():
+                result_out(fall).wait_recv()
+                inward(fall).wait_send()
+
+                @pl.when(line < top)
                 def _():
-                    to_mate(done, spot(outgo, done)).wait_send()
-
-
-def slots_of(chunks, lines):
-    return chunks + LAG * (2 * lines + 1)
+                    result_out(fall).start()
+
+        inside = slot - 2 - (top - 1) - 1
+
+        @pl.when(within(inside) & (lax.rem(jnp.maximum(inside, 0), 2) > 0) & (line == 0))
+        def _():
+            result_in(inside).wait_recv()
+            outward(inside).wait_send()
+
+        end_root = lax.rem(jnp.maximum(finish, 0), 2)
+
+        @pl.when(within(finish))
+        def _():
+            @pl.when((line >= end_root) & (line < top))
+            def _():
+                result_out(finish).wait_send()
+
+            @pl.when(line == end_root)
+            def _():
+                to_mate(finish).wait_send()
+
+                @pl.when(end_root > 0)
+                def _():
+                    result_in(finish).wait_send()
+
+
+def settle(lines):
+    return 2 * lines + 1
 
 
 def reduce_scratch(width):
     return (
-        [pltpu.VMEM((2, DEPTH, 8, width), jnp.float32)] * 3
-        + [pltpu.VMEM((2, DEPTH, 16, width), jnp.float32)] * 3
-        + [pltpu.VMEM((2, DEPTH, 8, width), jnp.float32), pltpu.SemaphoreType.DMA((8, 4, DEPTH))]
+        [pltpu.VMEM((SPLIT, DEPTH, 8, width), jnp.float32)] * 4
+        + [pltpu.VMEM((WHOLE, DEPTH, 16, width), jnp.float32)] * 4
+        + [pltpu.SemaphoreType.DMA((10, SPLIT + WHOLE, DEPTH))]
     )
 
 
@@ -1107,10 +1179,12 @@
         self.close(k, 0).wait_recv()
         self.close(k, 2).start()
 
+    def sent(self):
+        for k in range(1, self.n):
+            self.out(k).wait_send()
+
     def finish(self):
         for k in range(self.n):
-            if k:
-                self.out(k).wait_send()
             self.close(k, 0).wait_send()
             self.close(k, 1).wait()
             self.close(k, 2).wait()
@@ -1118,29 +1192,26 @@
 
 def tail_kernel(
     heads, key_dim, value_dim, ranges, chunks,
-    part2_hbm, ffn_hbm, fgate_hbm, fup_hbm, down_hbm, pre_hbm, core_hbm, update_hbm, state_hbm,
-    resid1_ref, upstream_ref, resid_ref, mixed_ref, hidden1_ref,
+    part2_hbm, ffn_hbm, down_hbm, pre_hbm, core_hbm, update_hbm, state_hbm,
+    resid1_ref, upstream_ref, resid_ref, mixed_ref, hidden1_ref, hidden2_ref, units_ref,
     w_out_ref, w_mix_ref, w_gate_ref, w_small_ref, norm1_ref, norm2_ref,
     gate_ref, small_ref, taps_ref, rate_ref, gain_ref, inverse_ref,
-    output_ref, inputs_grad_ref, fgate_out, fup_out, down_out, out_out, gate_out,
-    query_out, key_out, value_out, small_out,
-    data, split_x, split_z, split_out, whole_x, whole_z, whole_out, aside, sems,
+    data, output_ref, inputs_grad_ref,
+    split_x, split_z, split_out, split_aside, whole_x, whole_z, whole_s, whole_out, sems,
     part, total, half, land_mate, land_across, sum_send, sum_recv,
     resid1_grad, resid1_low, mixed_grad, low, gate_low, small_low,
     taps_grad, gain_grad, rate_grad, norm1_grad, norm2_grad, ahead, pad, now,
-    shuffled, swap_send, swap_recv, close_send, close_recv, load_sem, out_sem,
+    shuffled, swap_send, swap_recv, close_send, close_recv, load_sem,
 ):
     n, lines, me, t, z, x = grid_place()
     _, mate, across = tensor_peers()
     length, width = resid1_ref.shape
     qk = heads * key_dim
     values = heads * value_dim
-    at_fgate, at_fup, at_down, at_out, at_gate, at_mix, at_small, rows_all = ranges
+    at_down, at_units, at_out, at_gate, at_mix, at_small, at_end, rows_all = ranges
     loads = [
         (part2_hbm, part),
-        (fgate_hbm, data.at[pl.ds(at_fgate, at_fup - at_fgate)]),
-        (fup_hbm, data.at[pl.ds(at_fup, at_down - at_fup)]),
-        (down_hbm, data.at[pl.ds(at_down, at_out - at_down)]),
+        (down_hbm, data.at[pl.ds(at_down, at_units - at_down)]),
         (pre_hbm, data.at[pl.ds(at_mix, length)]),
         (core_hbm, data.at[pl.ds(at_mix + length, length), pl.ds(0, values)]),
         (update_hbm, data.at[pl.ds(at_mix + length, length), pl.ds(values, values)]),
@@ -1168,10 +1239,19 @@
     norm1_grad[...] = jnp.zeros_like(norm1_grad)
     norm2_grad[...] = jnp.zeros_like(norm2_grad)
     backward_start(refs, SPAN)
+    data[at_end:rows_all] = jnp.zeros((rows_all - at_end, width), jnp.float32)
     loads[0].wait()
     sums[0].start()
-    for load in loads[1:]:
-        load.wait()
+    loads[1].wait()
+
+    def units_piece(i):
+        data[pl.ds(pl.multiple_of(at_units + i * 128, 64), 128)] = dot_tn(
+            units_ref[:, aligned(i * 128, 128)], hidden2_ref[...]
+        )
+
+    def wait_loads():
+        for load in loads[2:]:
+            load.wait()
 
     def norm_back(value, grad, gain, gain_grad_ref):
         scale = lax.rsqrt(jnp.mean(value * value, -1, keepdims=True) + EPS)
@@ -1234,7 +1314,7 @@
 
     def small_piece():
         base = at_small
-        data[base : rows_all] = jnp.zeros((rows_all - base, width), jnp.float32)
+        data[base : at_end] = jnp.zeros((at_end - base, width), jnp.float32)
         data[base : base + 4] = taps_grad[...]
         data[base + 4 : base + 5] = norm1_grad[...]
         data[base + 5 : base + 6] = norm2_grad[...]
@@ -1250,9 +1330,13 @@
     pieces = []
 
     def plan(first, count, each, run):
+        assert count % each == 0
         pieces.append((first, count, each, run))
         return first + -(-count // each)
 
+    plan(0, (at_out - at_units) // 128, 1, units_piece)
+    assert all(i + 1 <= (at_units + 128 * i) // SLOT for i in range((at_out - at_units) // 128))
+    plan(0, 1, 1, lambda i: wait_loads())
     at = plan(0, BLOCKS, 2, sums[0].cross)
     at = plan(at, BLOCKS, 2, sums[0].share)
     at = plan(at, 1, 1, lambda i: sums[0].finish())
@@ -1270,6 +1354,8 @@
     side = plan(side, length // 64, 4, output_piece)
     side = plan(side, 1, 1, lambda i: swaps[0].start())
     side = plan(side, n, 2, swaps[0].gather)
+    side = plan(side, 1, 1, lambda i: swaps[0].sent())
+    total_free = side
     side = plan(side, n, 2, swaps[0].forward)
     side = plan(side, 1, 1, lambda i: swaps[0].finish())
     side = plan(side, length // 64, 4, round_piece)
@@ -1278,7 +1364,7 @@
     at = plan(at, width // 256, 1, mix_piece)
     at_ready_mix = at
     at = plan(max(at, part_free), width // 256, 1, hidden_piece)
-    at = plan(max(at, side), 1, 1, lambda i: sums[2].start())
+    at = plan(max(at, total_free), 1, 1, lambda i: sums[2].start())
     at = plan(at, BLOCKS, 2, sums[2].cross)
     at = plan(at, BLOCKS, 2, sums[2].share)
     at = plan(at, 1, 1, lambda i: sums[2].finish())
@@ -1287,52 +1373,17 @@
     at_ready_small = at
     at = plan(at, 1, 1, lambda i: swaps[1].start())
     at = plan(at, n, 2, swaps[1].gather)
+    plan(at, 1, 1, lambda i: swaps[1].sent())
     at = plan(at, n, 2, swaps[1].forward)
     at = plan(at, 1, 1, lambda i: swaps[1].finish())
     assert at_ready_out <= at_out // SLOT and at_ready_gate <= at_gate // SLOT
     assert at_ready_mix <= at_mix // SLOT and at_ready_small <= at_small // SLOT
-    delay = LAG * (2 * lines + 1)
-    last = max(chunks + delay + 1, at)
-
-    def writes(chunk, act):
-        row = chunk * SLOT
-
-        def put(sem, src_cols, dst, start):
-            rows = pl.ds(pl.multiple_of(row, SLOT), SLOT)
-            src = data.at[rows] if src_cols is None else data.at[rows, pl.ds(*src_cols)]
-            copy = pltpu.make_async_copy(src, dst.at[pl.ds(pl.multiple_of(row - start, SLOT), SLOT)], out_sem.at[sem])
-            copy.start() if act == "start" else copy.wait()
-
-        def segment(low_row, high_row, run):
-            @pl.when((row >= low_row) & (row < high_row))
-            def _():
-                run()
-
-        segment(at_fgate, at_fup, lambda: put(0, None, fgate_out, at_fgate))
-        segment(at_fup, at_down, lambda: put(0, None, fup_out, at_fup))
-        segment(at_down, at_out, lambda: put(0, None, down_out, at_down))
-        segment(at_out, at_gate, lambda: put(0, None, out_out, at_out))
-
-        def gates():
-            put(0, (0, values), gate_out, at_gate)
-            put(1, (values, values), gate_out, at_gate - width // 2)
-
-        segment(at_gate, at_mix, gates)
-
-        def mixes():
-            put(0, (0, qk), query_out, at_mix)
-            put(1, (qk, qk), key_out, at_mix)
-            put(2, (2 * qk, values), value_out, at_mix)
-
-        segment(at_mix, at_small, mixes)
-        segment(at_small, rows_all, lambda: put(0, None, small_out, at_small))
+    last = max(chunks + settle(lines), at, side)
 
     def step(slot, carry):
         reduce_slot(
-            slot, chunks, data, (split_x, split_z, split_out), (whole_x, whole_z, whole_out), aside, sems
+            slot, chunks, data, (split_x, split_z, split_out, split_aside), (whole_x, whole_z, whole_s, whole_out), sems
         )
-        writes(slot - delay - 1, "wait")
-        writes(slot - delay, "start")
         for first, count, each, run in pieces:
             steps = -(-count // each)
 
@@ -1349,11 +1400,11 @@
 
         return carry
 
-    lax.fori_loop(0, last + 1, step, 0)
+    lax.fori_loop(0, last, step, 0)
 
 
 def tail(
-    part2, ffn, fgate, fup, down, pre, core, update, states, resid1, upstream, resid, mixed, hidden1,
+    part2, ffn, down, pre, core, update, states, resid1, upstream, resid, mixed, hidden1, hidden2, units,
     w_out, w_mix, w_gate, w_small, norm1, norm2, gate, small, taps, rate, gain, inverses,
     heads, key_dim, value_dim, places, collective_id,
 ):
@@ -1361,32 +1412,23 @@
     values = heads * value_dim
     qk = heads * key_dim
     lanes = small.shape[1]
-    heights = [fgate.shape[0], fup.shape[0], down.shape[0], values, values, width, SLOT]
+    heights = [down.shape[0], units.shape[1], values, values, width, 64]
     ranges = [0]
     for height in heights:
         ranges.append(ranges[-1] + height)
-    rows_all = ranges[-1]
+    rows_all = -(-ranges[-1] // SLOT) * SLOT
     chunks = rows_all // SLOT
     f32, bf = jnp.float32, jnp.bfloat16
     shape = jax.ShapeDtypeStruct
     out_shape = [
-        shape((length, width), bf),
-        shape((length, width), f32),
-        shape(fgate.shape, f32),
-        shape(fup.shape, f32),
-        shape(down.shape, f32),
-        shape((values, width), f32),
-        shape((width, values), f32),
-        shape((width, qk), f32),
-        shape((width, qk), f32),
-        shape((width, values), f32),
-        shape((SLOT, width), f32),
+        pltpu.VMEM((rows_all, width), f32),
+        pltpu.VMEM((length, width), bf),
+        pltpu.VMEM((length, width), f32),
     ]
     vmem, any_ = VM, pl.BlockSpec(memory_space=pl.ANY)
     dma = pltpu.SemaphoreType.DMA
     scratch = (
-        [pltpu.VMEM((rows_all, width), f32)]
-        + reduce_scratch(width)
+        reduce_scratch(width)
         + [
             pltpu.VMEM((length, width), f32),
             pltpu.VMEM((length, width), f32),
@@ -1415,66 +1457,86 @@
             dma((2, 3, places)),
             dma((2, 3, places)),
             dma((9,)),
-            dma((3,)),
         ]
     )
     return pl.pallas_call(
-        functools.partial(tail_kernel, heads, key_dim, value_dim, tuple(ranges[:7]) + (rows_all,), chunks),
+        functools.partial(tail_kernel, heads, key_dim, value_dim, tuple(ranges) + (rows_all,), chunks),
         out_shape=out_shape,
-        in_specs=[any_] * 9 + [vmem] * 17,
-        out_specs=[vmem] * 2 + [any_] * 9,
+        in_specs=[any_] * 7 + [vmem] * 19,
+        out_specs=[vmem] * 3,
         scratch_shapes=scratch,
         compiler_params=pltpu.CompilerParams(
-            collective_id=collective_id, has_side_effects=True, vmem_limit_bytes=67043328
+            collective_id=collective_id, has_side_effects=True,
+            vmem_limit_bytes=67043328 - 4 * width * rows_all - 6 * width * length - (1 << 18),
         ),
         name="tail",
     )(
-        part2, ffn, fgate, fup, down, pre, core, update, states, resid1, upstream, resid, mixed, hidden1,
+        part2, ffn, down, pre, core, update, states, resid1, upstream, resid, mixed, hidden1, hidden2, units,
         w_out, w_mix, w_gate, w_small, norm1, norm2, gate, small, taps, rate, gain, inverses,
-    )
-
-
-def finish_kernel(count, heads, qk, values, *refs):
-    sources, rows = refs[:count], refs[count]
-    results = refs[count + 1 : 2 * count + 1]
-    norm1, norm2, head, rate, beta, decay, query, key, value = refs[2 * count + 1 : 2 * count + 10]
-    held, sems = refs[2 * count + 10 : 3 * count + 10], refs[-1]
-    loads = [pltpu.make_async_copy(sources[i], held[i], sems.at[0, i]) for i in range(count)]
-    stores = [pltpu.make_async_copy(held[i], results[i], sems.at[1, i]) for i in range(count)]
-    for load in loads:
-        load.start()
-    norm1[...] = rows[4:5]
-    norm2[...] = rows[5:6]
-    head[...] = rows[6:7, 0:values]
-    rate[...] = rows[6:7, values : values + 2 * heads][:, heads:]
-    beta[...] = rows[8 : 8 + heads]
-    decay[...] = rows[8 + heads : 8 + 2 * heads]
-    query[...] = rows[0:4, 0:qk]
-    key[...] = rows[0:4, qk : 2 * qk]
-    value[...] = rows[0:4, 2 * qk :]
-    for load, store in zip(loads, stores):
-        load.wait()
-        store.start()
-    for store in stores:
-        store.wait()
-
-
-def finish(arrays, rows, heads, qk, values):
-    count = len(arrays)
-    width = rows.shape[1]
+    ), tuple(ranges)
+
+
+def finish_kernel(heads, qk, values, ranges, data, output, inputs_grad, *refs):
+    big, smalls, sems = refs[:10], refs[10:19], refs[19]
+    at_down, at_units, at_out, at_gate, at_mix, at_small, _ = ranges
+    width = data.shape[1]
+    units = big[2].shape[0]
+
+    def rows(start, height, left=0, wide=None):
+        return data.at[pl.ds(start, height), pl.ds(left, width if wide is None else wide)]
+
+    half = width // 2
+    moves = [
+        (output, big[0]),
+        (inputs_grad, big[1]),
+        (rows(at_units, units), big[2]),
+        (rows(at_units + units, units), big[3]),
+        (rows(at_down, units), big[4]),
+        (rows(at_out, values), big[5]),
+        (rows(at_gate, half, 0, values), big[6].at[pl.ds(0, half)]),
+        (rows(at_gate, half, values, values), big[6].at[pl.ds(half, half)]),
+        (rows(at_mix, width, 0, qk), big[7]),
+        (rows(at_mix, width, qk, qk), big[8]),
+        (rows(at_mix, width, 2 * qk, values), big[9]),
+    ]
+    moves = [pltpu.make_async_copy(src, dst, sems.at[i]) for i, (src, dst) in enumerate(moves)]
+    for move in moves:
+        move.start()
+    norm1, norm2, head, rate, beta, decay, query, key, value = smalls
+    small = data[at_small : at_small + 16]
+    norm1[...] = small[4:5]
+    norm2[...] = small[5:6]
+    head[...] = small[6:7, 0:values]
+    rate[...] = small[6:7, values : values + 2 * heads][:, heads:]
+    beta[...] = small[8 : 8 + heads]
+    decay[...] = small[8 + heads : 8 + 2 * heads]
+    query[...] = small[0:4, 0:qk]
+    key[...] = small[0:4, qk : 2 * qk]
+    value[...] = small[0:4, 2 * qk :]
+    for move in moves:
+        move.wait()
+
+
+def finish(data, output, inputs_grad, ranges, units, heads, qk, values):
+    width = data.shape[1]
+    length = output.shape[0]
     any_ = pl.BlockSpec(memory_space=pl.ANY)
     f32 = jnp.float32
+    bigs = [
+        (units, width), (units, width), (units, width), (values, width), (width, values), (width, qk), (width, qk), (width, values)
+    ]
     smalls = [(1, width), (1, width), (1, values), (1, heads), (heads, width), (heads, width), (4, qk), (4, qk), (4, values)]
+    held = [pltpu.with_memory_space_constraint(a, pltpu.VMEM) for a in (data, output, inputs_grad)]
     return pl.pallas_call(
-        functools.partial(finish_kernel, count, heads, qk, values),
-        out_shape=[jax.ShapeDtypeStruct(a.shape, a.dtype) for a in arrays]
-        + [jax.ShapeDtypeStruct(shape, f32) for shape in smalls],
-        in_specs=[any_] * count + [VM],
-        out_specs=[any_] * count + [VM] * len(smalls),
-        scratch_shapes=[pltpu.VMEM(a.shape, a.dtype) for a in arrays] + [pltpu.SemaphoreType.DMA((2, count))],
-        compiler_params=pltpu.CompilerParams(vmem_limit_bytes=67043328),
+        functools.partial(finish_kernel, heads, qk, values, ranges),
+        out_shape=[jax.ShapeDtypeStruct((length, width), output.dtype), jax.ShapeDtypeStruct((length, width), f32)]
+        + [jax.ShapeDtypeStruct(shape, f32) for shape in bigs + smalls],
+        in_specs=[VM] * 3,
+        out_specs=[any_] * 10 + [VM] * len(smalls),
+        scratch_shapes=[pltpu.SemaphoreType.DMA((11,))],
+        compiler_params=pltpu.CompilerParams(vmem_limit_bytes=8 << 20),
         name="finish",
-    )(*arrays, rows)
+    )(*held)
 
 
 PAIR = 2
@@ -1610,6 +1672,7 @@
     total.share(chunks - 3)
     total.share(chunks - 2)
     total.share(chunks - 1)
+    swap.sent()
     swap.finish()
 
     def turn_low(i, carry):
@@ -1737,12 +1800,11 @@
     grad_fgate = grad_fgate.astype(bf)
     grad_fup = grad_fup.astype(bf)
     part2 = back_project(grad_fgate, w_ffn_gate) + back_project(grad_fup, w_ffn_up)
-    fgate = contract_rows(grad_fgate, hidden2)
-    fup = contract_rows(grad_fup, hidden2)
     down = contract_rows(inner, upstream)
     ffn = project(inner, w_ffn_down)
-    *arrays, rows = tail(
-        part2, ffn, fgate, fup, down, pre, core, update, states, resid1, upstream, resid.astype(bf), mixed, hidden1,
+    held, ranges = tail(
+        part2, ffn, down, pre, core, update, states, resid1, upstream, resid.astype(bf), mixed, hidden1,
+        hidden2, jnp.concatenate([grad_fgate, grad_fup], axis=1),
         w_out, w_mix, w_gate, w_small, norm1_gain[None], norm2_gain[None],
         gate_pre, small, taps, rate, gain, inverses,
         heads, key_dim, value_dim, places, 7,
@@ -1751,7 +1813,7 @@
         output, grad_inputs, fgate, fup, grad_down, grad_out_w, grad_gate_w, grad_query_w, grad_key_w, grad_value_w,
         grad_norm1_gain, grad_norm2_gain, grad_head, grad_rate, grad_beta_w, grad_decay_w,
         grad_convq, grad_convk, grad_convv,
-    ) = finish(arrays, rows, heads, qk_width, heads * value_dim)
+    ) = finish(*held, ranges, inner.shape[1], heads, qk_width, heads * value_dim)
     return (
         output.reshape(batch, seg, width),
         grad_inputs.reshape(batch, seg, width),
@@ -1785,7 +1847,7 @@
     return (
         batch == places and places == 8 and ranks == 4 and length == places * SPAN and BLOCKS == places and heads <= 4
         and width == 2 * qk + values and width == 2 * values and width % 512 == 0 and length % 256 == 0
-        and units % SLOT == 0 and values % 256 == 0
+        and units % 64 == 0 and values % 256 == 0
         and length // SPAN * args[2].shape[1] // ranks * (values // heads) <= values * width
     )
 

time: 487 us -> 454 us (0.932)
  Pallas kernels: 450 us -> 420 us
    pallas_call x1, Pallas kernels: 353 us -> 332 us  [tail(): pl.pallas_call(functools.partial(tail_kernel, heads, key_dim, value_dim,...]
    pallas_call x1, Pallas kernels: 16.4 us -> 7.67 us  [finish(): pl.pallas_call(functools.partial(finish_kernel, heads, qk, values, ranges...]
    dot_general x3 -> x1, matrix products: 7.47 us -> 2.51 us  [contract_rows(): jnp.einsum('ra,rb->ab', left, right, preferred_element_type=jnp.float32)]
where the time goes in v4:
time: 454 us
  Pallas kernels  420 us (93%)
  matrix products  17.2 us (4%)
  local copies, waits for them, and re-layouts  9.71 us (2%)
  other arithmetic  6.02 us (1%)
    pallas_call x1, Pallas kernels, tail(): pl.pallas_call(functools.partial(tail_kernel, heads, key_dim, value_dim,...  332 us
    pallas_call x1, Pallas kernels, head_part(): pl.pallas_call(functools.partial(head_kernel, heads, key_dim, value_dim),...  55.6 us
    pallas_call x1, Pallas kernels, swap(): pl.pallas_call(functools.partial(swap_kernel, count, narrow), out_shape=[...  24.3 us
    dot_general x6, matrix products, project(): return jnp.dot(left, right, preferred_element_type=jnp.float32)  10.4 us

profile of v4, /device:TPU:0, one launch (start us, length us, event | category | flops | bytes accessed | tf_op | source)
XLA Modules:
  0.0 453.8 jit_solution(6304163227066477090)
XLA Ops:
  0.7 0.7 pad_bitcast_fusion
  1.4 0.5 pad.14.rate_ref
  1.9 0.7 pad_maximum_fusion.1
  2.6 0.7 constant_dynamic-update-slice_fusion.5
  3.3 0.7 constant_dynamic-update-slice_fusion.4
  4.0 0.7 constant_dynamic-update-slice_fusion.3.taps_ref
  4.7 0.2 copy.47
  4.9 0.8 pad.12.w_small_ref
  5.7 1.2 copy-done.1
  6.9 24.3 %swap.1.resid_ref = f32[512,1024]{1,0:T(8,128)S(1)} custom-call(bf16[512,1024]{1,0:T(8,128)(2,1)S(1)} %bitcast.36), custom_call_target="tpu_custom_call" | custom-call | tf_op jit(solution)/shard_map/swap/pallas_call | solution.py:788
  31.3 0.0 copy-start
  31.3 0.2 multiply_reduce_fusion.1
  31.5 0.0 copy-done.12
  31.5 0.0 copy-done.13
  31.5 0.0 copy-start.9
  31.5 1.4 fusion.6
  32.9 0.0 copy-done
  32.9 1.2 fusion.4.small_ref
  34.1 0.0 copy-done.9
  34.1 1.7 fusion.9.gate_ref
  35.8 0.0 copy-done.10
  35.8 0.1 constant_dynamic-update-slice_fusion.2
  35.9 0.0 copy-done.11
  35.9 0.1 constant_dynamic-update-slice_fusion.1
  35.9 0.0 copy-done.8
  35.9 0.1 constant_dynamic-update-slice_fusion.w_mix_ref
  36.1 0.0 copy-start.6
  36.1 1.3 copy-done.6
  37.4 2.6 fusion.8.pre_ref.pre_hbm
  40.0 55.6 %head.1 = (bf16[512,512]{1,0:T(8,128)(2,1)}, f32[512,512]{1,0:T(8,128)}, f32[512,512]{1,0:T(8,128)}, f32[512,1024]{1,0:T(8,128)}, f32[8,2,64,64]{3,2,1,0:T(8,128...) custom-call(f32[512,1024]{1,0:T(8,128)} %fusion.8.pre_ref.pre_hbm, f32[512,512]{1,0:T(8,128)} %fusion.9.gate_ref, ...), custom_call_target="tpu_custom_call" | custom-call | tf_op jit(solution)/shard_map/head/pallas_call | solution.py:1704
  95.6 0.0 copy-start.14
  95.6 1.9 multiply_reduce_fusion
  97.6 0.2 copy-done.2
  97.8 0.2 multiply_convert_fusion.hidden2_ref
  98.1 0.9 copy-done.15
  99.0 1.0 fusion.11
  100.0 0.6 copy-done.5
  100.6 0.5 copy-done.16
  101.1 1.0 fusion.10
  102.1 0.3 copy-done.7
  102.4 1.6 multiply_convert_fusion.2
  104.1 1.5 pad_maximum_fusion.units_ref
  105.6 1.0 fusion.12
  106.6 2.3 convolution_add_fusion.part2_hbm
  108.9 2.3 fusion.13.ffn_hbm
  111.2 2.5 fusion.14.down_hbm
  113.7 332.2 %tail.1 = (f32[4240,1024]{1,0:T(8,128)S(1)}, bf16[512,1024]{1,0:T(8,128)(2,1)S(1)}, f32[512,1024]{1,0:T(8,128)S(1)}) custom-call(f32[512,1024]{1,0:T(8,128)} %convolution_add_fusion.part2_hbm, f32[512,1024]{1,0:T(8,128)} %fusion.13.ffn_hbm, f32[704,1024]{1,0:T(8,128)} %fusion.14.down_hbm, f32[512,1024]{1,0:T(8,128)} %fusion.8.pre_ref.pre_hbm, ...), custom_call_target="tpu_custom_call" | custom-call | tf_op jit(solution)/shard_map/tail/pallas_call | solution.py:1462
  445.9 7.7 %finish.1 = (bf16[512,1024]{1,0:T(8,128)(2,1)}, f32[512,1024]{1,0:T(8,128)}, f32[704,1024]{1,0:T(8,128)}, f32[704,1024]{1,0:T(8,128)}, f32[704,1024]{1,0:T(8,128...) custom-call(f32[4240,1024]{1,0:T(8,128)S(1)} %get-tuple-element.55.d, ...), custom_call_target="tpu_custom_call" | custom-call | tf_op jit(solution)/shard_map/finish/pallas_call | solution.py:1530
  (18 shorter events, 0.0 us)
Async XLA Ops:
  4.7 26.8 %copy-start.12 = (f32[4,1024]{1,0:T(4,128)}, f32[4,1024]{1,0:T(4,128)S(1)}, u32[]{:S(2)}) copy-start(f32[4,1024]{1,0:T(4,128)S(1)} %constant_dynamic-update-slice_fusion.3.taps_ref) | copy-start | bytes 49156
  5.7 1.2 copy-start.1
  6.9 24.6 %copy-start.13 = (f32[1024]{0:T(1024)S(1)}, f32[1024]{0:T(1024)}, u32[]{:S(2)}) copy-start(f32[1024]{0:T(1024)} %param.20) | copy-start | bytes 12292
  31.3 1.7 copy-start
  31.5 2.6 copy-start.9
  32.9 3.2 copy-start.3
  34.1 1.7 copy-start.10
  34.1 1.8 copy-start.11
  34.1 1.8 copy-start.8
  36.1 1.3 copy-start.6
  95.6 2.2 copy-start.2
  95.6 2.2 copy-start.14
  97.6 1.4 copy-start.15
  99.0 3.1 copy-start.4
  99.0 1.6 copy-start.5
  99.0 2.1 copy-start.16
  101.1 1.4 copy-start.7

commit v5 on v4

--- a/solution.py
+++ b/solution.py
@@ -643,11 +643,19 @@
 VM = pl.BlockSpec(memory_space=pltpu.VMEM)
 
 
-def greet(peers):
+def call_out(peers):
     barrier = pltpu.get_barrier_semaphore()
     for peer in peers:
         pl.semaphore_signal(barrier, inc=1, device_id=peer, device_id_type=MESH)
-    pl.semaphore_wait(barrier, len(peers))
+
+
+def hear_all(peers):
+    pl.semaphore_wait(pltpu.get_barrier_semaphore(), len(peers))
+
+
+def greet(peers):
+    call_out(peers)
+    hear_all(peers)
 
 
 def remote(src, dst, send, recv, peer):
@@ -1116,10 +1124,12 @@
         self.half[slot] = self.part[self.span(block, self.core)] + self.land_mate[slot]
         self.second(block).start()
 
-    def share(self, block):
+    def share(self, block, beside=None):
         self.second(block).wait_recv()
         slot = self.slot(block)
-        self.total[self.span(block, self.core)] = self.half[slot] + self.land_across[slot]
+        mine = self.span(block, self.core)
+        value = self.half[slot] + self.land_across[slot]
+        self.total[mine] = value if beside is None else value + beside[mine].astype(value.dtype)
         self.third(block).start()
 
     def finish(self):
@@ -1190,13 +1200,51 @@
             self.close(k, 2).wait()
 
 
+class PlaneSwap(Swap):
+    def __init__(self, source, result, send, recv, close_send, close_recv):
+        super().__init__(source, result, send, recv, close_send, close_recv)
+        self.core = lax.rem(self.t, 2)
+        self.part = self.seg // 2
+
+    def out(self, k):
+        other = lax.rem(self.me + k, self.n)
+        return remote(
+            self.source.at[self.at(other, self.core)], self.result.at[self.at(self.me, self.core)],
+            self.sems[0].at[k], self.sems[1].at[k], (other, self.t),
+        )
+
+    def close(self, k, leg):
+        origin = lax.rem(self.me + self.n - k, self.n)
+        here = self.result.at[self.at(origin, self.core)]
+        return remote(here, here, self.sems[2].at[leg, k], self.sems[3].at[leg, k], self.mate)
+
+    def start(self):
+        mine = self.at(self.me, self.core)
+        self.result[mine] = self.source[mine]
+        for k in range(1, self.n):
+            self.out(k).start()
+
+    def gather(self, k):
+        @pl.when(k > 0)
+        def _():
+            self.out(k).wait_recv()
+
+        self.close(k, 1).start()
+
+    def finish(self):
+        for k in range(self.n):
+            self.close(k, 1).wait()
+
+
 def tail_kernel(
     heads, key_dim, value_dim, ranges, chunks,
-    part2_hbm, ffn_hbm, down_hbm, pre_hbm, core_hbm, update_hbm, state_hbm,
+    part2_hbm, ffn_hbm, pre_hbm, core_hbm, update_hbm, state_hbm,
+    resid1_hbm, upstream_hbm, resid_hbm, mixed_hbm, hidden1_hbm, hidden2_hbm, units_hbm,
+    w_out_hbm, query_hbm, key_hbm, value_hbm, w_gate_hbm, w_small_hbm, gate_hbm, small_hbm, inverse_hbm,
+    norm1_ref, norm2_ref, taps_ref, rate_ref, gain_ref,
+    data, output_ref, inputs_grad_ref,
     resid1_ref, upstream_ref, resid_ref, mixed_ref, hidden1_ref, hidden2_ref, units_ref,
-    w_out_ref, w_mix_ref, w_gate_ref, w_small_ref, norm1_ref, norm2_ref,
-    gate_ref, small_ref, taps_ref, rate_ref, gain_ref, inverse_ref,
-    data, output_ref, inputs_grad_ref,
+    w_out_ref, w_mix_ref, w_gate_ref, w_small_ref, gate_ref, small_ref, inverse_ref,
     split_x, split_z, split_out, split_aside, whole_x, whole_z, whole_s, whole_out, sems,
     part, total, half, land_mate, land_across, sum_send, sum_recv,
     resid1_grad, resid1_low, mixed_grad, low, gate_low, small_low,
@@ -1205,23 +1253,39 @@
 ):
     n, lines, me, t, z, x = grid_place()
     _, mate, across = tensor_peers()
-    length, width = resid1_ref.shape
+    length, width = resid1_hbm.shape
     qk = heads * key_dim
     values = heads * value_dim
     at_down, at_units, at_out, at_gate, at_mix, at_small, at_end, rows_all = ranges
     loads = [
         (part2_hbm, part),
-        (down_hbm, data.at[pl.ds(at_down, at_units - at_down)]),
+        (units_hbm, units_ref),
+        (upstream_hbm, upstream_ref),
+        (hidden2_hbm, hidden2_ref),
+        (resid1_hbm, resid1_ref),
+        (w_out_hbm, w_out_ref),
+        (mixed_hbm, mixed_ref),
         (pre_hbm, data.at[pl.ds(at_mix, length)]),
         (core_hbm, data.at[pl.ds(at_mix + length, length), pl.ds(0, values)]),
         (update_hbm, data.at[pl.ds(at_mix + length, length), pl.ds(values, values)]),
         (state_hbm, data.at[pl.ds(at_gate, state_hbm.shape[0])]),
+        (gate_hbm, gate_ref),
+        (small_hbm, small_ref),
+        (inverse_hbm, inverse_ref),
+        (hidden1_hbm, hidden1_ref),
+        (query_hbm, w_mix_ref.at[:, pl.ds(0, qk)]),
+        (key_hbm, w_mix_ref.at[:, pl.ds(qk, qk)]),
+        (value_hbm, w_mix_ref.at[:, pl.ds(2 * qk, values)]),
+        (w_gate_hbm, w_gate_ref),
+        (w_small_hbm, w_small_ref),
+        (resid_hbm, resid_ref),
     ]
     loads = [pltpu.make_async_copy(src, dst, load_sem.at[i]) for i, (src, dst) in enumerate(loads)]
     load_ffn = pltpu.make_async_copy(ffn_hbm, part, load_sem.at[len(loads)])
+    peers = [(lax.rem(me + k, n), t) for k in range(1, n)] + [mate, across]
+    call_out(peers)
     for load in loads:
         load.start()
-    greet([(lax.rem(me + k, n), t) for k in range(1, n)] + [mate, across])
     refs = (
         data.at[pl.ds(at_mix, length)], gate_ref, small_ref, taps_ref, rate_ref, gain_ref,
         data.at[pl.ds(at_mix + length, length), pl.ds(0, values)],
@@ -1240,17 +1304,44 @@
     norm2_grad[...] = jnp.zeros_like(norm2_grad)
     backward_start(refs, SPAN)
     data[at_end:rows_all] = jnp.zeros((rows_all - at_end, width), jnp.float32)
+    count_units = (at_units - at_down)
+    tiles = units_ref.shape[2] // 128
+
+    def units_piece(i):
+        kind = lax.div(i, tiles)
+        tile = lax.rem(i, tiles)
+        left = units_ref[kind, :, aligned(tile * 128, 128)]
+        start = at_down + kind * count_units + tile * 128
+
+        def put(right):
+            value = dot_tn(left, right)
+
+            @pl.when(tile < tiles - 1)
+            def _():
+                data[pl.ds(pl.multiple_of(start, 64), 128)] = value
+
+            @pl.when(tile == tiles - 1)
+            def _():
+                rest = count_units - (tiles - 1) * 128
+                data[pl.ds(pl.multiple_of(start, 64), rest)] = value[0:rest]
+
+        @pl.when(kind == 0)
+        def _():
+            put(upstream_ref[...])
+
+        @pl.when(kind > 0)
+        def _():
+            put(hidden2_ref[...])
+
     loads[0].wait()
+    hear_all(peers)
     sums[0].start()
     loads[1].wait()
-
-    def units_piece(i):
-        data[pl.ds(pl.multiple_of(at_units + i * 128, 64), 128)] = dot_tn(
-            units_ref[:, aligned(i * 128, 128)], hidden2_ref[...]
-        )
+    loads[2].wait()
+    units_piece(0)
 
     def wait_loads():
-        for load in loads[2:]:
+        for load in loads[3:]:
             load.wait()
 
     def norm_back(value, grad, gain, gain_grad_ref):
@@ -1295,7 +1386,7 @@
         tile = aligned(i * 256, 256)
         part[:, tile] = (
             dot_nt(low[...], w_mix_ref[tile]) + dot_nt(gate_low[...], w_gate_ref[tile])
-            + dot_nt(small_low[...], w_small_ref[tile])
+            + dot_plain(small_low[...], w_small_ref[:, tile])
         )
 
     def output_piece(i):
@@ -1334,9 +1425,10 @@
         pieces.append((first, count, each, run))
         return first + -(-count // each)
 
-    plan(0, (at_out - at_units) // 128, 1, units_piece)
-    assert all(i + 1 <= (at_units + 128 * i) // SLOT for i in range((at_out - at_units) // 128))
     plan(0, 1, 1, lambda i: wait_loads())
+    plan(0, 3 * tiles - 1, 1, lambda i: units_piece(i + 1))
+    for i in range(1, 3 * tiles):
+        assert i <= (at_down + i // tiles * count_units + i % tiles * 128) // SLOT
     at = plan(0, BLOCKS, 2, sums[0].cross)
     at = plan(at, BLOCKS, 2, sums[0].share)
     at = plan(at, 1, 1, lambda i: sums[0].finish())
@@ -1404,15 +1496,15 @@
 
 
 def tail(
-    part2, ffn, down, pre, core, update, states, resid1, upstream, resid, mixed, hidden1, hidden2, units,
-    w_out, w_mix, w_gate, w_small, norm1, norm2, gate, small, taps, rate, gain, inverses,
-    heads, key_dim, value_dim, places, collective_id,
+    part2, ffn, pre, core, update, states, resid1, upstream, resid, mixed, hidden1, hidden2, units,
+    w_out, w_query, w_key, w_value, w_gate, w_small, gate, small, inverses, norm1, norm2, taps, rate, gain,
+    heads, key_dim, value_dim, count_units, places, collective_id,
 ):
     length, width = resid1.shape
     values = heads * value_dim
     qk = heads * key_dim
     lanes = small.shape[1]
-    heights = [down.shape[0], units.shape[1], values, values, width, 64]
+    heights = [count_units, 2 * count_units, values, values, width, 64]
     ranges = [0]
     for height in heights:
         ranges.append(ranges[-1] + height)
@@ -1428,7 +1520,14 @@
     vmem, any_ = VM, pl.BlockSpec(memory_space=pl.ANY)
     dma = pltpu.SemaphoreType.DMA
     scratch = (
-        reduce_scratch(width)
+        [
+            pltpu.VMEM(a.shape, a.dtype)
+            for a in (
+                resid1, upstream, resid, mixed, hidden1, hidden2, units, w_out, shape((width, width), bf), w_gate, w_small,
+                gate, small, inverses,
+            )
+        ]
+        + reduce_scratch(width)
         + [
             pltpu.VMEM((length, width), f32),
             pltpu.VMEM((length, width), f32),
@@ -1456,13 +1555,13 @@
             dma((2, places)),
             dma((2, 3, places)),
             dma((2, 3, places)),
-            dma((9,)),
+            dma((24,)),
         ]
     )
     return pl.pallas_call(
         functools.partial(tail_kernel, heads, key_dim, value_dim, tuple(ranges) + (rows_all,), chunks),
         out_shape=out_shape,
-        in_specs=[any_] * 7 + [vmem] * 19,
+        in_specs=[any_] * 22 + [vmem] * 5,
         out_specs=[vmem] * 3,
         scratch_shapes=scratch,
         compiler_params=pltpu.CompilerParams(
@@ -1471,8 +1570,8 @@
         ),
         name="tail",
     )(
-        part2, ffn, down, pre, core, update, states, resid1, upstream, resid, mixed, hidden1, hidden2, units,
-        w_out, w_mix, w_gate, w_small, norm1, norm2, gate, small, taps, rate, gain, inverses,
+        part2, ffn, pre, core, update, states, resid1, upstream, resid, mixed, hidden1, hidden2, units,
+        w_out, w_query, w_key, w_value, w_gate, w_small, gate, small, inverses, norm1, norm2, taps, rate, gain,
     ), tuple(ranges)
 
 
@@ -1570,17 +1669,14 @@
     qk = heads * key_dim
     n, _, me, t, _, _ = grid_place()
     _, mate, across = tensor_peers()
-    greet([(lax.rem(me + k, n), t) for k in range(1, n)] + [mate, across])
+    peers = [(lax.rem(me + k, n), t) for k in range(1, n)] + [mate, across]
+    call_out(peers)
     total = TensorSum(part, resid1_ref, land_mate, land_across, half, sum_send, sum_recv)
-    swap = Swap(staged, arrived, swap_send, swap_recv, close_send, close_recv)
-    for place in range(n):
-        mine = swap.at(place, t)
-        staged[mine] = cotangent_ref[mine].astype(jnp.float32)
-    swap.start()
+    swap = PlaneSwap(staged, arrived, swap_send, swap_recv, close_send, close_recv)
     pad[0:HALO] = jnp.zeros((HALO, width), jnp.float32)
     now[...] = jnp.zeros_like(now)
 
-    def prepare_pair(turn, carry):
+    def prepare_pair(turn):
         items = []
         for k in range(PAIR):
             index = turn * PAIR + k
@@ -1621,30 +1717,8 @@
             inverse_ref[index, head] = inverse
             update_ref[here, head * value_dim : (head + 1) * value_dim] = solution_[:, :value_dim]
             solved_key[here, head * key_dim : (head + 1) * key_dim] = solution_[:, value_dim:]
-        for k in range(PAIR):
-            swap.gather(turn * PAIR + k)
-        return carry
-
-    lax.fori_loop(0, chunks // PAIR, prepare_pair, 0)
-
-    def project_out(index):
-        here = aligned(index * span, span)
-        part[here] = dot_plain(mixed_ref[here], w_out_ref[...])
-        total.first(index).start()
-
-    def chain(index, carry):
-        @pl.when(index > 0)
-        def _():
-            project_out(index - 1)
-
-        @pl.when(index > 1)
-        def _():
-            total.cross(index - 2)
-
-        @pl.when(index > 3)
-        def _():
-            total.share(index - 4)
-
+
+    def chain(index):
         here = aligned(index * span, span)
         gate = gate_ref[here, :]
         gated = gate * sigmoid(gate) * gain_ref[...]
@@ -1661,17 +1735,59 @@
             core_ref[here, wide] = core
             normed = core * lax.rsqrt(jnp.mean(core * core, -1, keepdims=True) + EPS)
             mixed_ref[here, wide] = (normed * gated[:, wide]).astype(mixed_ref.dtype)
-        swap.forward(index)
+
+    def chain_pair(turn):
+        for k in range(PAIR):
+            chain(turn * PAIR + k)
+
+    def send_pair(turn):
+        here = aligned(turn * PAIR * span, PAIR * span)
+        part[here] = dot_plain(mixed_ref[here], w_out_ref[...])
+        for k in range(PAIR):
+            total.first(turn * PAIR + k).start()
+
+    def cross_pair(turn):
+        for k in range(PAIR):
+            total.cross(turn * PAIR + k)
+
+    def share_pair(turn):
+        for k in range(PAIR):
+            total.share(turn * PAIR + k, resid_ref)
+
+    pairs = chunks // PAIR
+    for place in range(n):
+        mine = swap.at(place, swap.core)
+        staged[mine] = cotangent_ref[mine].astype(jnp.float32)
+    prepare_pair(0)
+    hear_all(peers)
+    swap.start()
+
+    def step(turn, carry):
+        chain_pair(turn - 1)
+        prepare_pair(turn)
+        send_pair(turn - 1)
+
+        cross_pair(turn - 1)
+
+        @pl.when(turn > 1)
+        def _():
+            share_pair(turn - 2)
+
         return carry
 
-    lax.fori_loop(0, chunks, chain, 0)
-    project_out(chunks - 1)
-    total.cross(chunks - 2)
-    total.share(chunks - 4)
-    total.cross(chunks - 1)
-    total.share(chunks - 3)
-    total.share(chunks - 2)
-    total.share(chunks - 1)
+    lax.fori_loop(1, pairs, step, 0)
+    chain_pair(pairs - 1)
+    send_pair(pairs - 1)
+    cross_pair(pairs - 1)
+    share_pair(pairs - 2)
+
+    def gather(k, carry):
+        swap.gather(k)
+        return carry
+
+    lax.fori_loop(0, n, gather, 0)
+
+    share_pair(pairs - 1)
     swap.sent()
     swap.finish()
 
@@ -1682,13 +1798,6 @@
 
     lax.fori_loop(0, length // 64, turn_low, 0)
     total.finish()
-
-    def add_resid(i, carry):
-        here = aligned(i * 64, 64)
-        resid1_ref[here] = resid1_ref[here] + resid_ref[here]
-        return carry
-
-    lax.fori_loop(0, length // 64, add_resid, 0)
 
 
 def head_part(
@@ -1736,14 +1845,214 @@
             dma((3, places)),
         ],
         compiler_params=pltpu.CompilerParams(
-            collective_id=collective_id, has_side_effects=True, vmem_limit_bytes=56 << 20
+            collective_id=collective_id, has_side_effects=True, vmem_limit_bytes=67043328
         ),
         name="head",
     )(pre, gate, small, taps, rate, gain, w_out, resid, cotangent)
 
 
-def lane_pad(array, lanes):
-    return jnp.pad(array, ((0, 0), (0, lanes - array.shape[1])))
+def prep_kernel(
+    heads,
+    x_ref, norm1_ref, query_hbm, key_hbm, value_hbm, gate_hbm, beta_ref, decay_ref, rate_ref, taps_q, taps_k, taps_v,
+    low_ref, hidden_ref, pre_ref, gate_pre_ref, small_ref, w_small_ref, taps_ref, rate_row_ref,
+    w_mix, w_gate, rows16, staged, arrived, send, recv, close_send, close_recv, load_sem,
+):
+    length, width = x_ref.shape
+    qk = query_hbm.shape[1]
+    values = value_hbm.shape[1]
+    n, _, me, t, _, _ = grid_place()
+    _, mate, across = tensor_peers()
+    peers = [(lax.rem(me + k, n), t) for k in range(1, n)] + [mate, across]
+    call_out(peers)
+    loads = [
+        (query_hbm, w_mix.at[:, pl.ds(0, qk)]),
+        (key_hbm, w_mix.at[:, pl.ds(qk, qk)]),
+        (value_hbm, w_mix.at[:, pl.ds(2 * qk, values)]),
+        (gate_hbm, w_gate),
+    ]
+    loads = [pltpu.make_async_copy(src, dst, load_sem.at[i]) for i, (src, dst) in enumerate(loads)]
+    for load in loads:
+        load.start()
+    swap = Swap(staged, arrived, send, recv, close_send, close_recv)
+    for place in range(n):
+        mine = swap.at(place, t)
+        staged[mine] = x_ref[mine].astype(jnp.float32)
+    hear_all(peers)
+    swap.start()
+    taps_ref[:, 0:qk] = taps_q[...]
+    taps_ref[:, qk : 2 * qk] = taps_k[...]
+    taps_ref[:, 2 * qk :] = taps_v[...]
+    lanes = rate_row_ref.shape[1]
+    lane = lax.broadcasted_iota(jnp.int32, (1, lanes), 1)
+    row = jnp.zeros((1, lanes), jnp.float32)
+    for head in range(heads):
+        row = jnp.where(lane == heads + head, rate_ref[:, head : head + 1], row)
+    rate_row_ref[...] = row
+    rows16[...] = jnp.zeros_like(rows16)
+    rows16[0:heads] = beta_ref[...].astype(jnp.float32)
+    rows16[heads : 2 * heads] = decay_ref[...].astype(jnp.float32)
+    w_small_ref[...] = jnp.zeros_like(w_small_ref)
+    w_small_ref[0:16] = rows16[...].astype(w_small_ref.dtype)
+
+    def gather(k, carry):
+        swap.gather(k)
+        return carry
+
+    def forward(k, carry):
+        swap.forward(k)
+        return carry
+
+    lax.fori_loop(0, n, gather, 0)
+    lax.fori_loop(0, n, forward, 0)
+    for load in loads:
+        load.wait()
+    swap.sent()
+    swap.finish()
+
+    def norm(i, carry):
+        here = aligned(i * 64, 64)
+        value = arrived[here]
+        low_ref[here] = value.astype(low_ref.dtype)
+        scale = lax.rsqrt(jnp.mean(value * value, -1, keepdims=True) + EPS)
+        hidden_ref[here] = (value * scale * norm1_ref[...]).astype(hidden_ref.dtype)
+        return carry
+
+    lax.fori_loop(0, length // 64, norm, 0)
+
+    def mix_tile(i, carry):
+        tile = aligned(i * 256, 256)
+        pre_ref[:, tile] = dot_plain(hidden_ref[...], w_mix[:, tile])
+        return carry
+
+    def gate_tile(i, carry):
+        tile = aligned(i * 256, 256)
+        gate_pre_ref[:, tile] = dot_plain(hidden_ref[...], w_gate[:, tile])
+        return carry
+
+    lax.fori_loop(0, width // 256, mix_tile, 0)
+    lax.fori_loop(0, values // 256, gate_tile, 0)
+    small_ref[...] = dot_nt(hidden_ref[...], w_small_ref[...])
+
+
+def prep(x, norm1, w_query, w_key, w_value, w_gate, w_beta_t, w_decay_t, rate, taps_q, taps_k, taps_v, places, collective_id):
+    length, width = x.shape
+    heads = rate.shape[1]
+    values = w_value.shape[1]
+    lanes = 128
+    f32, bf = jnp.float32, jnp.bfloat16
+    shape = jax.ShapeDtypeStruct
+    dma = pltpu.SemaphoreType.DMA
+    any_ = pl.BlockSpec(memory_space=pl.ANY)
+    return pl.pallas_call(
+        functools.partial(prep_kernel, heads),
+        out_shape=[
+            shape((length, width), bf),
+            shape((length, width), bf),
+            shape((length, width), f32),
+            shape((length, values), f32),
+            shape((length, lanes), f32),
+            shape((lanes, width), bf),
+            shape((taps_q.shape[0], width), f32),
+            shape((1, lanes), f32),
+        ],
+        in_specs=[VM] * 2 + [any_] * 4 + [VM] * 6,
+        out_specs=[VM] * 8,
+        scratch_shapes=[
+            pltpu.VMEM((width, width), bf),
+            pltpu.VMEM((width, values), bf),
+            pltpu.VMEM((16, width), f32),
+            pltpu.VMEM((length, width), f32),
+            pltpu.VMEM((length, width), f32),
+            dma((places,)),
+            dma((places,)),
+            dma((3, places)),
+            dma((3, places)),
+            dma((4,)),
+        ],
+        compiler_params=pltpu.CompilerParams(
+            collective_id=collective_id, has_side_effects=True, vmem_limit_bytes=67043328
+        ),
+        name="prep",
+    )(x, norm1, w_query, w_key, w_value, w_gate, w_beta_t, w_decay_t, rate, taps_q, taps_k, taps_v)
+
+
+def feed_kernel(
+    resid1_ref, norm2_ref, upstream_hbm, gate_hbm, up_hbm, down_hbm,
+    hidden_ref, units_ref, part2_ref, ffn_ref,
+    upstream, w_gate, w_up, w_down, gate_pre, up_pre, inner_grad, load_sem,
+):
+    length, width = resid1_ref.shape
+    units = w_gate.shape[0]
+    loads = [(gate_hbm, w_gate), (up_hbm, w_up), (upstream_hbm, upstream), (down_hbm, w_down)]
+    loads = [pltpu.make_async_copy(src, dst, load_sem.at[i]) for i, (src, dst) in enumerate(loads)]
+    for load in loads:
+        load.start()
+
+    def norm(i, carry):
+        here = aligned(i * 64, 64)
+        value = resid1_ref[here]
+        scale = lax.rsqrt(jnp.mean(value * value, -1, keepdims=True) + EPS)
+        hidden_ref[here] = (value * scale * norm2_ref[...]).astype(hidden_ref.dtype)
+        return carry
+
+    lax.fori_loop(0, length // 64, norm, 0)
+    loads[0].wait()
+    gate_pre[...] = dot_nt(hidden_ref[...], w_gate[...])
+    loads[1].wait()
+    up_pre[...] = dot_nt(hidden_ref[...], w_up[...])
+    loads[2].wait()
+    loads[3].wait()
+    inner_grad[...] = dot_nt(upstream[...], w_down[...])
+    units_ref[:, :, units // 128 * 128 :] = jnp.zeros((3, length, units_ref.shape[2] - units // 128 * 128), units_ref.dtype)
+
+    def bend(i, carry):
+        here = aligned(i * 64, 64)
+        gate = gate_pre[here]
+        upper = up_pre[here]
+        grad = inner_grad[here]
+        sig = sigmoid(gate)
+        silu = gate * sig
+        low = units_ref.dtype
+        units_ref[0, here, 0:units] = (silu * upper).astype(low)
+        units_ref[1, here, 0:units] = (grad * upper * (sig * (1.0 + gate * (1.0 - sig)))).astype(low)
+        units_ref[2, here, 0:units] = (grad * silu).astype(low)
+        return carry
+
+    lax.fori_loop(0, length // 64, bend, 0)
+    part2_ref[...] = dot_plain(units_ref[1, :, 0:units], w_gate[...]) + dot_plain(units_ref[2, :, 0:units], w_up[...])
+    ffn_ref[...] = dot_plain(units_ref[0, :, 0:units], w_down[...])
+
+
+def feed(resid1, norm2, upstream, w_gate_t, w_up_t, w_down):
+    length, width = resid1.shape
+    units = w_down.shape[0]
+    padded = -(-units // 128) * 128
+    f32, bf = jnp.float32, jnp.bfloat16
+    shape = jax.ShapeDtypeStruct
+    any_ = pl.BlockSpec(memory_space=pl.ANY)
+    return pl.pallas_call(
+        feed_kernel,
+        out_shape=[
+            shape((length, width), bf),
+            shape((3, length, padded), bf),
+            shape((length, width), f32),
+            shape((length, width), f32),
+        ],
+        in_specs=[VM] * 2 + [any_] * 4,
+        out_specs=[VM] * 4,
+        scratch_shapes=[
+            pltpu.VMEM((length, width), bf),
+            pltpu.VMEM((units, width), bf),
+            pltpu.VMEM((units, width), bf),
+            pltpu.VMEM((units, width), bf),
+            pltpu.VMEM((length, units), f32),
+            pltpu.VMEM((length, units), f32),
+            pltpu.VMEM((length, units), f32),
+            pltpu.SemaphoreType.DMA((4,)),
+        ],
+        compiler_params=pltpu.CompilerParams(vmem_limit_bytes=67043328),
+        name="feed",
+    )(resid1, norm2, upstream, w_gate_t, w_up_t, w_down)
 
 
 def whole_sequences(
@@ -1773,47 +2082,30 @@
     key_dim = w_query.shape[1] // heads
     value_dim = w_value.shape[1] // heads
     qk_width = heads * key_dim
-    lanes = 128
-    bf = jnp.bfloat16
     places = lax.axis_size("dp")
-    resid, = swap([inputs.reshape(count, width)], places, 1)
-    hidden1 = rms_apply(resid, norm1_gain).astype(bf)
-    w_mix = jnp.concatenate([w_query, w_key, w_value], axis=1)
-    w_small = lane_pad(jnp.concatenate([w_beta, w_decay], axis=1), lanes)
-    pre = project(hidden1, w_mix)
-    gate_pre = project(hidden1, w_gate)
-    small = project(hidden1, w_small)
-    taps = jnp.concatenate([conv_query, conv_key, conv_value], axis=1)
-    rate = lane_pad(jnp.pad(decay_rate, (heads, 0))[None], lanes)
+    resid, hidden1, pre, gate_pre, small, w_small, taps, rate = prep(
+        inputs.reshape(count, width), norm1_gain[None], w_query, w_key, w_value, w_gate, w_beta.T, w_decay.T,
+        decay_rate[None], conv_query, conv_key, conv_value, places, 1,
+    )
     gain = head_gain[None]
     mixed, core, update, states, inverses, resid1, upstream = head_part(
         pre, gate_pre, small, taps, rate, gain, w_out, resid, cotangent.reshape(count, width),
         heads, key_dim, value_dim, places, 2,
     )
-    hidden2 = rms_apply(resid1, norm2_gain).astype(bf)
-    ffn_gate = project(hidden2, w_ffn_gate)
-    ffn_up = project(hidden2, w_ffn_up)
-    inner_full, swiglu_back = jax.vjp(swiglu, ffn_gate, ffn_up)
-    inner = inner_full.astype(bf)
-    grad_inner = back_project(upstream, w_ffn_down)
-    grad_fgate, grad_fup = swiglu_back(grad_inner)
-    grad_fgate = grad_fgate.astype(bf)
-    grad_fup = grad_fup.astype(bf)
-    part2 = back_project(grad_fgate, w_ffn_gate) + back_project(grad_fup, w_ffn_up)
-    down = contract_rows(inner, upstream)
-    ffn = project(inner, w_ffn_down)
+    hidden2, units, part2, ffn = feed(
+        resid1, norm2_gain[None], upstream, w_ffn_gate.T, w_ffn_up.T, w_ffn_down
+    )
     held, ranges = tail(
-        part2, ffn, down, pre, core, update, states, resid1, upstream, resid.astype(bf), mixed, hidden1,
-        hidden2, jnp.concatenate([grad_fgate, grad_fup], axis=1),
-        w_out, w_mix, w_gate, w_small, norm1_gain[None], norm2_gain[None],
-        gate_pre, small, taps, rate, gain, inverses,
-        heads, key_dim, value_dim, places, 7,
+        part2, ffn, pre, core, update, states, resid1, upstream, resid, mixed, hidden1, hidden2, units,
+        w_out, w_query, w_key, w_value, w_gate, w_small, gate_pre, small, inverses,
+        norm1_gain[None], norm2_gain[None], taps, rate, gain,
+        heads, key_dim, value_dim, w_ffn_down.shape[0], places, 7,
     )
     (
         output, grad_inputs, fgate, fup, grad_down, grad_out_w, grad_gate_w, grad_query_w, grad_key_w, grad_value_w,
         grad_norm1_gain, grad_norm2_gain, grad_head, grad_rate, grad_beta_w, grad_decay_w,
         grad_convq, grad_convk, grad_convv,
-    ) = finish(*held, ranges, inner.shape[1], heads, qk_width, heads * value_dim)
+    ) = finish(*held, ranges, w_ffn_down.shape[0], heads, qk_width, heads * value_dim)
     return (
         output.reshape(batch, seg, width),
         grad_inputs.reshape(batch, seg, width),

time: 454 us -> 428 us (0.943)
  matrix products: 17.2 us -> 0 us
  local copies, waits for them, and re-layouts: 9.71 us -> 0 us
  Pallas kernels: 420 us -> 427 us
  other arithmetic: 6.02 us -> 0 us
    pallas_call x1 -> x2, Pallas kernels: 24.3 us -> 43.8 us  [the longest x1 31.4 us: prep(): pl.pallas_call(functools.partial(prep_kernel, heads), out_shape=[shape((l...]
    dot_general x10 -> x0, matrix products: 17.2 us -> none  [the longest x6 10.4 us: project(): return jnp.dot(left, right, preferred_element_type=jnp.float32)]
    pallas_call x1, Pallas kernels: 55.6 us -> 46.3 us  [head_part(): pl.pallas_call(functools.partial(head_kernel, heads, key_dim, value_dim),...]
    unnamed x38 -> x0, local copies, waits for them, and re-layouts: 6.64 us -> none
where the time goes in v5:
time: 428 us
  Pallas kernels  427 us (100%)
    pallas_call x1, Pallas kernels, tail(): pl.pallas_call(functools.partial(tail_kernel, heads, key_dim, value_dim,...  329 us
    pallas_call x1, Pallas kernels, head_part(): pl.pallas_call(functools.partial(head_kernel, heads, key_dim, value_dim),...  46.3 us
    pallas_call x1, Pallas kernels, prep(): pl.pallas_call(functools.partial(prep_kernel, heads), out_shape=[shape((l...  31.4 us
    pallas_call x1, Pallas kernels, feed(): pl.pallas_call(feed_kernel, out_shape=[shape((length, width), bf), shape(...  12.4 us

profile of v5, /device:TPU:0, one launch (start us, length us, event | category | flops | bytes accessed | tf_op | source)
XLA Modules:
  0.0 427.7 jit_solution(2841420783827964776)
XLA Ops:
  0.7 31.4 %prep.1 = (bf16[512,1024]{1,0:T(8,128)(2,1)}, bf16[512,1024]{1,0:T(8,128)(2,1)}, f32[512,1024]{1,0:T(8,128)}, f32[512,512]{1,0:T(8,128)}, f32[512,128]{1,0:T(8,1...) custom-call(bf16[512,1024]{1,0:T(8,128)(2,1)} %bitcast.22, f32[1,1024]{1,0:T(1,128)} %bitcast.24, ...), custom_call_target="tpu_custom_call" | custom-call | tf_op jit(solution)/shard_map/prep/pallas_call | solution.py:1946
  32.1 46.3 %head.1 = (bf16[512,512]{1,0:T(8,128)(2,1)}, f32[512,512]{1,0:T(8,128)}, f32[512,512]{1,0:T(8,128)}, f32[512,1024]{1,0:T(8,128)}, f32[8,2,64,64]{3,2,1,0:T(8,128...) custom-call(f32[512,1024]{1,0:T(8,128)} %get-tuple-element.60.pre_ref.pre_hbm, ...), custom_call_target="tpu_custom_call" | custom-call | tf_op jit(solution)/shard_map/head/pallas_call | solution.py:1813
  78.4 12.4 %feed.1 = (bf16[512,1024]{1,0:T(8,128)(2,1)}, bf16[3,512,768]{2,1,0:T(8,128)(2,1)}, f32[512,1024]{1,0:T(8,128)}, f32[512,1024]{1,0:T(8,128)}) custom-call(f32[512,1024]{1,0:T(8,128)} %get-tuple-element.66.resid1_ref.resid1_hbm, f32[1,1024]{1,0:T(1,128)} %bitcast.26, bf16[512,1024]{1,0:T(8,128)(2,1)} %get-tuple-element.67.upstream_hbm, ...), custom_call_target="tpu_custom_call" | custom-call | tf_op jit(solution)/shard_map/feed/pallas_call | solution.py:2033
  90.8 329.1 %tail.1 = (f32[4240,1024]{1,0:T(8,128)S(1)}, bf16[512,1024]{1,0:T(8,128)(2,1)S(1)}, f32[512,1024]{1,0:T(8,128)S(1)}) custom-call(f32[512,1024]{1,0:T(8,128)} %get-tuple-element.68.part2_hbm, f32[512,1024]{1,0:T(8,128)} %get-tuple-element.69.ffn_hbm, f32[512,1024]{1,0:T(8,128)} %get-tuple-element.60.pre_ref.pre_hbm, f32[512,512]{1,0:T(8,128)} %get-tuple-element.70.core_hbm, ...), custom_call_target="tpu_custom_call" | custom-call | tf_op jit(solution)/shard_map/tail/pallas_call | solution.py:1561
  419.9 7.7 %finish.1 = (bf16[512,1024]{1,0:T(8,128)(2,1)}, f32[512,1024]{1,0:T(8,128)}, f32[704,1024]{1,0:T(8,128)}, f32[704,1024]{1,0:T(8,128)}, f32[704,1024]{1,0:T(8,128...) custom-call(f32[4240,1024]{1,0:T(8,128)S(1)} %get-tuple-element.79.d, ...), custom_call_target="tpu_custom_call" | custom-call | tf_op jit(solution)/shard_map/finish/pallas_call | solution.py:1629

commit v6 on v5

--- a/solution.py
+++ b/solution.py
@@ -1132,8 +1132,8 @@
         self.total[mine] = value if beside is None else value + beside[mine].astype(value.dtype)
         self.third(block).start()
 
-    def finish(self):
-        for block in range(BLOCKS):
+    def finish(self, had=0):
+        for block in range(had, BLOCKS):
             self.third(block).wait_recv()
         for block in range(BLOCKS):
             self.first(block).wait_send()
@@ -1654,13 +1654,14 @@
     return inverses
 
 
-def head_kernel(
-    heads, key_dim, value_dim,
-    pre_ref, gate_ref, small_ref, taps_ref, rate_ref, gain_ref, w_out_ref, resid_ref, cotangent_ref,
-    mixed_ref, core_ref, update_ref, state_ref, inverse_ref, resid1_ref, upstream_ref,
+def head_body(
+    heads, key_dim, value_dim, begin, early, halfway,
+    pre_ref, gate_ref, small_ref, taps_ref, rate_ref, gain_ref, w_out_ref, resid_ref, norm2_ref,
+    w_gate_hbm, w_up_hbm, w_down_hbm,
+    mixed_ref, core_ref, update_ref, state_ref, inverse_ref, resid1_ref, upstream_ref, hidden_ref, units_ref, part2_ref, ffn_ref,
     pad, now, solved_key, rise_query, key_tail, attend_all, ends,
     part, land_mate, land_across, half, sum_send, sum_recv,
-    staged, arrived, swap_send, swap_recv, close_send, close_recv,
+    arrived, w_gate, w_up, w_down, gate_pre, up_pre, inner_grad, load_sem,
 ):
     length, width = pre_ref.shape
     span = SPAN
@@ -1669,10 +1670,12 @@
     qk = heads * key_dim
     n, _, me, t, _, _ = grid_place()
     _, mate, across = tensor_peers()
-    peers = [(lax.rem(me + k, n), t) for k in range(1, n)] + [mate, across]
-    call_out(peers)
+    loads = [(w_gate_hbm, w_gate), (w_up_hbm, w_up), (w_down_hbm, w_down)]
+    loads = [pltpu.make_async_copy(src, dst, load_sem.at[i]) for i, (src, dst) in enumerate(loads)]
+    for load in loads:
+        load.start()
     total = TensorSum(part, resid1_ref, land_mate, land_across, half, sum_send, sum_recv)
-    swap = PlaneSwap(staged, arrived, swap_send, swap_recv, close_send, close_recv)
+    swap = begin
     pad[0:HALO] = jnp.zeros((HALO, width), jnp.float32)
     now[...] = jnp.zeros_like(now)
 
@@ -1755,12 +1758,7 @@
             total.share(turn * PAIR + k, resid_ref)
 
     pairs = chunks // PAIR
-    for place in range(n):
-        mine = swap.at(place, swap.core)
-        staged[mine] = cotangent_ref[mine].astype(jnp.float32)
     prepare_pair(0)
-    hear_all(peers)
-    swap.start()
 
     def step(turn, carry):
         chain_pair(turn - 1)
@@ -1787,7 +1785,6 @@
 
     lax.fori_loop(0, n, gather, 0)
 
-    share_pair(pairs - 1)
     swap.sent()
     swap.finish()
 
@@ -1797,62 +1794,209 @@
         return carry
 
     lax.fori_loop(0, length // 64, turn_low, 0)
-    total.finish()
-
-
-def head_part(
-    pre, gate, small, taps, rate, gain, w_out, resid, cotangent, heads, key_dim, value_dim, places, collective_id
+    for load in loads:
+        load.wait()
+    units = w_gate.shape[0]
+    whole = units // 128 * 128
+    low = units_ref.dtype
+    units_ref[:, :, whole:] = jnp.zeros((3, length, units_ref.shape[2] - whole), low)
+    some = length // 2
+
+    def feed(first):
+        def norm(i, carry):
+            here = aligned(first + i * 64, 64)
+            value = resid1_ref[here]
+            scale = lax.rsqrt(jnp.mean(value * value, -1, keepdims=True) + EPS)
+            hidden_ref[here] = (value * scale * norm2_ref[...]).astype(low)
+            return carry
+
+        lax.fori_loop(0, some // 64, norm, 0)
+        block = pl.ds(first, some)
+        gate_pre[...] = dot_nt(hidden_ref[block], w_gate[...])
+        up_pre[...] = dot_nt(hidden_ref[block], w_up[...])
+        inner_grad[...] = dot_nt(upstream_ref[block], w_down[...])
+
+        def bend(i, carry):
+            at = aligned(i * 64, 64)
+            here = aligned(first + i * 64, 64)
+            gate = gate_pre[at]
+            upper = up_pre[at]
+            grad = inner_grad[at]
+            sig = sigmoid(gate)
+            silu = gate * sig
+            units_ref[0, here, 0:units] = (silu * upper).astype(low)
+            units_ref[1, here, 0:units] = (grad * upper * (sig * (1.0 + gate * (1.0 - sig)))).astype(low)
+            units_ref[2, here, 0:units] = (grad * silu).astype(low)
+            return carry
+
+        lax.fori_loop(0, some // 64, bend, 0)
+        part2_ref[block] = dot_plain(units_ref[1, block, 0:units], w_gate[...]) + dot_plain(
+            units_ref[2, block, 0:units], w_up[...]
+        )
+        ffn_ref[block] = dot_plain(units_ref[0, block, 0:units], w_down[...])
+
+    early()
+    for block in range(BLOCKS // 2):
+        total.third(block).wait_recv()
+    feed(0)
+    halfway()
+    share_pair(pairs - 1)
+    total.finish(BLOCKS // 2)
+    feed(some)
+
+
+def front_kernel(
+    heads, key_dim, value_dim,
+    x_ref, norm1_ref, beta_ref, decay_ref, rate_ref, taps_q, taps_k, taps_v, gain_ref, cotangent_ref, norm2_ref,
+    query_hbm, key_hbm, value_hbm, gate_hbm, w_out_hbm, w_gate_hbm, w_up_hbm, w_down_hbm,
+    low_out, hidden1_out, pre_out, gate_out, small_out, w_small_out,
+    mixed_out, core_out, update_out, state_out, inverse_out, upstream_out, resid1_out,
+    hidden2_out, units_out, part2_out, ffn_out, taps_ref, rate_row_ref,
+    low, hidden1, pre, gate_pre, small, w_small, mixed, core, update, state, inverse, upstream, resid1,
+    hidden2, units, part2, ffn, w_out,
+    w_mix, w_gate_mix, rows16, staged, arrived, send, recv, close_send, close_recv, load_sem,
+    pad, now, solved_key, rise_query, key_tail, attend_all, ends,
+    part, land_mate, land_across, half, sum_send, sum_recv,
+    staged2, arrived2, send2, recv2, close_send2, close_recv2,
+    w_gate, w_up, w_down, gate_in, up_in, inner_grad, load_sem2, out_sem,
 ):
-    length, width = pre.shape
+    load_w_out = pltpu.make_async_copy(w_out_hbm, w_out, out_sem.at[0])
+    load_w_out.start()
+    cotangents = PlaneSwap(staged2, arrived2, send2, recv2, close_send2, close_recv2)
+
+    def between():
+        for place in range(cotangents.n):
+            mine = cotangents.at(place, cotangents.core)
+            staged2[mine] = cotangent_ref[mine].astype(jnp.float32)
+        cotangents.start()
+
+    prep_part(
+        heads, between, x_ref, norm1_ref, query_hbm, key_hbm, value_hbm, gate_hbm, beta_ref, decay_ref, rate_ref,
+        taps_q, taps_k, taps_v, low, hidden1, pre, gate_pre, small, w_small, taps_ref, rate_row_ref,
+        w_mix, w_gate_mix, rows16, staged, arrived, send, recv, close_send, close_recv, load_sem,
+    )
+    pairs = [
+        (low, low_out), (hidden1, hidden1_out), (pre, pre_out), (gate_pre, gate_out), (small, small_out),
+        (w_small, w_small_out),
+    ]
+    later = [
+        (mixed, mixed_out), (core, core_out), (update, update_out), (state, state_out), (inverse, inverse_out),
+        (upstream, upstream_out),
+    ]
+    rows = hidden2.shape[0]
+    halves = [pl.ds(0, rows // 2), pl.ds(rows // 2, rows // 2)]
+    last = [
+        [
+            (hidden2.at[span], hidden2_out.at[span]), (part2.at[span], part2_out.at[span]), (ffn.at[span], ffn_out.at[span]),
+            (resid1.at[span], resid1_out.at[span]),
+        ]
+        + [(units.at[k, span], units_out.at[k, span]) for k in range(3)]
+        for span in halves
+    ]
+    every = pairs + later + last[0] + last[1]
+    copies = [pltpu.make_async_copy(src, dst, out_sem.at[1 + i]) for i, (src, dst) in enumerate(every)]
+    one, two, three = len(pairs), len(pairs) + len(later), len(pairs) + len(later) + len(last[0])
+
+    def begin_copies(start, stop):
+        for copy in copies[start:stop]:
+            copy.start()
+
+    begin_copies(0, one)
+    load_w_out.wait()
+    head_body(
+        heads, key_dim, value_dim, cotangents, lambda: begin_copies(one, two), lambda: begin_copies(two, three),
+        pre, gate_pre, small, taps_ref, rate_row_ref, gain_ref, w_out, low, norm2_ref, w_gate_hbm, w_up_hbm, w_down_hbm,
+        mixed, core, update, state, inverse, resid1, upstream, hidden2, units, part2, ffn,
+        pad, now, solved_key, rise_query, key_tail, attend_all, ends,
+        part, land_mate, land_across, half, sum_send, sum_recv,
+        arrived2, w_gate, w_up, w_down, gate_in, up_in, inner_grad, load_sem2,
+    )
+    begin_copies(three, len(copies))
+    for copy in copies:
+        copy.wait()
+
+
+def front(
+    x, cotangent, norm1, norm2, w_query, w_key, w_value, w_gate, w_beta_t, w_decay_t, rate, taps_q, taps_k, taps_v, gain,
+    w_out, w_gate_t, w_up_t, w_down, heads, key_dim, value_dim, places, collective_id,
+):
+    length, width = x.shape
     values = heads * value_dim
     qk = heads * key_dim
+    lanes = 128
     chunks = length // SPAN
+    units = w_down.shape[0]
+    padded = -(-units // 128) * 128
     f32, bf = jnp.float32, jnp.bfloat16
-    shape = jax.ShapeDtypeStruct
     dma = pltpu.SemaphoreType.DMA
+    any_ = pl.BlockSpec(memory_space=pl.ANY)
+    shapes = [
+        ((length, width), bf),
+        ((length, width), bf),
+        ((length, width), f32),
+        ((length, values), f32),
+        ((length, lanes), f32),
+        ((lanes, width), bf),
+        ((length, values), bf),
+        ((length, values), f32),
+        ((length, values), f32),
+        ((chunks * heads * key_dim * value_dim // width, width), f32),
+        ((chunks, heads, SPAN, SPAN), f32),
+        ((length, width), bf),
+        ((length, width), f32),
+        ((length, width), bf),
+        ((3, length, padded), bf),
+        ((length, width), f32),
+        ((length, width), f32),
+    ]
+    smalls = [((taps_q.shape[0], width), f32), ((1, lanes), f32)]
+    vmem = [
+        (w_out.shape, bf),
+        ((width, width), bf),
+        ((width, values), bf),
+        ((16, width), f32),
+        ((length, width), f32),
+        ((length, width), f32),
+    ]
+    swap_sems = [dma((places,)), dma((places,)), dma((3, places)), dma((3, places))]
+    more = [
+        ((HALO + SPAN, width), f32),
+        ((heads, key_dim, value_dim), f32),
+        ((length, qk), f32),
+        ((length, qk), f32),
+        ((length, qk), f32),
+        ((chunks, heads, SPAN, SPAN), f32),
+        ((chunks, heads, 8, 128), f32),
+        ((length, width), f32),
+        ((length // 2, width), f32),
+        ((length // 2, width), f32),
+        ((length // 2, width), f32),
+    ]
+    last = [((units, width), bf)] * 3 + [((length // 2, units), f32)] * 3
+
+    def scratch(items):
+        return [pltpu.VMEM(shape, kind) for shape, kind in items]
+
     return pl.pallas_call(
-        functools.partial(head_kernel, heads, key_dim, value_dim),
-        out_shape=[
-            shape((length, values), bf),
-            shape((length, values), f32),
-            shape((length, values), f32),
-            shape((chunks * heads * key_dim * value_dim // width, width), f32),
-            shape((chunks, heads, SPAN, SPAN), f32),
-            shape((length, width), f32),
-            shape((length, width), bf),
-        ],
-        in_specs=[VM] * 9,
-        out_specs=[VM] * 7,
-        scratch_shapes=[
-            pltpu.VMEM((HALO + SPAN, width), f32),
-            pltpu.VMEM((heads, key_dim, value_dim), f32),
-            pltpu.VMEM((length, qk), f32),
-            pltpu.VMEM((length, qk), f32),
-            pltpu.VMEM((length, qk), f32),
-            pltpu.VMEM((chunks, heads, SPAN, SPAN), f32),
-            pltpu.VMEM((chunks, heads, 8, 128), f32),
-            pltpu.VMEM((length, width), f32),
-            pltpu.VMEM((length // 2, width), f32),
-            pltpu.VMEM((length // 2, width), f32),
-            pltpu.VMEM((length // 2, width), f32),
-            dma((3, BLOCKS)),
-            dma((3, BLOCKS)),
-            pltpu.VMEM((length, width), f32),
-            pltpu.VMEM((length, width), f32),
-            dma((places,)),
-            dma((places,)),
-            dma((3, places)),
-            dma((3, places)),
-        ],
+        functools.partial(front_kernel, heads, key_dim, value_dim),
+        out_shape=[jax.ShapeDtypeStruct(shape, kind) for shape, kind in shapes + smalls],
+        in_specs=[VM] * 11 + [any_] * 8,
+        out_specs=[any_] * len(shapes) + [VM] * len(smalls),
+        scratch_shapes=scratch(shapes) + scratch(vmem) + swap_sems + [dma((4,))] + scratch(more)
+        + [dma((3, BLOCKS)), dma((3, BLOCKS))] + scratch([((length, width), f32)] * 2) + swap_sems + scratch(last)
+        + [dma((3,)), dma((32,))],
         compiler_params=pltpu.CompilerParams(
             collective_id=collective_id, has_side_effects=True, vmem_limit_bytes=67043328
         ),
-        name="head",
-    )(pre, gate, small, taps, rate, gain, w_out, resid, cotangent)
-
-
-def prep_kernel(
-    heads,
+        name="front",
+    )(
+        x, norm1, w_beta_t, w_decay_t, rate, taps_q, taps_k, taps_v, gain, cotangent, norm2,
+        w_query, w_key, w_value, w_gate, w_out, w_gate_t, w_up_t, w_down,
+    )
+
+
+def prep_part(
+    heads, between,
     x_ref, norm1_ref, query_hbm, key_hbm, value_hbm, gate_hbm, beta_ref, decay_ref, rate_ref, taps_q, taps_k, taps_v,
     low_ref, hidden_ref, pre_ref, gate_pre_ref, small_ref, w_small_ref, taps_ref, rate_row_ref,
     w_mix, w_gate, rows16, staged, arrived, send, recv, close_send, close_recv, load_sem,
@@ -1903,6 +2047,7 @@
         return carry
 
     lax.fori_loop(0, n, gather, 0)
+    between()
     lax.fori_loop(0, n, forward, 0)
     for load in loads:
         load.wait()
@@ -1932,127 +2077,6 @@
     lax.fori_loop(0, width // 256, mix_tile, 0)
     lax.fori_loop(0, values // 256, gate_tile, 0)
     small_ref[...] = dot_nt(hidden_ref[...], w_small_ref[...])
-
-
-def prep(x, norm1, w_query, w_key, w_value, w_gate, w_beta_t, w_decay_t, rate, taps_q, taps_k, taps_v, places, collective_id):
-    length, width = x.shape
-    heads = rate.shape[1]
-    values = w_value.shape[1]
-    lanes = 128
-    f32, bf = jnp.float32, jnp.bfloat16
-    shape = jax.ShapeDtypeStruct
-    dma = pltpu.SemaphoreType.DMA
-    any_ = pl.BlockSpec(memory_space=pl.ANY)
-    return pl.pallas_call(
-        functools.partial(prep_kernel, heads),
-        out_shape=[
-            shape((length, width), bf),
-            shape((length, width), bf),
-            shape((length, width), f32),
-            shape((length, values), f32),
-            shape((length, lanes), f32),
-            shape((lanes, width), bf),
-            shape((taps_q.shape[0], width), f32),
-            shape((1, lanes), f32),
-        ],
-        in_specs=[VM] * 2 + [any_] * 4 + [VM] * 6,
-        out_specs=[VM] * 8,
-        scratch_shapes=[
-            pltpu.VMEM((width, width), bf),
-            pltpu.VMEM((width, values), bf),
-            pltpu.VMEM((16, width), f32),
-            pltpu.VMEM((length, width), f32),
-            pltpu.VMEM((length, width), f32),
-            dma((places,)),
-            dma((places,)),
-            dma((3, places)),
-            dma((3, places)),
-            dma((4,)),
-        ],
-        compiler_params=pltpu.CompilerParams(
-            collective_id=collective_id, has_side_effects=True, vmem_limit_bytes=67043328
-        ),
-        name="prep",
-    )(x, norm1, w_query, w_key, w_value, w_gate, w_beta_t, w_decay_t, rate, taps_q, taps_k, taps_v)
-
-
-def feed_kernel(
-    resid1_ref, norm2_ref, upstream_hbm, gate_hbm, up_hbm, down_hbm,
-    hidden_ref, units_ref, part2_ref, ffn_ref,
-    upstream, w_gate, w_up, w_down, gate_pre, up_pre, inner_grad, load_sem,
-):
-    length, width = resid1_ref.shape
-    units = w_gate.shape[0]
-    loads = [(gate_hbm, w_gate), (up_hbm, w_up), (upstream_hbm, upstream), (down_hbm, w_down)]
-    loads = [pltpu.make_async_copy(src, dst, load_sem.at[i]) for i, (src, dst) in enumerate(loads)]
-    for load in loads:
-        load.start()
-
-    def norm(i, carry):
-        here = aligned(i * 64, 64)
-        value = resid1_ref[here]
-        scale = lax.rsqrt(jnp.mean(value * value, -1, keepdims=True) + EPS)
-        hidden_ref[here] = (value * scale * norm2_ref[...]).astype(hidden_ref.dtype)
-        return carry
-
-    lax.fori_loop(0, length // 64, norm, 0)
-    loads[0].wait()
-    gate_pre[...] = dot_nt(hidden_ref[...], w_gate[...])
-    loads[1].wait()
-    up_pre[...] = dot_nt(hidden_ref[...], w_up[...])
-    loads[2].wait()
-    loads[3].wait()
-    inner_grad[...] = dot_nt(upstream[...], w_down[...])
-    units_ref[:, :, units // 128 * 128 :] = jnp.zeros((3, length, units_ref.shape[2] - units // 128 * 128), units_ref.dtype)
-
-    def bend(i, carry):
-        here = aligned(i * 64, 64)
-        gate = gate_pre[here]
-        upper = up_pre[here]
-        grad = inner_grad[here]
-        sig = sigmoid(gate)
-        silu = gate * sig
-        low = units_ref.dtype
-        units_ref[0, here, 0:units] = (silu * upper).astype(low)
-        units_ref[1, here, 0:units] = (grad * upper * (sig * (1.0 + gate * (1.0 - sig)))).astype(low)
-        units_ref[2, here, 0:units] = (grad * silu).astype(low)
-        return carry
-
-    lax.fori_loop(0, length // 64, bend, 0)
-    part2_ref[...] = dot_plain(units_ref[1, :, 0:units], w_gate[...]) + dot_plain(units_ref[2, :, 0:units], w_up[...])
-    ffn_ref[...] = dot_plain(units_ref[0, :, 0:units], w_down[...])
-
-
-def feed(resid1, norm2, upstream, w_gate_t, w_up_t, w_down):
-    length, width = resid1.shape
-    units = w_down.shape[0]
-    padded = -(-units // 128) * 128
-    f32, bf = jnp.float32, jnp.bfloat16
-    shape = jax.ShapeDtypeStruct
-    any_ = pl.BlockSpec(memory_space=pl.ANY)
-    return pl.pallas_call(
-        feed_kernel,
-        out_shape=[
-            shape((length, width), bf),
-            shape((3, length, padded), bf),
-            shape((length, width), f32),
-            shape((length, width), f32),
-        ],
-        in_specs=[VM] * 2 + [any_] * 4,
-        out_specs=[VM] * 4,
-        scratch_shapes=[
-            pltpu.VMEM((length, width), bf),
-            pltpu.VMEM((units, width), bf),
-            pltpu.VMEM((units, width), bf),
-            pltpu.VMEM((units, width), bf),
-            pltpu.VMEM((length, units), f32),
-            pltpu.VMEM((length, units), f32),
-            pltpu.VMEM((length, units), f32),
-            pltpu.SemaphoreType.DMA((4,)),
-        ],
-        compiler_params=pltpu.CompilerParams(vmem_limit_bytes=67043328),
-        name="feed",
-    )(resid1, norm2, upstream, w_gate_t, w_up_t, w_down)
 
 
 def whole_sequences(
@@ -2083,17 +2107,14 @@
     value_dim = w_value.shape[1] // heads
     qk_width = heads * key_dim
     places = lax.axis_size("dp")
-    resid, hidden1, pre, gate_pre, small, w_small, taps, rate = prep(
-        inputs.reshape(count, width), norm1_gain[None], w_query, w_key, w_value, w_gate, w_beta.T, w_decay.T,
-        decay_rate[None], conv_query, conv_key, conv_value, places, 1,
-    )
     gain = head_gain[None]
-    mixed, core, update, states, inverses, resid1, upstream = head_part(
-        pre, gate_pre, small, taps, rate, gain, w_out, resid, cotangent.reshape(count, width),
-        heads, key_dim, value_dim, places, 2,
-    )
-    hidden2, units, part2, ffn = feed(
-        resid1, norm2_gain[None], upstream, w_ffn_gate.T, w_ffn_up.T, w_ffn_down
+    (
+        resid, hidden1, pre, gate_pre, small, w_small, mixed, core, update, states, inverses, upstream, resid1,
+        hidden2, units, part2, ffn, taps, rate,
+    ) = front(
+        inputs.reshape(count, width), cotangent.reshape(count, width), norm1_gain[None], norm2_gain[None],
+        w_query, w_key, w_value, w_gate, w_beta.T, w_decay.T, decay_rate[None], conv_query, conv_key, conv_value, gain,
+        w_out, w_ffn_gate.T, w_ffn_up.T, w_ffn_down, heads, key_dim, value_dim, places, 2,
     )
     held, ranges = tail(
         part2, ffn, pre, core, update, states, resid1, upstream, resid, mixed, hidden1, hidden2, units,

time: 428 us -> 417 us (0.974)
  Pallas kernels: 427 us -> 416 us
    pallas_call x3 -> x1, Pallas kernels: 90.1 us -> 76.8 us  [front(): pl.pallas_call(functools.partial(front_kernel, heads, key_dim, value_dim)...]
where the time goes in v6:
time: 417 us; the launch traced here: 416 us
  Pallas kernels  416 us (100%)
    pallas_call x1, Pallas kernels, tail(): pl.pallas_call(functools.partial(tail_kernel, heads, key_dim, value_dim,...  331 us
    pallas_call x1, Pallas kernels, front(): pl.pallas_call(functools.partial(front_kernel, heads, key_dim, value_dim)...  76.8 us

profile of v6, /device:TPU:0, one launch (start us, length us, event | category | flops | bytes accessed | tf_op | source)
XLA Modules:
  0.0 416.4 jit_solution(17647228377199096401)
XLA Ops:
  0.7 76.8 %front.1 = (bf16[512,1024]{1,0:T(8,128)(2,1)}, bf16[512,1024]{1,0:T(8,128)(2,1)}, f32[512,1024]{1,0:T(8,128)}, f32[512,512]{1,0:T(8,128)}, f32[512,128]{1,0:T(8,...) custom-call(bf16[512,1024]{1,0:T(8,128)(2,1)} %bitcast.22, ...), custom_call_target="tpu_custom_call" | custom-call | tf_op jit(solution)/shard_map/front/pallas_call | solution.py:1980
  77.5 331.1 %tail.1 = (f32[4240,1024]{1,0:T(8,128)S(1)}, bf16[512,1024]{1,0:T(8,128)(2,1)S(1)}, f32[512,1024]{1,0:T(8,128)S(1)}) custom-call(f32[512,1024]{1,0:T(8,128)} %get-tuple-element.60.part2_hbm, f32[512,1024]{1,0:T(8,128)} %get-tuple-element.61.ffn_hbm, f32[512,1024]{1,0:T(8,128)} %get-tuple-element.62.pre_hbm, f32[512,512]{1,0:T(8,128)} %get-tuple-element.63.core_hbm, ...), custom_call_target="tpu_custom_call" | custom-call | tf_op jit(solution)/shard_map/tail/pallas_call | solution.py:1561
  408.6 7.7 %finish.1 = (bf16[512,1024]{1,0:T(8,128)(2,1)}, f32[512,1024]{1,0:T(8,128)}, f32[704,1024]{1,0:T(8,128)}, f32[704,1024]{1,0:T(8,128)}, f32[704,1024]{1,0:T(8,128...) custom-call(f32[4240,1024]{1,0:T(8,128)S(1)} %get-tuple-element.79.d, ...), custom_call_target="tpu_custom_call" | custom-call | tf_op jit(solution)/shard_map/finish/pallas_call | solution.py:1629

commit v7 on v6

--- a/solution.py
+++ b/solution.py
@@ -813,6 +813,7 @@
 DEPTH = 10
 SPLIT = 3
 WHOLE = 2
+ORDER = (0, 1, 2, 3)
 
 
 def grid_place():
@@ -838,7 +839,7 @@
     def within(chunk):
         return (chunk >= 0) & (chunk < chunks)
 
-    for stream in range(SPLIT):
+    def split_stream(stream):
         land_x, land_z, outgo, aside = split_rings
         up = stream % 2 == 0
         level = z if up else top - z
@@ -876,56 +877,62 @@
 
             close(chunk, x).start()
 
-        @pl.when(slot < chunks)
-        def _():
+        def enter():
+          @pl.when(slot < chunks)
+          def _():
             aside[stream, ring(slot)] = data[rows(slot, 1 - x)]
             to_mate(slot).start()
 
-        rise = slot - 1 - level
-
-        @pl.when(within(rise))
-        def _():
-            here = rows(rise, x)
-            at = ring(rise)
-            to_mate(rise).wait_recv()
-
-            @pl.when(level > 0)
+        def climb():
+            rise = slot - 1 - level
+
+            @pl.when(within(rise))
             def _():
-                to_after(rise).wait_recv()
-                outgo[stream, at] = data[here] + land_x[stream, at] + land_z[stream, at]
-
-            @pl.when(level == 0)
+                here = rows(rise, x)
+                at = ring(rise)
+                to_mate(rise).wait_recv()
+
+                @pl.when(level > 0)
+                def _():
+                    to_after(rise).wait_recv()
+                    outgo[stream, at] = data[here] + land_x[stream, at] + land_z[stream, at]
+
+                @pl.when(level == 0)
+                def _():
+                    outgo[stream, at] = data[here] + land_x[stream, at]
+
+                @pl.when(level < top)
+                def _():
+                    to_after(rise).start()
+
+                @pl.when(level == top)
+                def _():
+                    data[here] = outgo[stream, at]
+                    give_back(rise)
+
+        def descend():
+            fall = slot - 1 - 2 * top + level
+
+            @pl.when(within(fall) & (level < top))
             def _():
-                outgo[stream, at] = data[here] + land_x[stream, at]
-
-            @pl.when(level < top)
+                result(fall, after).wait_recv()
+                to_after(fall).wait_send()
+                give_back(fall)
+
+        def leave():
+            @pl.when(within(finish))
             def _():
-                to_after(rise).start()
-
-            @pl.when(level == top)
-            def _():
-                data[here] = outgo[stream, at]
-                give_back(rise)
-
-        fall = slot - 1 - 2 * top + level
-
-        @pl.when(within(fall) & (level < top))
-        def _():
-            result(fall, after).wait_recv()
-            to_after(fall).wait_send()
-            give_back(fall)
-
-        @pl.when(within(finish))
-        def _():
-            @pl.when(level > 0)
-            def _():
-                result(finish, prior).wait_send()
-
-            close(finish, x).wait_send()
-            close(finish, 1 - x).wait_recv()
-            to_mate(finish).wait_send()
-
-    for stream in range(WHOLE):
+                @pl.when(level > 0)
+                def _():
+                    result(finish, prior).wait_send()
+
+                close(finish, x).wait_send()
+                close(finish, 1 - x).wait_recv()
+                to_mate(finish).wait_send()
+
+        return enter, climb, descend, leave
+
+    def whole_stream(stream):
         land_x, land_z, land_s, outgo = whole_rings
         line = z if stream == 0 else top - z
         step = 2 if stream == 0 else -2
@@ -960,96 +967,107 @@
             here = data.at[rows(chunk)]
             return copy(send_s, recv_d, chunk, here, here, inner)
 
-        rise = slot - 1 - (top - line)
-        root = lax.rem(jnp.maximum(rise, 0), 2)
-
-        @pl.when(within(rise) & (line >= root))
-        def _():
-            here = rows(rise)
-            at = ring(rise)
-
-            @pl.when(line < top)
+        def enter():
+            leaf = slot - 1
+
+            @pl.when(within(leaf) & (line == 0) & (lax.rem(jnp.maximum(leaf, 0), 2) > 0))
             def _():
-                inward(rise).wait_recv()
-
-            is_fork = (line == root) & (root > 0)
-
-            @pl.when(is_fork)
+                outgo[stream, ring(leaf)] = data[rows(leaf)]
+                outward(leaf).start()
+
+        def climb():
+            rise = slot - 1 - (top - line)
+            root = lax.rem(jnp.maximum(rise, 0), 2)
+
+            @pl.when(within(rise) & (line >= root))
             def _():
-                outward(rise).wait_recv()
-                outgo[stream, at] = data[here] + land_z[stream, at] + land_s[stream, at]
-
-            @pl.when((line < top) & jnp.logical_not(is_fork))
-            def _():
-                outgo[stream, at] = data[here] + land_z[stream, at]
-
-            @pl.when(line == top)
-            def _():
-                outgo[stream, at] = data[here]
-
-            @pl.when(line > root)
-            def _():
-                inward(rise).start()
-
-            @pl.when(line == root)
-            def _():
-                to_mate(rise).start()
-
-        leaf = slot - 1
-
-        @pl.when(within(leaf) & (line == 0) & (lax.rem(jnp.maximum(leaf, 0), 2) > 0))
-        def _():
-            outgo[stream, ring(leaf)] = data[rows(leaf)]
-            outward(leaf).start()
-
-        meet = slot - 2 - (top - line)
-        meet_root = lax.rem(jnp.maximum(meet, 0), 2)
-
-        @pl.when(within(meet) & (line == meet_root))
-        def _():
-            at = ring(meet)
-            to_mate(meet).wait_recv()
-            data[rows(meet)] = outgo[stream, at] + land_x[stream, at]
-            result_out(meet).start()
-
-            @pl.when(meet_root > 0)
-            def _():
-                result_in(meet).start()
-
-        for parity in range(2):
-            fall = slot - 2 - (top - parity) - (line - parity)
-
-            @pl.when(within(fall) & (lax.rem(jnp.maximum(fall, 0), 2) == parity) & (line > parity))
-            def _():
-                result_out(fall).wait_recv()
-                inward(fall).wait_send()
+                here = rows(rise)
+                at = ring(rise)
 
                 @pl.when(line < top)
                 def _():
-                    result_out(fall).start()
-
-        inside = slot - 2 - (top - 1) - 1
-
-        @pl.when(within(inside) & (lax.rem(jnp.maximum(inside, 0), 2) > 0) & (line == 0))
-        def _():
-            result_in(inside).wait_recv()
-            outward(inside).wait_send()
-
-        end_root = lax.rem(jnp.maximum(finish, 0), 2)
-
-        @pl.when(within(finish))
-        def _():
-            @pl.when((line >= end_root) & (line < top))
+                    inward(rise).wait_recv()
+
+                is_fork = (line == root) & (root > 0)
+
+                @pl.when(is_fork)
+                def _():
+                    outward(rise).wait_recv()
+                    outgo[stream, at] = data[here] + land_z[stream, at] + land_s[stream, at]
+
+                @pl.when((line < top) & jnp.logical_not(is_fork))
+                def _():
+                    outgo[stream, at] = data[here] + land_z[stream, at]
+
+                @pl.when(line == top)
+                def _():
+                    outgo[stream, at] = data[here]
+
+                @pl.when(line > root)
+                def _():
+                    inward(rise).start()
+
+                @pl.when(line == root)
+                def _():
+                    to_mate(rise).start()
+
+        def descend():
+            meet = slot - 2 - (top - line)
+            meet_root = lax.rem(jnp.maximum(meet, 0), 2)
+
+            @pl.when(within(meet) & (line == meet_root))
             def _():
-                result_out(finish).wait_send()
-
-            @pl.when(line == end_root)
+                at = ring(meet)
+                to_mate(meet).wait_recv()
+                data[rows(meet)] = outgo[stream, at] + land_x[stream, at]
+                result_out(meet).start()
+
+                @pl.when(meet_root > 0)
+                def _():
+                    result_in(meet).start()
+
+            for parity in range(2):
+                fall = slot - 2 - (top - parity) - (line - parity)
+
+                @pl.when(within(fall) & (lax.rem(jnp.maximum(fall, 0), 2) == parity) & (line > parity))
+                def _():
+                    result_out(fall).wait_recv()
+                    inward(fall).wait_send()
+
+                    @pl.when(line < top)
+                    def _():
+                        result_out(fall).start()
+
+            inside = slot - 2 - (top - 1) - 1
+
+            @pl.when(within(inside) & (lax.rem(jnp.maximum(inside, 0), 2) > 0) & (line == 0))
             def _():
-                to_mate(finish).wait_send()
-
-                @pl.when(end_root > 0)
+                result_in(inside).wait_recv()
+                outward(inside).wait_send()
+
+        def leave():
+            end_root = lax.rem(jnp.maximum(finish, 0), 2)
+
+            @pl.when(within(finish))
+            def _():
+                @pl.when((line >= end_root) & (line < top))
                 def _():
-                    result_in(finish).wait_send()
+                    result_out(finish).wait_send()
+
+                @pl.when(line == end_root)
+                def _():
+                    to_mate(finish).wait_send()
+
+                    @pl.when(end_root > 0)
+                    def _():
+                        result_in(finish).wait_send()
+
+        return enter, climb, descend, leave
+
+    streams = [whole_stream(stream) for stream in range(WHOLE)] + [split_stream(stream) for stream in range(SPLIT)]
+    for stream in streams:
+        for phase in ORDER:
+            stream[phase]()
 
 
 def settle(lines):

time: 417 us -> 414 us (level)
  no operation moved by 1% of the time
where the time goes in v7:
time: 414 us; the launch traced here: 413 us
  Pallas kernels  413 us (100%)
    pallas_call x1, Pallas kernels, tail(): pl.pallas_call(functools.partial(tail_kernel, heads, key_dim, value_dim,...  328 us
    pallas_call x1, Pallas kernels, front(): pl.pallas_call(functools.partial(front_kernel, heads, key_dim, value_dim)...  76.8 us

profile of v7, /device:TPU:0, one launch (start us, length us, event | category | flops | bytes accessed | tf_op | source)
XLA Modules:
  0.0 413.4 jit_solution(6637384809937937231)
XLA Ops:
  0.7 76.8 %front.1 = (bf16[512,1024]{1,0:T(8,128)(2,1)}, bf16[512,1024]{1,0:T(8,128)(2,1)}, f32[512,1024]{1,0:T(8,128)}, f32[512,512]{1,0:T(8,128)}, f32[512,128]{1,0:T(8,...) custom-call(bf16[512,1024]{1,0:T(8,128)(2,1)} %bitcast.22, ...), custom_call_target="tpu_custom_call" | custom-call | tf_op jit(solution)/shard_map/front/pallas_call | solution.py:1998
  77.5 328.1 %tail.1 = (f32[4240,1024]{1,0:T(8,128)S(1)}, bf16[512,1024]{1,0:T(8,128)(2,1)S(1)}, f32[512,1024]{1,0:T(8,128)S(1)}) custom-call(f32[512,1024]{1,0:T(8,128)} %get-tuple-element.60.part2_hbm, f32[512,1024]{1,0:T(8,128)} %get-tuple-element.61.ffn_hbm, f32[512,1024]{1,0:T(8,128)} %get-tuple-element.62.pre_hbm, f32[512,512]{1,0:T(8,128)} %get-tuple-element.63.core_hbm, ...), custom_call_target="tpu_custom_call" | custom-call | tf_op jit(solution)/shard_map/tail/pallas_call | solution.py:1579
  405.5 7.7 %finish.1 = (bf16[512,1024]{1,0:T(8,128)(2,1)}, f32[512,1024]{1,0:T(8,128)}, f32[704,1024]{1,0:T(8,128)}, f32[704,1024]{1,0:T(8,128)}, f32[704,1024]{1,0:T(8,128...) custom-call(f32[4240,1024]{1,0:T(8,128)S(1)} %get-tuple-element.79.d, ...), custom_call_target="tpu_custom_call" | custom-call | tf_op jit(solution)/shard_map/finish/pallas_call | solution.py:1647

commit v8 on v7

--- a/solution.py
+++ b/solution.py
@@ -1276,9 +1276,9 @@
     values = heads * value_dim
     at_down, at_units, at_out, at_gate, at_mix, at_small, at_end, rows_all = ranges
     loads = [
-        (part2_hbm, part),
         (units_hbm, units_ref),
         (upstream_hbm, upstream_ref),
+        (part2_hbm, part),
         (hidden2_hbm, hidden2_ref),
         (resid1_hbm, resid1_ref),
         (w_out_hbm, w_out_ref),
@@ -1352,11 +1352,11 @@
             put(hidden2_ref[...])
 
     loads[0].wait()
+    loads[1].wait()
+    units_piece(0)
+    loads[2].wait()
     hear_all(peers)
     sums[0].start()
-    loads[1].wait()
-    loads[2].wait()
-    units_piece(0)
 
     def wait_loads():
         for load in loads[3:]:
@@ -2065,8 +2065,8 @@
         return carry
 
     lax.fori_loop(0, n, gather, 0)
+    lax.fori_loop(0, n, forward, 0)
     between()
-    lax.fori_loop(0, n, forward, 0)
     for load in loads:
         load.wait()
     swap.sent()

time: 414 us -> 412 us (level)
  no operation moved by 1% of the time
where the time goes in v8:
time: 412 us
  Pallas kernels  411 us (100%)
    pallas_call x1, Pallas kernels, tail(): pl.pallas_call(functools.partial(tail_kernel, heads, key_dim, value_dim,...  327 us
    pallas_call x1, Pallas kernels, front(): pl.pallas_call(functools.partial(front_kernel, heads, key_dim, value_dim)...  76.8 us

profile of v8, /device:TPU:0, one launch (start us, length us, event | category | flops | bytes accessed | tf_op | source)
XLA Modules:
  0.0 412.2 jit_solution(140337010467661039)
XLA Ops:
  0.7 76.8 %front.1 = (bf16[512,1024]{1,0:T(8,128)(2,1)}, bf16[512,1024]{1,0:T(8,128)(2,1)}, f32[512,1024]{1,0:T(8,128)}, f32[512,512]{1,0:T(8,128)}, f32[512,128]{1,0:T(8,...) custom-call(bf16[512,1024]{1,0:T(8,128)(2,1)} %bitcast.22, ...), custom_call_target="tpu_custom_call" | custom-call | tf_op jit(solution)/shard_map/front/pallas_call | solution.py:1998
  77.4 327.0 %tail.1 = (f32[4240,1024]{1,0:T(8,128)S(1)}, bf16[512,1024]{1,0:T(8,128)(2,1)S(1)}, f32[512,1024]{1,0:T(8,128)S(1)}) custom-call(f32[512,1024]{1,0:T(8,128)} %get-tuple-element.60.part2_hbm, f32[512,1024]{1,0:T(8,128)} %get-tuple-element.61.ffn_hbm, f32[512,1024]{1,0:T(8,128)} %get-tuple-element.62.pre_hbm, f32[512,512]{1,0:T(8,128)} %get-tuple-element.63.core_hbm, ...), custom_call_target="tpu_custom_call" | custom-call | tf_op jit(solution)/shard_map/tail/pallas_call | solution.py:1579
  404.4 7.7 %finish.1 = (bf16[512,1024]{1,0:T(8,128)(2,1)}, f32[512,1024]{1,0:T(8,128)}, f32[704,1024]{1,0:T(8,128)}, f32[704,1024]{1,0:T(8,128)}, f32[704,1024]{1,0:T(8,128...) custom-call(f32[4240,1024]{1,0:T(8,128)S(1)} %get-tuple-element.79.d, ...), custom_call_target="tpu_custom_call" | custom-call | tf_op jit(solution)/shard_map/finish/pallas_call | solution.py:1647
